TPU v7x, 32 devices: a whole 2x2x4 slice. The times are simulated.
32 devices in a mesh: dp: 8 (over z, y), group: 4 (over x, core).
Axes of the slice: x: 2, y: 2, z: 4, core: 2. Of those that a mesh axis runs over, the one named last changes fastest.
Arguments:
- deltas: bfloat16 [2048, 16, 4096], P(('dp', 'group')), may hold values from -96 to 96
- labels: int32 [2048, 1], P(('dp', 'group')), may hold values from 0 to 7; in each aligned block of 64 rows (0 to 63, 64 to 127, ...) at most 16 rows name the same one
Outputs:
- returned: bfloat16 [2048, 16, 4096], P(('dp', 'group'))
- cluster_rank: int32 [2048], P(('dp', 'group'))
Inputs may be any that keep to these rules, and one draw needn't show every extreme that they name: `labels`: among the clients of one device at most 16 carry the same label, and that many do on some device; every cluster has at least one client.
All inputs are finite; a program needn't handle non-finite values.
Results may differ from a plain program's by a relative error of at most 0.0004.
Values may be sent and summed in bfloat16 or wider, within the bound.
No kernel may reach another device: no remote copies, remote signals or barrier semaphores. Data moves between devices by JAX's collectives and lax.ppermute only.
A program may use at most 128 MiB of HBM per device.

v0:
```python
import jax
import jax.numpy as jnp
from jax import lax
from jax.sharding import PartitionSpec as P

CLUSTERS = 8


def carried_in(value, axis, join, neutral):
    count, mine = (lax.axis_size(axis), lax.axis_index(axis))
    pieces = lax.all_gather(value, axis)
    total = jnp.full_like(value, 0) + jnp.asarray(neutral, value.dtype)

    def turn(position, total):
        longer = join(total, pieces[position])
        return jnp.where(position < mine, longer, total)

    return lax.fori_loop(0, count - 1, turn, total)


def add_counts(earlier, later):
    return earlier + later


def on_device(deltas, labels):
    clients_here = deltas.shape[0]
    width_all = deltas.shape[1] * deltas.shape[2]
    flat = deltas.reshape(clients_here, width_all)
    label_list = labels[:, 0]
    cluster_ids = jnp.arange(CLUSTERS, dtype=jnp.int32)
    one_hot = (label_list[:, None] == cluster_ids[None, :]).astype(jnp.int32)
    counts = jnp.sum(one_hot, axis=0)
    local_rank = jnp.sum((jnp.cumsum(one_hot, axis=0) - one_hot) * one_hot, axis=1)
    offsets = carried_in(counts, ("dp", "group"), add_counts, jnp.zeros((CLUSTERS,), jnp.int32))
    totals = lax.psum(counts.astype(jnp.float32), ("dp", "group"))
    cluster_rank = (local_rank + jnp.sum(one_hot * offsets[None, :], axis=1)).astype(jnp.int32)
    local_sums = jnp.dot(one_hot.T.astype(jnp.bfloat16), flat, preferred_element_type=jnp.float32)
    summed = lax.psum(local_sums, ("dp", "group"))
    models = (summed / totals[:, None]).astype(jnp.bfloat16)
    returned = jnp.dot(one_hot.astype(jnp.bfloat16), models, preferred_element_type=jnp.float32)
    returned = returned.astype(jnp.bfloat16).reshape(deltas.shape)
    return (returned, cluster_rank)


def solution(mesh):
    placed = (P(("dp", "group"), None, None), P(("dp", "group"), None))
    return jax.shard_map(
        on_device,
        mesh=mesh,
        in_specs=placed,
        out_specs=(P(("dp", "group"), None, None), P(("dp", "group"))),
        check_vma=False,
    )
```

profile of v0, /device:TPU:0, one launch (start us, length us, event | category | flops | bytes accessed | tf_op | source)
XLA Modules:
  0.0 189.7 jit_solution(11993705674040085526)
XLA Ops:
  7.2 0.0 all-reduce.3.cloned.1.call-start
  7.2 0.0 copy-start
  7.2 12.2 %copy.4 = bf16[8,8,16,4096]{3,1,2,0:T(8,128)(2,1)} copy(bf16[8,8,16,4096]{3,2,1,0:T(8,128)(2,1)} %bitcast.12) | data formatting | bytes 16777216
  19.4 0.0 copy-done
  19.4 5.9 %fusion.5 = f32[8,65536]{1,0:T(8,128)} fusion(bf16[64,65536]{1,0:T(8,128)(2,1)} %bitcast.11, s32[64]{0:T(128)S(1)} %bitcast.14), kind=kOutput, calls=%fused_computation.16 | convolution fusion | flops 67110400 | bytes 10486016 | tf_op jit(solution)/shard_map/dot_general | solution.py:37
  25.3 0.0 all-reduce.3.cloned.1.call-update
  25.3 0.1 convert_reduce_fusion
  25.5 0.2 dynamic-update-slice
  25.7 42.1 %all-reduce = s32[256]{0:T(256)S(1)} all-reduce(s32[256]{0:T(256)S(1)} %dynamic-update-slice), channel_id=2, replica_groups=mesh['dp'=8,'group'=4] {'dp','group'}, use_global_device_ids=true, to_apply=%add | all-reduce | flops 256 | bytes 2048
  67.8 0.1 reshape.14
  67.9 1.2 while.14
  69.2 40.3 %psum.15 = f32[8]{0:T(128)S(1)} all-reduce(f32[8]{0:T(128)S(1)} %convert_element_type.25), channel_id=1, replica_groups=mesh['dp'=8,'group'=4] {'dp','group'}, use_global_device_ids=true, to_apply=%region_2.3 | all-reduce | flops 8 | bytes 64 | tf_op jit(solution)/shard_map/psum | solution.py:35
  109.5 0.1 fusion.3
  109.5 0.1 reduce_window_sum.11
  109.6 0.2 select_reduce_fusion
  109.8 0.5 add.39
  110.3 53.1 %all-reduce.3.cloned.1.call-done = f32[8,65536]{1,0:T(8,128)} async-done(((f32[8,65536]{1,0:T(8,128)}), f32[8,65536]{1,0:T(8,128)}) %all-reduce.3.cloned.1.call-update) | async-done | bytes 2097168 | tf_op jit(solution)/shard_map/psum | solution.py:38
  163.5 7.2 %convolution_convert_fusion = bf16[64,65536]{1,0:T(8,128)(2,1)} fusion(f32[8,65536]{1,0:T(8,128)} %all-reduce.3.cloned.1.call-done, f32[8]{0:T(128)S(1)} %psum.15, s32[64]{0:T(128)S(1)} %bitcast.18), kind=kOutput, calls=%fused_computation.2 | convolution fusion | flops 72353280 | bytes 10486048 | tf_op jit(solution)/shard_map/dot_general | solution.py:40
  170.7 12.1 %copy.5 = bf16[8,8,16,4096]{3,2,1,0:T(8,128)(2,1)} copy(bf16[8,8,16,4096]{3,1,2,0:T(8,128)(2,1)} %bitcast.10) | data formatting | bytes 16777216
  (34 shorter events, 0.5 us)
Async XLA Ops:
  7.2 156.3 %all-reduce.3.cloned.1.call-start = ((), (), s32[]{:S(2)}) async-start(), calls=%async_computation | async-start | bytes 4194304 | tf_op jit(solution)/shard_map/psum | solution.py:38
  7.2 12.2 %copy-start = (s32[64,1]{0,1:T(1,128)S(1)}, s32[64,1]{0,1:T(1,128)}, u32[]{:S(2)}) copy-start(s32[64,1]{0,1:T(1,128)} %param.5) | copy-start | bytes 772
Sparse Core Ops, SparseCore 0:
  25.5 137.9 all-reduce.2
where the time goes:
time: 190 us
  blocking collectives  82.4 us (43%)
  waiting for transfers between devices  53.2 us (28%)
  local copies, waits for them, and re-layouts  24.6 us (13%)
  between operations  14.1 us (7%)
  matrix products  13.1 us (7%)
    psum x1, waiting for transfers between devices, on_device(): summed = lax.psum(local_sums, ('dp', 'group'))  53.1 us
    unnamed x1, blocking collectives  42.1 us
    psum x1, blocking collectives, on_device(): totals = lax.psum(counts.astype(jnp.float32), ('dp', 'group'))  40.3 us
    unnamed x6, local copies, waits for them, and re-layouts  24.5 us
    dot_general x1, matrix products, on_device(): jnp.dot(one_hot.astype(jnp.bfloat16), models, preferred_element_type=jnp....  7.19 us
    dot_general x1, matrix products, on_device(): jnp.dot(one_hot.T.astype(jnp.bfloat16), flat, preferred_element_type=jnp....  5.93 us
  transfers between devices with their start and end apart: 1, of which 1 were waited for; matrix products, arithmetic and copies ran while one was open for 1% of the time, Pallas kernels for 0%

commit v1 on v0

v1 whole, which is shorter than its diff:
```python
import functools

import jax
import jax.numpy as jnp
from jax import lax
from jax.experimental import pallas as pl
from jax.experimental.pallas import tpu as pltpu
from jax.sharding import PartitionSpec as P

CLUSTERS = 8
LANES = 128
AXES = ("dp", "group")
CHAINS = 2

VMEM = pl.BlockSpec(memory_space=pltpu.VMEM)
SMEM = pl.BlockSpec(memory_space=pltpu.SMEM)
ANY = pl.BlockSpec(memory_space=pl.ANY)


def count_rows(devices):
    return CLUSTERS * pl.cdiv(devices, LANES)


def local_sums_kernel(chain, devices, where, deltas, labels_row, other, mine, held, sems):
    clients, blocks, width = deltas.shape
    me = where[0]
    core = me & 1
    columns = width // CHAINS // 4
    copies = []
    for part in range(4):
        half = (1 - core) if part < 2 else core
        start = ((chain * 2 + half) * 2 + part % 2) * columns
        copies.append(pltpu.make_async_copy(
            deltas.at[:, :, pl.ds(pl.multiple_of(start, LANES), columns)], held.at[part], sems.at[part]))
        copies[-1].start()

    rows, depth = CLUSTERS * blocks, clients * blocks
    labels = labels_row[...]
    spread = (lax.broadcasted_iota(jnp.int32, (clients, depth), 1) // blocks
              == lax.broadcasted_iota(jnp.int32, (clients, depth), 0)).astype(jnp.bfloat16)
    wide = jnp.dot(jnp.broadcast_to(labels, (16, clients)).astype(jnp.bfloat16), spread,
                   preferred_element_type=jnp.float32)[0:1].astype(jnp.int32)
    row = lax.broadcasted_iota(jnp.int32, (rows, depth), 0)
    column = lax.broadcasted_iota(jnp.int32, (rows, depth), 1)
    pick = ((wide == row // blocks) & (column % blocks == row % blocks)).astype(jnp.bfloat16)

    hits = (labels == lax.broadcasted_iota(jnp.int32, (CLUSTERS, clients), 0)).astype(jnp.float32)
    counts = jnp.sum(hits, axis=1, keepdims=True)
    lane = lax.broadcasted_iota(jnp.int32, (CLUSTERS, LANES), 1)
    filled = 4 * (columns // 2) // LANES * rows
    for tile in range(count_rows(devices) // CLUSTERS):
        table = jnp.where(lane + tile * LANES == me, counts, 0.0)
        at = filled + tile * CLUSTERS
        other[at:at + CLUSTERS, :] = table
        mine[at:at + CLUSTERS, :] = table

    per_part = columns // LANES
    for part in range(4):
        copies[part].wait()
        sums = jnp.dot(pick, held[part].reshape(depth, columns), preferred_element_type=jnp.float32)
        target = other if part < 2 else mine
        for block in range(per_part):
            at = (part % 2 * per_part + block) * rows
            target[at:at + rows, :] = sums[:, block * LANES:(block + 1) * LANES]


def local_sums(chain, devices, where, deltas, labels_row):
    clients, blocks, width = deltas.shape
    columns = width // CHAINS // 4
    height = 2 * columns // LANES * CLUSTERS * blocks + count_rows(devices)
    out = jax.ShapeDtypeStruct((height, LANES), jnp.float32)
    return pl.pallas_call(
        functools.partial(local_sums_kernel, chain, devices),
        out_shape=(out, out),
        in_specs=[SMEM, ANY, VMEM],
        out_specs=(VMEM, VMEM),
        scratch_shapes=[pltpu.VMEM((4, clients, blocks, columns), jnp.bfloat16), pltpu.SemaphoreType.DMA((4,))],
        name="local_sums",
    )(where, deltas, labels_row)


def split_kernel(tail, pick, kept, arrived, send, keep):
    half = (kept.shape[0] - tail) // 2
    bit = pick[0]
    for target, which in ((send, 1 - bit), (keep, bit)):
        rows = pl.ds(pl.multiple_of(which * half, CLUSTERS), half)
        target[0:half, :] = kept[rows, :] + arrived[rows, :]
        target[half:half + tail, :] = kept[2 * half:2 * half + tail, :] + arrived[2 * half:2 * half + tail, :]


def split(tail, bit, kept, arrived):
    half = (kept.shape[0] - tail) // 2
    out = jax.ShapeDtypeStruct((half + tail, LANES), jnp.float32)
    return pl.pallas_call(
        functools.partial(split_kernel, tail),
        out_shape=(out, out),
        in_specs=[SMEM, VMEM, VMEM],
        out_specs=(VMEM, VMEM),
        name="split",
    )(bit, kept, arrived)


def finish_kernel(tail, blocks, kept, arrived, models):
    rows = CLUSTERS * blocks
    height = kept.shape[0] - tail
    totals = jnp.zeros((CLUSTERS, 1), jnp.float32)
    for at in range(height, height + tail, CLUSTERS):
        table = kept[at:at + CLUSTERS, :] + arrived[at:at + CLUSTERS, :]
        totals = totals + jnp.sum(table, axis=1, keepdims=True)
    for cluster in range(CLUSTERS):
        total = jnp.broadcast_to(totals[cluster:cluster + 1, :], (blocks, LANES))
        for block in range(height // rows):
            at = block * rows + cluster * blocks
            sums = kept[at:at + blocks, :] + arrived[at:at + blocks, :]
            models[cluster * blocks:(cluster + 1) * blocks, block * LANES:(block + 1) * LANES] = (
                sums / total).astype(jnp.bfloat16)


def finish(tail, blocks, kept, arrived):
    rows = CLUSTERS * blocks
    columns = (kept.shape[0] - tail) // rows * LANES
    return pl.pallas_call(
        functools.partial(finish_kernel, tail, blocks),
        out_shape=jax.ShapeDtypeStruct((rows, columns), jnp.bfloat16),
        in_specs=[VMEM, VMEM],
        out_specs=VMEM,
        name="finish",
    )(kept, arrived)


def rank_kernel(tail, where, kept, arrived, labels_row, labels_column, rank):
    height = kept.shape[0] - tail
    clients = labels_row.shape[1]
    lane = lax.broadcasted_iota(jnp.int32, (CLUSTERS, LANES), 1)
    before = jnp.zeros((CLUSTERS, 1), jnp.float32)
    for tile in range(tail // CLUSTERS):
        at = height + tile * CLUSTERS
        table = kept[at:at + CLUSTERS, :] + arrived[at:at + CLUSTERS, :]
        before = before + jnp.sum(jnp.where(lane + tile * LANES < where[0], table, 0.0), axis=1, keepdims=True)
    labels = labels_row[...]
    hits = labels == lax.broadcasted_iota(jnp.int32, (CLUSTERS, clients), 0)
    offset = jnp.sum(jnp.where(hits, before, 0.0), axis=0, keepdims=True)
    earlier = (lax.broadcasted_iota(jnp.int32, (clients, clients), 0)
               < lax.broadcasted_iota(jnp.int32, (clients, clients), 1))
    local = jnp.sum(jnp.where((labels_column[...] == labels) & earlier, 1.0, 0.0), axis=0, keepdims=True)
    rank[...] = (offset + local).astype(jnp.int32)


def ranks(tail, where, kept, arrived, labels_row, labels_column):
    return pl.pallas_call(
        functools.partial(rank_kernel, tail),
        out_shape=jax.ShapeDtypeStruct(labels_row.shape, jnp.int32),
        in_specs=[SMEM, VMEM, VMEM, VMEM, VMEM],
        out_specs=VMEM,
        name="ranks",
    )(where, kept, arrived, labels_row, labels_column)


def return_kernel(pick, labels, models, *rest):
    returned, laid, sem = rest[-3:]
    pieces, rows, columns = models.shape
    clients, blocks, _ = returned.shape
    for piece in range(pieces):
        slot = piece ^ pick[1]
        for cluster in range(CLUSTERS):
            laid[cluster, :, piece * columns:(piece + 1) * columns] = models[
                slot, cluster * blocks:(cluster + 1) * blocks, :]
    start = pl.multiple_of(pick[0] * (pieces * columns), LANES)

    def copy(client):
        return pltpu.make_async_copy(
            laid.at[labels[client]], returned.at[client, :, pl.ds(start, pieces * columns)], sem)

    for client in range(clients):
        copy(client).start()
    for client in range(clients):
        copy(client).wait()


def give_back(pick, labels, models, shape, returned):
    pieces, rows, columns = models.shape
    blocks = shape[1]
    given = () if returned is None else (returned,)
    return pl.pallas_call(
        return_kernel,
        out_shape=jax.ShapeDtypeStruct(shape, jnp.bfloat16),
        in_specs=[SMEM, SMEM, VMEM] + [ANY] * len(given),
        out_specs=ANY,
        scratch_shapes=[pltpu.VMEM((CLUSTERS, blocks, pieces * columns), jnp.bfloat16), pltpu.SemaphoreType.DMA],
        input_output_aliases={3: 0} if given else {},
        name="give_back",
    )(pick, labels, models, *given)


def on_device(devices, deltas, labels):
    clients, blocks, width = deltas.shape
    me = lax.axis_index(AXES).astype(jnp.int32)
    where = me.reshape(1)
    labels_row = labels.reshape(1, clients)
    labels_list = labels.reshape(clients)
    tail = count_rows(devices)
    bits = devices.bit_length() - 1
    core = me & 1

    def send(value, flip):
        return lax.ppermute(value, AXES, [(i, i ^ flip(i)) for i in range(devices)])

    def order(chain, low, high):
        def at(step):
            def flip(i):
                taken = list(range(low, high))
                if (i & 1) ^ chain:
                    taken = taken[::-1]
                return 1 << taken[step]
            return flip
        return at

    def bit_at(core, chain, step):
        return (me >> (1 + (core ^ chain ^ step))) & 1

    state = []
    for chain in range(CHAINS):
        state.append(local_sums(chain, devices, where, deltas, labels_row))
    returned, rank = None, None
    kept = [None] * CHAINS
    for chain in range(CHAINS):
        other, mine = state[chain]
        arrived = send(other, lambda i: 1)
        kept[chain] = split(tail, bit_at(core, chain, 0).reshape(1), mine, arrived)
    scatter = [order(chain, 1, 3) for chain in range(CHAINS)]
    reduce = [order(chain, 3, bits) for chain in range(CHAINS)]
    for chain in range(CHAINS):
        out, keep = kept[chain]
        kept[chain] = split(tail, bit_at(core, chain, 1).reshape(1), keep, send(out, scatter[chain](0)))
    for chain in range(CHAINS):
        out, keep = kept[chain]
        kept[chain] = (keep, send(out, scatter[chain](1)))
    for step in range(bits - 3):
        for chain in range(CHAINS):
            keep, arrived = kept[chain]
            total = keep + arrived
            kept[chain] = (total, send(total, reduce[chain](step)))
    rank = ranks(tail, where, *kept[0], labels_row, labels)
    models = [finish(tail, blocks, *kept[chain])[None] for chain in range(CHAINS)]
    for step in (1, 0):
        for chain in range(CHAINS):
            own = models[chain]
            models[chain] = jnp.concatenate([own, send(own, scatter[chain](step))], axis=0)
    for chain in range(CHAINS):
        arrived = send(models[chain], lambda i: 1)
        for half, value in ((core, models[chain]), (1 - core, arrived)):
            mask = bit_at(half, chain, 0) * 2 + bit_at(half, chain, 1)
            pick = jnp.stack([chain * 2 + half, mask])
            returned = give_back(pick, labels_list, value, deltas.shape, returned)
    return returned, rank.reshape(clients)


def solution(mesh):
    devices = mesh.shape["dp"] * mesh.shape["group"]
    placed = (P(AXES, None, None), P(AXES, None))
    return jax.shard_map(
        functools.partial(on_device, devices),
        mesh=mesh,
        in_specs=placed,
        out_specs=(P(AXES, None, None), P(AXES)),
        check_vma=False,
    )
```

time: 190 us -> 80.3 us (0.42)
  blocking collectives: 82.4 us -> 0 us
  waiting for transfers between devices: 53.2 us -> 8.92 us
  Pallas kernels: 0 us -> 29.8 us
  starting transfers between devices: 0.04 us -> 26 us
  local copies, waits for them, and re-layouts: 24.6 us -> 6.38 us
  between operations: 14.1 us -> 0.83 us
  matrix products: 13.1 us -> 0 us
  other arithmetic: 1.51 us -> 7.83 us
    psum x1 -> x0, waiting for transfers between devices: 53.1 us -> none  [on_device(): summed = lax.psum(local_sums, ('dp', 'group'))]
    unnamed x1 -> x0, blocking collectives: 42.1 us -> none
    psum x1 -> x0, blocking collectives: 40.3 us -> none  [on_device(): totals = lax.psum(counts.astype(jnp.float32), ('dp', 'group'))]
    pallas_call x0 -> x13, Pallas kernels: none -> 29.8 us  [the longest x4 9.11 us: give_back(): pl.pallas_call(return_kernel, out_shape=jax.ShapeDtypeStruct(shape, jnp.b...]
    ppermute x0 -> x16, starting transfers between devices: none -> 26 us  [send(): return lax.ppermute(value, AXES, [(i, i ^ flip(i)) for i in range(devices)])]
    unnamed x6 -> x27, local copies, waits for them, and re-layouts: 24.5 us -> 6.38 us
    dot_general x2 -> x0, matrix products: 13.1 us -> none  [the longest x1 7.19 us: on_device(): jnp.dot(one_hot.astype(jnp.bfloat16), models, preferred_element_type=jnp....]
    ppermute x0 -> x16, waiting for transfers between devices: none -> 8.92 us  [send(): return lax.ppermute(value, AXES, [(i, i ^ flip(i)) for i in range(devices)])]
  transfers between devices with their start and end apart: 1 -> 16, of which waited for: 1 -> 7; matrix products, arithmetic and copies ran while one was open for 1% -> 11% of each run, Pallas kernels for 0% -> 29%
where the time goes in v1:
time: 80.3 us; the launch traced here: 79.7 us
  Pallas kernels  29.8 us (37%)
  starting transfers between devices  26 us (32%)
  waiting for transfers between devices  8.92 us (11%)
  other arithmetic  7.83 us (10%)
  local copies, waits for them, and re-layouts  6.38 us (8%)
  between operations  0.83 us (1%)
    ppermute x16, starting transfers between devices, send(): return lax.ppermute(value, AXES, [(i, i ^ flip(i)) for i in range(devices)])  26 us
    pallas_call x4, Pallas kernels, give_back(): pl.pallas_call(return_kernel, out_shape=jax.ShapeDtypeStruct(shape, jnp.b...  9.11 us
    ppermute x16, waiting for transfers between devices, send(): return lax.ppermute(value, AXES, [(i, i ^ flip(i)) for i in range(devices)])  8.92 us
    pallas_call x2, Pallas kernels, local_sums(): pl.pallas_call(functools.partial(local_sums_kernel, chain, devices), out_...  8 us
    pallas_call x4, Pallas kernels, split(): pl.pallas_call(functools.partial(split_kernel, tail), out_shape=(out, out...  7.69 us
    unnamed x27, local copies, waits for them, and re-layouts  6.38 us
    concatenate x4, other arithmetic, on_device(): jnp.concatenate([own, send(own, scatter[chain](step))], axis=0)  3.44 us
    pallas_call x2, Pallas kernels, finish(): pl.pallas_call(functools.partial(finish_kernel, tail, blocks), out_shape=...  3.37 us
  transfers between devices with their start and end apart: 16, of which 7 were waited for; matrix products, arithmetic and copies ran while one was open for 11% of the time, Pallas kernels for 29%

profile of v1, /device:TPU:0, one launch (start us, length us, event | category | flops | bytes accessed | tf_op | source)
XLA Modules:
  0.0 79.7 jit_solution(2679364297079487403)
XLA Ops:
  0.6 4.0 %local_sums.3 = (f32[1032,128]{1,0:T(8,128)}, f32[1032,128]{1,0:T(8,128)}) custom-call(s32[1]{0:T(128)} %bitcast.5.where, bf16[64,16,4096]{2,1,0:T(8,128)(2,1)} %deltas.3, s32[1,64]{1,0:T(1,128)} %bitcast.23), custom_call_target="tpu_custom_call" | custom-call | tf_op jit(solution)/shard_map/local_sums/pallas_call | solution.py:72
  5.2 4.0 %local_sums.2 = (f32[1032,128]{1,0:T(8,128)}, f32[1032,128]{1,0:T(8,128)}) custom-call(s32[1]{0:T(128)} %bitcast.5.where, bf16[64,16,4096]{2,1,0:T(8,128)(2,1)} %deltas.3, s32[1,64]{1,0:T(1,128)} %bitcast.24), custom_call_target="tpu_custom_call" | custom-call | tf_op jit(solution)/shard_map/local_sums/pallas_call | solution.py:72
  10.1 2.1 %split.6 = (f32[520,128]{1,0:T(8,128)}, f32[520,128]{1,0:T(8,128)}) custom-call(s32[1]{0:T(128)} %bitcast.12.pick, f32[1032,128]{1,0:T(8,128)} %get-tuple-element.20.kept, f32[1032,128]{1,0:T(8,128)} %copy-done.6), custom_call_target="tpu_custom_call" | custom-call | tf_op jit(solution)/shard_map/split/pallas_call | solution.py:94
  12.2 3.0 %collective-permute-start.9 = (f32[520,128]{1,0:T(8,128)}, f32[520,128]{1,0:T(8,128)S(1)}, u32[]{:S(2)}, u32[]{:S(2)}) collective-permute-start(f32[520,128]{1,0:T(8,128)} %get-tuple-element.23), channel_id=1, source_target_pairs={{0,2},{1,5},{2,0},{3,7},{4,6},{5,1},{6,4},{7,3},{8,10},{9,13},{10,... | collective-permute-start | bytes 798728 | tf_op jit(solution)/shard_map/ppermute | solution.py:206
  15.9 2.1 %split.4 = (f32[520,128]{1,0:T(8,128)}, f32[520,128]{1,0:T(8,128)}) custom-call(s32[1]{0:T(128)} %bitcast.4.pick, f32[1032,128]{1,0:T(8,128)} %get-tuple-element.14.kept, f32[1032,128]{1,0:T(8,128)} %copy-done.5), custom_call_target="tpu_custom_call" | custom-call | tf_op jit(solution)/shard_map/split/pallas_call | solution.py:94
  18.0 1.5 %collective-permute-start.1 = (f32[520,128]{1,0:T(8,128)}, f32[520,128]{1,0:T(8,128)S(1)}, u32[]{:S(2)}, u32[]{:S(2)}) collective-permute-start(f32[520,128]{1,0:T(8,128)} %get-tuple-element.17), channel_id=1, source_target_pairs={{0,4},{1,3},{2,6},{3,1},{4,0},{5,7},{6,2},{7,5},{8,12},{9,11},{10,... | collective-permute-start | bytes 798728 | tf_op jit(solution)/shard_map/ppermute | solution.py:206
  20.4 1.8 %split.7 = (f32[264,128]{1,0:T(8,128)}, f32[264,128]{1,0:T(8,128)}) custom-call(s32[1]{0:T(128)} %bitcast.4.pick, f32[520,128]{1,0:T(8,128)} %get-tuple-element.22.kept, f32[520,128]{1,0:T(8,128)} %copy-done.8), custom_call_target="tpu_custom_call" | custom-call | tf_op jit(solution)/shard_map/split/pallas_call | solution.py:94
  22.2 3.0 %collective-permute-start.10 = (f32[264,128]{1,0:T(8,128)}, f32[264,128]{1,0:T(8,128)S(1)}, u32[]{:S(2)}, u32[]{:S(2)}) collective-permute-start(f32[264,128]{1,0:T(8,128)} %get-tuple-element.25), channel_id=1, source_target_pairs={{0,4},{1,3},{2,6},{3,1},{4,0},{5,7},{6,2},{7,5},{8,12},{9,11},{10,... | collective-permute-start | bytes 405512 | tf_op jit(solution)/shard_map/ppermute | solution.py:206
  25.9 1.8 %split.5 = (f32[264,128]{1,0:T(8,128)}, f32[264,128]{1,0:T(8,128)}) custom-call(s32[1]{0:T(128)} %bitcast.3.pick, f32[520,128]{1,0:T(8,128)} %get-tuple-element.16.kept, f32[520,128]{1,0:T(8,128)} %copy-done.7), custom_call_target="tpu_custom_call" | custom-call | tf_op jit(solution)/shard_map/split/pallas_call | solution.py:94
  29.9 1.6 %collective-permute-start.11 = (f32[264,128]{1,0:T(8,128)S(1)}, f32[264,128]{1,0:T(8,128)S(1)}, u32[]{:S(2)}, u32[]{:S(2)}) collective-permute-start(f32[264,128]{1,0:T(8,128)S(1)} %add.73), channel_id=1, source_target_pairs={{0,8},{1,17},{2,10},{3,19},{4,12},{5,21},{6,14},{7,23},{8,0},{9,25... | collective-permute-start | bytes 405512 | tf_op jit(solution)/shard_map/ppermute | solution.py:206
  33.8 2.4 %collective-permute-start.3 = (f32[264,128]{1,0:T(8,128)S(1)}, f32[264,128]{1,0:T(8,128)S(1)}, u32[]{:S(2)}, u32[]{:S(2)}) collective-permute-start(f32[264,128]{1,0:T(8,128)S(1)} %add.66), channel_id=1, source_target_pairs={{0,16},{1,9},{2,18},{3,11},{4,20},{5,13},{6,22},{7,15},{8,24},{9,1... | collective-permute-start | bytes 405512 | tf_op jit(solution)/shard_map/ppermute | solution.py:206
  36.4 2.5 %collective-permute-start.12 = (f32[264,128]{1,0:T(8,128)S(1)}, f32[264,128]{1,0:T(8,128)S(1)}, u32[]{:S(2)}, u32[]{:S(2)}) collective-permute-start(f32[264,128]{1,0:T(8,128)S(1)} %add.74.kept), channel_id=1, source_target_pairs={{0,16},{1,9},{2,18},{3,11},{4,20},{5,13},{6,22},{7,15},{8,24},{9,1... | collective-permute-start | bytes 405512 | tf_op jit(solution)/shard_map/ppermute | solution.py:206
  38.9 1.8 %collective-permute-done.3 = f32[264,128]{1,0:T(8,128)S(1)} collective-permute-done((f32[264,128]{1,0:T(8,128)S(1)}, f32[264,128]{1,0:T(8,128)S(1)}, u32[]{:S(2)}, u32[]{:S(2)}) %collective-permute-start.3) | collective-permute-done | bytes 135200 | tf_op jit(solution)/shard_map/ppermute | solution.py:206
  40.8 5.0 %collective-permute-start.4 = (f32[264,128]{1,0:T(8,128)S(1)}, f32[264,128]{1,0:T(8,128)S(1)}, u32[]{:S(2)}, u32[]{:S(2)}) collective-permute-start(f32[264,128]{1,0:T(8,128)S(1)} %add.67.kept), channel_id=1, source_target_pairs={{0,8},{1,17},{2,10},{3,19},{4,12},{5,21},{6,14},{7,23},{8,0},{9,25... | collective-permute-start | bytes 405512 | tf_op jit(solution)/shard_map/ppermute | solution.py:206
  47.7 1.7 %finish.3 = bf16[128,256]{1,0:T(8,128)(2,1)} custom-call(f32[264,128]{1,0:T(8,128)} %copy-done, f32[264,128]{1,0:T(8,128)} %copy-done.3), custom_call_target="tpu_custom_call" | custom-call | tf_op jit(solution)/shard_map/finish/pallas_call | solution.py:122
  51.3 1.7 %finish.2 = bf16[128,256]{1,0:T(8,128)(2,1)} custom-call(f32[264,128]{1,0:T(8,128)} %copy-done.4, f32[264,128]{1,0:T(8,128)} %copy-done.11), custom_call_target="tpu_custom_call" | custom-call | tf_op jit(solution)/shard_map/finish/pallas_call | solution.py:122
  54.8 1.9 %collective-permute-start.14 = (bf16[2,128,256]{2,1,0:T(8,128)(2,1)S(1)}, bf16[2,128,256]{2,1,0:T(8,128)(2,1)S(1)}, u32[]{:S(2)}, u32[]{:S(2)}) collective-permute-start(bf16[2,128,256]{2,1,0:T(8,128)(2,1)S(1)} %pad_maximum_fusion.3), channel_id=1, source_target_pairs={{0,2},{1,5},{2,0},{3,7},{4,6},{5,1},{6,4},{7,3},{8,10},{9,13},{10,... | collective-permute-start | bytes 393224 | tf_op jit(solution)/shard_map/ppermute | solution.py:206
  56.7 1.4 %collective-permute-done.5 = bf16[1,128,256]{2,1,0:T(8,128)(2,1)S(1)} collective-permute-done((bf16[1,128,256]{2,1,0:T(8,128)(2,1)}, bf16[1,128,256]{2,1,0:T(8,128)(2,1)S(1)}, u32[]{:S(2)}, u32[]{:S(2)}) %collective-permute-start.5) | collective-permute-done | bytes 65568 | tf_op jit(solution)/shard_map/ppermute | solution.py:206
  61.4 2.6 %collective-permute-done.6 = bf16[2,128,256]{2,1,0:T(8,128)(2,1)S(1)} collective-permute-done((bf16[2,128,256]{2,1,0:T(8,128)(2,1)S(1)}, bf16[2,128,256]{2,1,0:T(8,128)(2,1)S(1)}, u32[]{:S(2)}, u32[]{:S(2)}) %collective-permute-start.6) | collective-permute-done | bytes 131104 | tf_op jit(solution)/shard_map/ppermute | solution.py:206
  67.6 1.6 %ranks.1 = s32[1,64]{1,0:T(1,128)} custom-call(s32[1]{0:T(128)} %bitcast.5.where, f32[264,128]{1,0:T(8,128)} %copy-done, f32[264,128]{1,0:T(8,128)} %copy-done.3, s32[1,64]{1,0:T(1,128)} %bitcast.25, s32[64,1]{1,0:T(8,128)} %copy.7.labels_column), custom_call_target="tpu_custom_call" | custom-call | tf_op jit(solution)/shard_map/ranks/pallas_call | solution.py:150
  69.2 2.3 %give_back.4.rest_0_ = bf16[64,16,4096]{2,1,0:T(8,128)(2,1)} custom-call(s32[2]{0:T(128)} %pad_add_fusion.3.pick, s32[64]{0:T(128)} %bitcast.26, bf16[4,128,256]{2,1,0:T(8,128)(2,1)} %copy-done.2), custom_call_target="tpu_custom_call" | custom-call | tf_op jit(solution)/shard_map/give_back/pallas_call | solution.py:184
  72.2 2.3 %give_back.5.rest_0_ = bf16[64,16,4096]{2,1,0:T(8,128)(2,1)} custom-call(s32[2]{0:T(128)} %pad_add_fusion.2.pick, s32[64]{0:T(128)} %bitcast.27, bf16[4,128,256]{2,1,0:T(8,128)(2,1)} %copy-done.9, bf16[64,16,4096]{2,1,0:T(8,128)(2,1)} %give_back.4.rest_0_), custom_call_target="tpu_custom_call", output_to_operand_aliasing={{}: (3, {})} | custom-call | tf_op jit(solution)/shard_map/give_back/pallas_call | solution.py:184
  74.5 2.3 %give_back.6.rest_0_ = bf16[64,16,4096]{2,1,0:T(8,128)(2,1)} custom-call(s32[2]{0:T(128)} %pad_add_fusion.1.pick, s32[64]{0:T(128)} %bitcast.28, bf16[4,128,256]{2,1,0:T(8,128)(2,1)} %copy-done.1, bf16[64,16,4096]{2,1,0:T(8,128)(2,1)} %give_back.5.rest_0_), custom_call_target="tpu_custom_call", output_to_operand_aliasing={{}: (3, {})} | custom-call | tf_op jit(solution)/shard_map/give_back/pallas_call | solution.py:184
  77.4 2.3 %give_back.7 = bf16[64,16,4096]{2,1,0:T(8,128)(2,1)} custom-call(s32[2]{0:T(128)} %pad_add_fusion.pick, s32[64]{0:T(128)} %bitcast.29, bf16[4,128,256]{2,1,0:T(8,128)(2,1)} %copy-done.10, bf16[64,16,4096]{2,1,0:T(8,128)(2,1)} %give_back.6.rest_0_), custom_call_target="tpu_custom_call", output_to_operand_aliasing={{}: (3, {})} | custom-call | tf_op jit(solution)/shard_map/give_back/pallas_call | solution.py:184
  (60 shorter events, 22.4 us)
Async XLA Ops:
  4.6 61.0 %copy-start.12 = (s32[64,1]{0,1:T(1,128)S(1)}, s32[64,1]{0,1:T(1,128)}, u32[]{:S(2)}) copy-start(s32[64,1]{0,1:T(1,128)} %param.3) | copy-start | bytes 772
  4.7 4.6 %collective-permute-start.8 = (f32[1032,128]{1,0:T(8,128)}, f32[1032,128]{1,0:T(8,128)S(1)}, u32[]{:S(2)}, u32[]{:S(2)}) collective-permute-start(f32[1032,128]{1,0:T(8,128)} %get-tuple-element.21), channel_id=1, source_target_pairs={{0,1},{1,0},{2,3},{3,2},{4,5},{5,4},{6,7},{7,6},{8,9},{9,8},{10,11... | collective-permute-start | bytes 1585160 | tf_op jit(solution)/shard_map/ppermute | solution.py:206
  9.2 5.9 %collective-permute-start = (f32[1032,128]{1,0:T(8,128)}, f32[1032,128]{1,0:T(8,128)S(1)}, u32[]{:S(2)}, u32[]{:S(2)}) collective-permute-start(f32[1032,128]{1,0:T(8,128)} %get-tuple-element.15), channel_id=1, source_target_pairs={{0,1},{1,0},{2,3},{3,2},{4,5},{5,4},{6,7},{7,6},{8,9},{9,8},{10,11... | collective-permute-start | bytes 1585160 | tf_op jit(solution)/shard_map/ppermute | solution.py:206
  9.3 0.8 copy-start.6
  12.2 7.6 %collective-permute-start.9 = (f32[520,128]{1,0:T(8,128)}, f32[520,128]{1,0:T(8,128)S(1)}, u32[]{:S(2)}, u32[]{:S(2)}) collective-permute-start(f32[520,128]{1,0:T(8,128)} %get-tuple-element.23), channel_id=1, source_target_pairs={{0,2},{1,5},{2,0},{3,7},{4,6},{5,1},{6,4},{7,3},{8,10},{9,13},{10,... | collective-permute-start | bytes 798728 | tf_op jit(solution)/shard_map/ppermute | solution.py:206
  15.1 0.8 copy-start.5
  18.0 7.2 %collective-permute-start.1 = (f32[520,128]{1,0:T(8,128)}, f32[520,128]{1,0:T(8,128)S(1)}, u32[]{:S(2)}, u32[]{:S(2)}) collective-permute-start(f32[520,128]{1,0:T(8,128)} %get-tuple-element.17), channel_id=1, source_target_pairs={{0,4},{1,3},{2,6},{3,1},{4,0},{5,7},{6,2},{7,5},{8,12},{9,11},{10,... | collective-permute-start | bytes 798728 | tf_op jit(solution)/shard_map/ppermute | solution.py:206
  22.2 6.7 %collective-permute-start.10 = (f32[264,128]{1,0:T(8,128)}, f32[264,128]{1,0:T(8,128)S(1)}, u32[]{:S(2)}, u32[]{:S(2)}) collective-permute-start(f32[264,128]{1,0:T(8,128)} %get-tuple-element.25), channel_id=1, source_target_pairs={{0,4},{1,3},{2,6},{3,1},{4,0},{5,7},{6,2},{7,5},{8,12},{9,11},{10,... | collective-permute-start | bytes 405512 | tf_op jit(solution)/shard_map/ppermute | solution.py:206
  25.2 0.7 copy-start.7
  27.7 5.2 %collective-permute-start.2 = (f32[264,128]{1,0:T(8,128)}, f32[264,128]{1,0:T(8,128)S(1)}, u32[]{:S(2)}, u32[]{:S(2)}) collective-permute-start(f32[264,128]{1,0:T(8,128)} %get-tuple-element.19), channel_id=1, source_target_pairs={{0,2},{1,5},{2,0},{3,7},{4,6},{5,1},{6,4},{7,3},{8,10},{9,13},{10,... | collective-permute-start | bytes 405512 | tf_op jit(solution)/shard_map/ppermute | solution.py:206
  29.9 6.5 %collective-permute-start.11 = (f32[264,128]{1,0:T(8,128)S(1)}, f32[264,128]{1,0:T(8,128)S(1)}, u32[]{:S(2)}, u32[]{:S(2)}) collective-permute-start(f32[264,128]{1,0:T(8,128)S(1)} %add.73), channel_id=1, source_target_pairs={{0,8},{1,17},{2,10},{3,19},{4,12},{5,21},{6,14},{7,23},{8,0},{9,25... | collective-permute-start | bytes 405512 | tf_op jit(solution)/shard_map/ppermute | solution.py:206
  33.8 6.9 %collective-permute-start.3 = (f32[264,128]{1,0:T(8,128)S(1)}, f32[264,128]{1,0:T(8,128)S(1)}, u32[]{:S(2)}, u32[]{:S(2)}) collective-permute-start(f32[264,128]{1,0:T(8,128)S(1)} %add.66), channel_id=1, source_target_pairs={{0,16},{1,9},{2,18},{3,11},{4,20},{5,13},{6,22},{7,15},{8,24},{9,1... | collective-permute-start | bytes 405512 | tf_op jit(solution)/shard_map/ppermute | solution.py:206
  36.4 10.6 %copy-start = (f32[264,128]{1,0:T(8,128)}, f32[264,128]{1,0:T(8,128)S(1)}, u32[]{:S(2)}) copy-start(f32[264,128]{1,0:T(8,128)S(1)} %add.74.kept) | copy-start | bytes 405508
  36.4 10.6 %collective-permute-start.12 = (f32[264,128]{1,0:T(8,128)S(1)}, f32[264,128]{1,0:T(8,128)S(1)}, u32[]{:S(2)}, u32[]{:S(2)}) collective-permute-start(f32[264,128]{1,0:T(8,128)S(1)} %add.74.kept), channel_id=1, source_target_pairs={{0,16},{1,9},{2,18},{3,11},{4,20},{5,13},{6,22},{7,15},{8,24},{9,1... | collective-permute-start | bytes 405512 | tf_op jit(solution)/shard_map/ppermute | solution.py:206
  40.8 9.9 %copy-start.4 = (f32[264,128]{1,0:T(8,128)}, f32[264,128]{1,0:T(8,128)S(1)}, u32[]{:S(2)}) copy-start(f32[264,128]{1,0:T(8,128)S(1)} %add.67.kept) | copy-start | bytes 405508
  40.8 9.9 %collective-permute-start.4 = (f32[264,128]{1,0:T(8,128)S(1)}, f32[264,128]{1,0:T(8,128)S(1)}, u32[]{:S(2)}, u32[]{:S(2)}) collective-permute-start(f32[264,128]{1,0:T(8,128)S(1)} %add.67.kept), channel_id=1, source_target_pairs={{0,8},{1,17},{2,10},{3,19},{4,12},{5,21},{6,14},{7,23},{8,0},{9,25... | collective-permute-start | bytes 405512 | tf_op jit(solution)/shard_map/ppermute | solution.py:206
  49.4 4.6 %collective-permute-start.13 = (bf16[1,128,256]{2,1,0:T(8,128)(2,1)}, bf16[1,128,256]{2,1,0:T(8,128)(2,1)S(1)}, u32[]{:S(2)}, u32[]{:S(2)}) collective-permute-start(bf16[1,128,256]{2,1,0:T(8,128)(2,1)} %bitcast.17), channel_id=1, source_target_pairs={{0,4},{1,3},{2,6},{3,1},{4,0},{5,7},{6,2},{7,5},{8,12},{9,11},{10,... | collective-permute-start | bytes 196616 | tf_op jit(solution)/shard_map/ppermute | solution.py:206
  53.0 5.2 %collective-permute-start.5 = (bf16[1,128,256]{2,1,0:T(8,128)(2,1)}, bf16[1,128,256]{2,1,0:T(8,128)(2,1)S(1)}, u32[]{:S(2)}, u32[]{:S(2)}) collective-permute-start(bf16[1,128,256]{2,1,0:T(8,128)(2,1)} %bitcast.20), channel_id=1, source_target_pairs={{0,2},{1,5},{2,0},{3,7},{4,6},{5,1},{6,4},{7,3},{8,10},{9,13},{10,... | collective-permute-start | bytes 196616 | tf_op jit(solution)/shard_map/ppermute | solution.py:206
  54.8 5.7 %collective-permute-start.14 = (bf16[2,128,256]{2,1,0:T(8,128)(2,1)S(1)}, bf16[2,128,256]{2,1,0:T(8,128)(2,1)S(1)}, u32[]{:S(2)}, u32[]{:S(2)}) collective-permute-start(bf16[2,128,256]{2,1,0:T(8,128)(2,1)S(1)} %pad_maximum_fusion.3), channel_id=1, source_target_pairs={{0,2},{1,5},{2,0},{3,7},{4,6},{5,1},{6,4},{7,3},{8,10},{9,13},{10,... | collective-permute-start | bytes 393224 | tf_op jit(solution)/shard_map/ppermute | solution.py:206
  59.0 5.0 %collective-permute-start.6 = (bf16[2,128,256]{2,1,0:T(8,128)(2,1)S(1)}, bf16[2,128,256]{2,1,0:T(8,128)(2,1)S(1)}, u32[]{:S(2)}, u32[]{:S(2)}) collective-permute-start(bf16[2,128,256]{2,1,0:T(8,128)(2,1)S(1)} %pad_maximum_fusion.2), channel_id=1, source_target_pairs={{0,4},{1,3},{2,6},{3,1},{4,0},{5,7},{6,2},{7,5},{8,12},{9,11},{10,... | collective-permute-start | bytes 393224 | tf_op jit(solution)/shard_map/ppermute | solution.py:206
  61.4 7.8 %copy-start.2 = (bf16[4,128,256]{2,1,0:T(8,128)(2,1)}, bf16[4,128,256]{2,1,0:T(8,128)(2,1)S(1)}, u32[]{:S(2)}) copy-start(bf16[4,128,256]{2,1,0:T(8,128)(2,1)S(1)} %pad_maximum_fusion.1.models) | copy-start | bytes 786436
  61.4 10.1 %collective-permute-start.15 = (bf16[4,128,256]{2,1,0:T(8,128)(2,1)S(1)}, bf16[4,128,256]{2,1,0:T(8,128)(2,1)S(1)}, u32[]{:S(2)}, u32[]{:S(2)}) collective-permute-start(bf16[4,128,256]{2,1,0:T(8,128)(2,1)S(1)} %pad_maximum_fusion.1.models), channel_id=1, source_target_pairs={{0,1},{1,0},{2,3},{3,2},{4,5},{5,4},{6,7},{7,6},{8,9},{9,8},{10,11... | collective-permute-start | bytes 786440 | tf_op jit(solution)/shard_map/ppermute | solution.py:206
  64.9 9.5 %copy-start.1 = (bf16[4,128,256]{2,1,0:T(8,128)(2,1)}, bf16[4,128,256]{2,1,0:T(8,128)(2,1)S(1)}, u32[]{:S(2)}) copy-start(bf16[4,128,256]{2,1,0:T(8,128)(2,1)S(1)} %pad_maximum_fusion.models) | copy-start | bytes 786436
  64.9 11.8 %collective-permute-start.7 = (bf16[4,128,256]{2,1,0:T(8,128)(2,1)S(1)}, bf16[4,128,256]{2,1,0:T(8,128)(2,1)S(1)}, u32[]{:S(2)}, u32[]{:S(2)}) collective-permute-start(bf16[4,128,256]{2,1,0:T(8,128)(2,1)S(1)} %pad_maximum_fusion.models), channel_id=1, source_target_pairs={{0,1},{1,0},{2,3},{3,2},{4,5},{5,4},{6,7},{7,6},{8,9},{9,8},{10,11... | collective-permute-start | bytes 786440 | tf_op jit(solution)/shard_map/ppermute | solution.py:206
  (5 other events, 3.4 us)

commit v2 on v0

v2 whole, which is shorter than its diff:
```python
import functools

import jax
import jax.numpy as jnp
from jax import lax
from jax.experimental import pallas as pl
from jax.experimental.pallas import tpu as pltpu
from jax.sharding import PartitionSpec as P


CLUSTERS = 8
LANES = 128
AXES = ("dp", "group")
SHARES = (2, 2)
COVER = 1 << 26

VMEM = pl.BlockSpec(memory_space=pltpu.VMEM)
SMEM = pl.BlockSpec(memory_space=pltpu.SMEM)
ANY = pl.BlockSpec(memory_space=pl.ANY)


def shares_of(width):
    unit = width // (8 * sum(SHARES))
    starts = [8 * unit * sum(SHARES[:at]) for at in range(len(SHARES))]
    return [(start, unit * share) for start, share in zip(starts, SHARES)]


def near(value):
    return pltpu.with_memory_space_constraint(value, pltpu.VMEM)


def count_rows(devices):
    return CLUSTERS * pl.cdiv(devices, LANES)


def local_sums_kernel(devices, where, deltas, labels_row, *rest):
    chains = len(SHARES)
    targets, helds, sems = rest[:2 * chains], rest[2 * chains:3 * chains], rest[-1]
    clients, blocks, width = deltas.shape
    me = where[0]
    core = me & 1
    work = []
    for chain, (first, columns) in enumerate(shares_of(width)):
        for part in range(4):
            half = (1 - core) if part < 2 else core
            start = pl.multiple_of(first + (half * 2 + part % 2) * 2 * columns, LANES)
            copy = pltpu.make_async_copy(
                deltas.at[:, :, pl.ds(start, 2 * columns)], helds[chain].at[part], sems.at[chain, part])
            copy.start()
            work.append((copy, helds[chain].at[part], targets[2 * chain + part // 2], part % 2))

    rows, depth = CLUSTERS * blocks, clients * blocks
    labels = labels_row[...]
    spread = (lax.broadcasted_iota(jnp.int32, (clients, depth), 1) // blocks
              == lax.broadcasted_iota(jnp.int32, (clients, depth), 0)).astype(jnp.bfloat16)
    wide = jnp.dot(jnp.broadcast_to(labels, (16, clients)).astype(jnp.bfloat16), spread,
                   preferred_element_type=jnp.float32)[0:1].astype(jnp.int32)
    row = lax.broadcasted_iota(jnp.int32, (rows, depth), 0)
    column = lax.broadcasted_iota(jnp.int32, (rows, depth), 1)
    pick = ((wide == row // blocks) & (column % blocks == row % blocks)).astype(jnp.bfloat16)

    hits = (labels == lax.broadcasted_iota(jnp.int32, (CLUSTERS, clients), 0)).astype(jnp.float32)
    counts = jnp.sum(hits, axis=1, keepdims=True)
    lane = lax.broadcasted_iota(jnp.int32, (CLUSTERS, LANES), 1)
    tail = count_rows(devices)
    for tile in range(tail // CLUSTERS):
        table = jnp.where(lane + tile * LANES == me, counts, 0.0)
        for target in targets:
            at = target.shape[0] - tail + tile * CLUSTERS
            target[at:at + CLUSTERS, :] = table

    for copy, held, target, part in work:
        copy.wait()
        columns = held.shape[2]
        sums = jnp.dot(pick, held[...].reshape(depth, columns), preferred_element_type=jnp.float32)
        for block in range(columns // LANES):
            to = (part * columns // LANES + block) * rows
            target[to:to + rows, :] = sums[:, block * LANES:(block + 1) * LANES]


def local_sums(devices, where, deltas, labels_row):
    clients, blocks, width = deltas.shape
    outs, helds = [], []
    for _, columns in shares_of(width):
        height = 4 * columns // LANES * CLUSTERS * blocks + count_rows(devices)
        outs += [pltpu.VMEM((height, LANES), jnp.float32)] * 2
        helds.append(pltpu.VMEM((4, clients, blocks, 2 * columns), jnp.bfloat16))
    sums = pl.pallas_call(
        functools.partial(local_sums_kernel, devices),
        out_shape=outs,
        in_specs=[SMEM, pl.BlockSpec(memory_space=pltpu.HBM), VMEM],
        out_specs=[VMEM] * len(outs),
        scratch_shapes=helds + [pltpu.SemaphoreType.DMA((len(SHARES), 4))],
        compiler_params=pltpu.CompilerParams(vmem_limit_bytes=24 << 20),
        name="local_sums",
    )(where, pltpu.with_memory_space_constraint(deltas, pltpu.HBM), labels_row)
    return list(zip(sums[::2], sums[1::2]))


def bit_at(me, core, step):
    return (me >> (1 + (core ^ step))) & 1


def split_kernel(tail, step, where, kept, arrived, send, keep):
    half = (kept.shape[0] - tail) // 2
    bit = bit_at(where[0], where[0] & 1, step)
    for target, which in ((send, 1 - bit), (keep, bit)):
        rows = pl.ds(pl.multiple_of(which * half, CLUSTERS), half)
        target[0:half, :] = kept[rows, :] + arrived[rows, :]
        target[half:half + tail, :] = kept[2 * half:2 * half + tail, :] + arrived[2 * half:2 * half + tail, :]


def split(tail, step, where, kept, arrived):
    half = (kept.shape[0] - tail) // 2
    out = pltpu.VMEM((half + tail, LANES), jnp.float32)
    return pl.pallas_call(
        functools.partial(split_kernel, tail, step),
        out_shape=(out, out),
        in_specs=[SMEM, VMEM, VMEM],
        out_specs=(VMEM, VMEM),
        compiler_params=pltpu.CompilerParams(vmem_limit_bytes=8 << 20),
        name="split",
    )(where, near(kept), near(arrived))


def table_of(tail, kept, arrived):
    ends = [kept.shape[0] - tail + at for at in range(0, tail, CLUSTERS)]
    return [kept[at:at + CLUSTERS, :] + arrived[at:at + CLUSTERS, :] for at in ends]


def finish_kernel(tail, blocks, kept, arrived, models):
    rows = CLUSTERS * blocks
    height = kept.shape[0] - tail
    totals = jnp.zeros((CLUSTERS, 1), jnp.float32)
    for counts in table_of(tail, kept, arrived):
        totals = totals + jnp.sum(counts, axis=1, keepdims=True)
    for cluster in range(CLUSTERS):
        total = jnp.broadcast_to(totals[cluster:cluster + 1, :], (blocks, LANES))
        for block in range(height // rows):
            at = block * rows + cluster * blocks
            sums = kept[at:at + blocks, :] + arrived[at:at + blocks, :]
            models[cluster * blocks:(cluster + 1) * blocks, block * LANES:(block + 1) * LANES] = (
                sums / total).astype(jnp.bfloat16)


def finish(tail, blocks, kept, arrived):
    rows = CLUSTERS * blocks
    columns = (kept.shape[0] - tail) // rows * LANES
    return pl.pallas_call(
        functools.partial(finish_kernel, tail, blocks),
        out_shape=pltpu.VMEM((rows, columns), jnp.bfloat16),
        in_specs=[VMEM, VMEM],
        out_specs=VMEM,
        compiler_params=pltpu.CompilerParams(vmem_limit_bytes=8 << 20),
        name="finish",
    )(near(kept), near(arrived))


def ranks_of(me, table, labels):
    clients = labels.shape[1]
    lane = lax.broadcasted_iota(jnp.int32, (CLUSTERS, LANES), 1)
    before = jnp.zeros((CLUSTERS, 1), jnp.float32)
    for tile, counts in enumerate(table):
        before = before + jnp.sum(jnp.where(lane + tile * LANES < me, counts, 0.0), axis=1, keepdims=True)
    hits = labels == lax.broadcasted_iota(jnp.int32, (CLUSTERS, clients), 0)
    earlier = (lax.broadcasted_iota(jnp.int32, (clients, clients), 0)
               < lax.broadcasted_iota(jnp.int32, (clients, clients), 1))
    local = jnp.dot(hits.astype(jnp.float32).astype(jnp.bfloat16), earlier.astype(jnp.float32).astype(jnp.bfloat16),
                    preferred_element_type=jnp.float32)
    return jnp.sum(jnp.where(hits, before + local, 0.0), axis=0, keepdims=True).astype(jnp.int32)


def give_back_kernel(first, tail, where, labels, near_by, taken, far, *rest):
    me = where[0]
    if tail:
        kept, arrived, labels_row, returned, rank, laid, sem = rest
    else:
        _, returned, laid, sem = rest
    _, _, columns = near_by.shape
    clients, blocks, _ = returned.shape
    core = me & 1
    beside, opposite = 2 << core, 4 >> core
    for source, slot, half, flip in (
            (near_by, 0, core, 0), (near_by, 1, 1 - core, 0), (taken, 0, core, 6), (taken, 1, core, beside),
            (taken, 2, 1 - core, beside), (far, 0, 1 - core, 6), (far, 1, 1 - core, opposite),
            (far, 2, core, opposite)):
        owner = me ^ flip
        piece = half * 4 + bit_at(owner, half, 0) * 2 + bit_at(owner, half, 1)
        to = pl.ds(pl.multiple_of(piece * columns, LANES), columns)
        for cluster in range(CLUSTERS):
            laid[cluster, :, to] = source[slot, cluster * blocks:(cluster + 1) * blocks, :]
    across = pl.ds(first, 8 * columns)
    for client in range(clients):
        pltpu.make_async_copy(laid.at[labels[client]], returned.at[client, :, across], sem).start()
    if tail:
        rank[...] = ranks_of(me, table_of(tail, kept, arrived), labels_row[...])
    whole = returned.at[:, :, across]
    pltpu.make_async_copy(whole, whole, sem).wait()


def give_back(first, where, labels, values, shape, returned=None, ranked=None):
    columns = values[0].shape[2]
    blocks = shape[1]
    out = [jax.ShapeDtypeStruct(shape, jnp.bfloat16)]
    if ranked is None:
        tail, more, more_specs, aliases = 0, (returned,), [ANY], {2 + len(values): 0}
    else:
        tail, kept, arrived, labels_row = ranked
        more, more_specs, aliases = (near(kept), near(arrived), labels_row), [VMEM] * 3, {}
        out.append(jax.ShapeDtypeStruct(labels_row.shape, jnp.int32))
    return pl.pallas_call(
        functools.partial(give_back_kernel, first, tail),
        out_shape=out,
        in_specs=[SMEM, SMEM] + [VMEM] * len(values) + more_specs,
        out_specs=[ANY, VMEM][:len(out)],
        scratch_shapes=[pltpu.VMEM((CLUSTERS, blocks, 8 * columns), jnp.bfloat16), pltpu.SemaphoreType.DMA],
        input_output_aliases=aliases,
        compiler_params=pltpu.CompilerParams(vmem_limit_bytes=8 << 20),
        cost_estimate=pl.CostEstimate(flops=COVER, bytes_accessed=0, transcendentals=0),
        name="give_back",
    )(where, labels, *[near(value) for value in values], *more)


def on_device(devices, deltas, labels):
    clients, blocks, width = deltas.shape
    where = lax.axis_index(AXES).astype(jnp.int32).reshape(1)
    labels_row = labels.reshape(1, clients)
    labels_list = labels.reshape(clients)
    tail = count_rows(devices)
    bits = devices.bit_length() - 1

    def send(value, flip):
        return lax.ppermute(value, AXES, [(i, i ^ flip(i)) for i in range(devices)])

    def cores(i):
        return 1

    def crossed(low, high, step):
        def flip(i):
            return 1 << (high - 1 - step if i & 1 else low + step)

        return flip

    kept = []
    for other, mine in local_sums(devices, where, deltas, labels_row):
        kept.append(split(tail, 0, where, mine, send(other, cores)))
    for chain, (out, keep) in enumerate(kept):
        kept[chain] = split(tail, 1, where, keep, send(out, crossed(1, 3, 0)))
    for chain, (out, keep) in enumerate(kept):
        kept[chain] = (keep, send(out, crossed(1, 3, 1)))
    for step in range(bits - 3):
        for chain, (keep, arrived) in enumerate(kept):
            total = keep + arrived
            kept[chain] = (total, send(total, crossed(3, bits, step)))
    values = []
    for pair in kept:
        own = finish(tail, blocks, *pair)[None]
        near_by = jnp.concatenate([own, send(own, cores)], axis=0)
        diagonal = send(own, lambda i: 6)
        beside = send(near_by, lambda i: 2 << (i & 1))
        taken = jnp.concatenate([diagonal, beside], axis=0)
        values.append((near_by, taken, send(taken, cores)))

    give = functools.partial(give_back, where=where, labels=labels_list, shape=deltas.shape)
    starts = [first for first, _ in shares_of(width)]
    returned, rank = give(starts[0], values=values[0], ranked=(tail, *kept[0], labels_row))
    for chain in range(1, len(SHARES)):
        returned, = give(starts[chain], values=values[chain], returned=returned)
    return returned, rank.reshape(clients)


def solution(mesh):
    devices = mesh.shape["dp"] * mesh.shape["group"]
    placed = (P(AXES, None, None), P(AXES, None))

    def body(deltas, labels):
        return on_device(devices, deltas, labels)

    return jax.shard_map(
        body,
        mesh=mesh,
        in_specs=placed,
        out_specs=(P(AXES, None, None), P(AXES)),
        check_vma=False,
    )
```

time: 190 us -> 53.1 us (0.28)
  blocking collectives: 82.4 us -> 0 us
  waiting for transfers between devices: 53.2 us -> 14.7 us
  starting transfers between devices: 0.04 us -> 26.5 us
  local copies, waits for them, and re-layouts: 24.6 us -> 0.68 us
  between operations: 14.1 us -> 0.76 us
  matrix products: 13.1 us -> 0 us
  Pallas kernels: 0 us -> 9.88 us
    psum x1 -> x0, waiting for transfers between devices: 53.1 us -> none  [on_device(): summed = lax.psum(local_sums, ('dp', 'group'))]
    unnamed x1 -> x0, blocking collectives: 42.1 us -> none
    psum x1 -> x0, blocking collectives: 40.3 us -> none  [on_device(): totals = lax.psum(counts.astype(jnp.float32), ('dp', 'group'))]
    ppermute x0 -> x18, starting transfers between devices: none -> 26.5 us  [send(): return lax.ppermute(value, AXES, [(i, i ^ flip(i)) for i in range(devices)])]
    unnamed x6 -> x4, local copies, waits for them, and re-layouts: 24.5 us -> 0.66 us
    ppermute x0 -> x18, waiting for transfers between devices: none -> 14.7 us  [send(): return lax.ppermute(value, AXES, [(i, i ^ flip(i)) for i in range(devices)])]
    dot_general x2 -> x0, matrix products: 13.1 us -> none  [the longest x1 7.19 us: on_device(): jnp.dot(one_hot.astype(jnp.bfloat16), models, preferred_element_type=jnp....]
    pallas_call x0 -> x9, Pallas kernels: none -> 9.88 us  [the longest x2 5.65 us: give_back(): pl.pallas_call(functools.partial(give_back_kernel, first, tail), out_shap...]
  transfers between devices with their start and end apart: 1 -> 18, of which waited for: 1 -> 11; matrix products, arithmetic and copies ran while one was open for 1% -> 0% of each run, Pallas kernels for 0% -> 7%
where the time goes in v2:
time: 53.1 us; the launch traced here: 52.7 us
  starting transfers between devices  26.5 us (50%)
  waiting for transfers between devices  14.7 us (28%)
  Pallas kernels  9.88 us (19%)
  between operations  0.76 us (1%)
  local copies, waits for them, and re-layouts  0.68 us (1%)
    ppermute x18, starting transfers between devices, send(): return lax.ppermute(value, AXES, [(i, i ^ flip(i)) for i in range(devices)])  26.5 us
    ppermute x18, waiting for transfers between devices, send(): return lax.ppermute(value, AXES, [(i, i ^ flip(i)) for i in range(devices)])  14.7 us
    pallas_call x2, Pallas kernels, give_back(): pl.pallas_call(functools.partial(give_back_kernel, first, tail), out_shap...  5.65 us
    pallas_call x1, Pallas kernels, local_sums(): pl.pallas_call(functools.partial(local_sums_kernel, devices), out_shape=o...  3.85 us
  transfers between devices with their start and end apart: 18, of which 11 were waited for; matrix products, arithmetic and copies ran while one was open for 0% of the time, Pallas kernels for 7%

profile of v2, /device:TPU:0, one launch (start us, length us, event | category | flops | bytes accessed | tf_op | source)
XLA Modules:
  0.0 52.7 jit_solution(218364669930815928)
XLA Ops:
  0.6 0.6 %copy-done = s32[64,1]{0,1:T(1,128)S(1)} copy-done((s32[64,1]{0,1:T(1,128)S(1)}, s32[64,1]{0,1:T(1,128)}, u32[]{:S(2)}) %copy-start) | copy-done | bytes 280
  1.3 3.9 %local_sums.1 = (f32[1032,128]{1,0:T(8,128)S(1)}, f32[1032,128]{1,0:T(8,128)S(1)}, f32[1032,128]{1,0:T(8,128)S(1)}, f32[1032,128]{1,0:T(8,128)S(1)}) custom-call(s32[1]{0:T(128)} %bitcast.where, bf16[64,16,4096]{2,1,0:T(8,128)(2,1)} %deltas.1, s32[1,64]{1,0:T(1,128)S(1)} %bitcast.12), custom_call_target="tpu_custom_call" | custom-call | tf_op jit(solution)/shard_map/local_sums/pallas_call | solution.py:88
  5.8 1.5 %collective-permute-done.arrived = f32[1032,128]{1,0:T(8,128)S(1)} collective-permute-done((f32[1032,128]{1,0:T(8,128)S(1)}, f32[1032,128]{1,0:T(8,128)S(1)}, u32[]{:S(2)}, u32[]{:S(2)}) %collective-permute-start) | collective-permute-done | bytes 528416 | tf_op jit(solution)/shard_map/ppermute | solution.py:233
  7.3 2.9 %collective-permute-start.1 = (f32[520,128]{1,0:T(8,128)S(1)}, f32[520,128]{1,0:T(8,128)S(1)}, u32[]{:S(2)}, u32[]{:S(2)}) collective-permute-start(f32[520,128]{1,0:T(8,128)S(1)} %get-tuple-element.19), channel_id=1, source_target_pairs={{0,2},{1,5},{2,0},{3,7},{4,6},{5,1},{6,4},{7,3},{8,10},{9,13},{10,... | collective-permute-start | bytes 798728 | tf_op jit(solution)/shard_map/ppermute | solution.py:233
  10.3 0.7 %collective-permute-start.10 = (f32[520,128]{1,0:T(8,128)S(1)}, f32[520,128]{1,0:T(8,128)S(1)}, u32[]{:S(2)}, u32[]{:S(2)}) collective-permute-start(f32[520,128]{1,0:T(8,128)S(1)} %get-tuple-element.25), channel_id=1, source_target_pairs={{0,2},{1,5},{2,0},{3,7},{4,6},{5,1},{6,4},{7,3},{8,10},{9,13},{10,... | collective-permute-start | bytes 798728 | tf_op jit(solution)/shard_map/ppermute | solution.py:233
  11.0 3.6 %collective-permute-done.1.arrived = f32[520,128]{1,0:T(8,128)S(1)} collective-permute-done((f32[520,128]{1,0:T(8,128)S(1)}, f32[520,128]{1,0:T(8,128)S(1)}, u32[]{:S(2)}, u32[]{:S(2)}) %collective-permute-start.1) | collective-permute-done | bytes 266272 | tf_op jit(solution)/shard_map/ppermute | solution.py:233
  14.7 2.1 %collective-permute-start.2 = (f32[264,128]{1,0:T(8,128)S(1)}, f32[264,128]{1,0:T(8,128)S(1)}, u32[]{:S(2)}, u32[]{:S(2)}) collective-permute-start(f32[264,128]{1,0:T(8,128)S(1)} %get-tuple-element.21), channel_id=1, source_target_pairs={{0,4},{1,3},{2,6},{3,1},{4,0},{5,7},{6,2},{7,5},{8,12},{9,11},{10,... | collective-permute-start | bytes 405512 | tf_op jit(solution)/shard_map/ppermute | solution.py:233
  16.8 1.3 %collective-permute-done.10.arrived = f32[520,128]{1,0:T(8,128)S(1)} collective-permute-done((f32[520,128]{1,0:T(8,128)S(1)}, f32[520,128]{1,0:T(8,128)S(1)}, u32[]{:S(2)}, u32[]{:S(2)}) %collective-permute-start.10) | collective-permute-done | bytes 266272 | tf_op jit(solution)/shard_map/ppermute | solution.py:233
  18.1 2.4 %collective-permute-start.11 = (f32[264,128]{1,0:T(8,128)S(1)}, f32[264,128]{1,0:T(8,128)S(1)}, u32[]{:S(2)}, u32[]{:S(2)}) collective-permute-start(f32[264,128]{1,0:T(8,128)S(1)} %get-tuple-element.27), channel_id=1, source_target_pairs={{0,4},{1,3},{2,6},{3,1},{4,0},{5,7},{6,2},{7,5},{8,12},{9,11},{10,... | collective-permute-start | bytes 405512 | tf_op jit(solution)/shard_map/ppermute | solution.py:233
  20.5 1.6 %collective-permute-start.3 = (f32[264,128]{1,0:T(8,128)S(1)}, f32[264,128]{1,0:T(8,128)S(1)}, u32[]{:S(2)}, u32[]{:S(2)}) collective-permute-start(f32[264,128]{1,0:T(8,128)S(1)} %add.16), channel_id=1, source_target_pairs={{0,8},{1,17},{2,10},{3,19},{4,12},{5,21},{6,14},{7,23},{8,0},{9,25... | collective-permute-start | bytes 405512 | tf_op jit(solution)/shard_map/ppermute | solution.py:233
  22.2 1.3 %collective-permute-done.11 = f32[264,128]{1,0:T(8,128)S(1)} collective-permute-done((f32[264,128]{1,0:T(8,128)S(1)}, f32[264,128]{1,0:T(8,128)S(1)}, u32[]{:S(2)}, u32[]{:S(2)}) %collective-permute-start.11) | collective-permute-done | bytes 135200 | tf_op jit(solution)/shard_map/ppermute | solution.py:233
  23.5 2.1 %collective-permute-start.12 = (f32[264,128]{1,0:T(8,128)S(1)}, f32[264,128]{1,0:T(8,128)S(1)}, u32[]{:S(2)}, u32[]{:S(2)}) collective-permute-start(f32[264,128]{1,0:T(8,128)S(1)} %add.18), channel_id=1, source_target_pairs={{0,8},{1,17},{2,10},{3,19},{4,12},{5,21},{6,14},{7,23},{8,0},{9,25... | collective-permute-start | bytes 405512 | tf_op jit(solution)/shard_map/ppermute | solution.py:233
  26.2 3.2 %collective-permute-start.4 = (f32[264,128]{1,0:T(8,128)S(1)}, f32[264,128]{1,0:T(8,128)S(1)}, u32[]{:S(2)}, u32[]{:S(2)}) collective-permute-start(f32[264,128]{1,0:T(8,128)S(1)} %add.17.kept), channel_id=1, source_target_pairs={{0,16},{1,9},{2,18},{3,11},{4,20},{5,13},{6,22},{7,15},{8,24},{9,1... | collective-permute-start | bytes 405512 | tf_op jit(solution)/shard_map/ppermute | solution.py:233
  29.3 0.6 %collective-permute-done.12 = f32[264,128]{1,0:T(8,128)S(1)} collective-permute-done((f32[264,128]{1,0:T(8,128)S(1)}, f32[264,128]{1,0:T(8,128)S(1)}, u32[]{:S(2)}, u32[]{:S(2)}) %collective-permute-start.12) | collective-permute-done | bytes 135200 | tf_op jit(solution)/shard_map/ppermute | solution.py:233
  29.9 3.1 %collective-permute-start.13 = (f32[264,128]{1,0:T(8,128)S(1)}, f32[264,128]{1,0:T(8,128)S(1)}, u32[]{:S(2)}, u32[]{:S(2)}) collective-permute-start(f32[264,128]{1,0:T(8,128)S(1)} %add.19.kept.rest_0_), channel_id=1, source_target_pairs={{0,16},{1,9},{2,18},{3,11},{4,20},{5,13},{6,22},{7,15},{8,24},{9,1... | collective-permute-start | bytes 405512 | tf_op jit(solution)/shard_map/ppermute | solution.py:233
  33.2 2.7 %collective-permute-start.6 = (bf16[1,128,256]{2,1,0:T(8,128)(2,1)S(1)}, bf16[1,128,256]{2,1,0:T(8,128)(2,1)S(1)}, u32[]{:S(2)}, u32[]{:S(2)}) collective-permute-start(bf16[1,128,256]{2,1,0:T(8,128)(2,1)S(1)} %bitcast.7), channel_id=1, source_target_pairs={{0,6},{1,7},{2,4},{3,5},{4,2},{5,3},{6,0},{7,1},{8,14},{9,15},{10,... | collective-permute-start | bytes 196616 | tf_op jit(solution)/shard_map/ppermute | solution.py:233
  36.2 2.8 %collective-permute-start.15 = (bf16[1,128,256]{2,1,0:T(8,128)(2,1)S(1)}, bf16[1,128,256]{2,1,0:T(8,128)(2,1)S(1)}, u32[]{:S(2)}, u32[]{:S(2)}) collective-permute-start(bf16[1,128,256]{2,1,0:T(8,128)(2,1)S(1)} %bitcast.9), channel_id=1, source_target_pairs={{0,6},{1,7},{2,4},{3,5},{4,2},{5,3},{6,0},{7,1},{8,14},{9,15},{10,... | collective-permute-start | bytes 196616 | tf_op jit(solution)/shard_map/ppermute | solution.py:233
  39.0 0.6 %collective-permute-start.7 = (bf16[2,128,256]{2,1,0:T(8,128)(2,1)S(1)}, bf16[2,128,256]{2,1,0:T(8,128)(2,1)S(1)}, u32[]{:S(2)}, u32[]{:S(2)}) collective-permute-start(bf16[2,128,256]{2,1,0:T(8,128)(2,1)S(1)} %pad_maximum_fusion.near_by), channel_id=1, source_target_pairs={{0,2},{1,5},{2,0},{3,7},{4,6},{5,1},{6,4},{7,3},{8,10},{9,13},{10,... | collective-permute-start | bytes 393224 | tf_op jit(solution)/shard_map/ppermute | solution.py:233
  39.6 0.6 %collective-permute-done.14 = bf16[1,128,256]{2,1,0:T(8,128)(2,1)S(1)} collective-permute-done((bf16[1,128,256]{2,1,0:T(8,128)(2,1)S(1)}, bf16[1,128,256]{2,1,0:T(8,128)(2,1)S(1)}, u32[]{:S(2)}, u32[]{:S(2)}) %collective-permute-start.14) | collective-permute-done | bytes 65568 | tf_op jit(solution)/shard_map/ppermute | solution.py:233
  40.3 0.9 %collective-permute-start.16 = (bf16[2,128,256]{2,1,0:T(8,128)(2,1)S(1)}, bf16[2,128,256]{2,1,0:T(8,128)(2,1)S(1)}, u32[]{:S(2)}, u32[]{:S(2)}) collective-permute-start(bf16[2,128,256]{2,1,0:T(8,128)(2,1)S(1)} %pad_maximum_fusion.1.near_by), channel_id=1, source_target_pairs={{0,2},{1,5},{2,0},{3,7},{4,6},{5,1},{6,4},{7,3},{8,10},{9,13},{10,... | collective-permute-start | bytes 393224 | tf_op jit(solution)/shard_map/ppermute | solution.py:233
  41.5 4.0 %collective-permute-done.16 = bf16[2,128,256]{2,1,0:T(8,128)(2,1)S(1)} collective-permute-done((bf16[2,128,256]{2,1,0:T(8,128)(2,1)S(1)}, bf16[2,128,256]{2,1,0:T(8,128)(2,1)S(1)}, u32[]{:S(2)}, u32[]{:S(2)}) %collective-permute-start.16) | collective-permute-done | bytes 131104 | tf_op jit(solution)/shard_map/ppermute | solution.py:233
  46.2 0.8 %collective-permute-done.17.far = bf16[3,128,256]{2,1,0:T(8,128)(2,1)S(1)} collective-permute-done((bf16[3,128,256]{2,1,0:T(8,128)(2,1)S(1)}, bf16[3,128,256]{2,1,0:T(8,128)(2,1)S(1)}, u32[]{:S(2)}, u32[]{:S(2)}) %collective-permute-start.17) | collective-permute-done | bytes 196640 | tf_op jit(solution)/shard_map/ppermute | solution.py:233
  47.0 3.1 %give_back.2 = (bf16[64,16,4096]{2,1,0:T(8,128)(2,1)}, s32[1,64]{1,0:T(1,128)}) custom-call(s32[1]{0:T(128)} %bitcast.where, s32[64]{0:T(128)S(1)} %bitcast.13, bf16[2,128,256]{2,1,0:T(8,128)(2,1)S(1)} %pad_maximum_fusion.1.near_by, bf16[3,128,256]{2,1,0:T(8,128)(2,1)S(1)} %constant_dynamic-update-slice_fusion.2.taken, ...), custom_call_target="tpu_custom_call" | custom-call | flops 67108864 | tf_op jit(solution)/shard_map/give_back/pallas_call | solution.py:211
  50.1 2.6 %give_back.3 = bf16[64,16,4096]{2,1,0:T(8,128)(2,1)} custom-call(s32[1]{0:T(128)} %bitcast.where, s32[64]{0:T(128)S(1)} %bitcast.15, bf16[2,128,256]{2,1,0:T(8,128)(2,1)S(1)} %pad_maximum_fusion.near_by, bf16[3,128,256]{2,1,0:T(8,128)(2,1)S(1)} %constant_dynamic-update-slice_fusion.taken, ...), custom_call_target="tpu_custom_call", output_to_operand_aliasing={{}: (5, {})} | custom-call | flops 67108864 | tf_op jit(solution)/shard_map/give_back/pallas_call | solution.py:211
  (33 shorter events, 2.8 us)
Async XLA Ops:
  0.6 0.7 %copy-start = (s32[64,1]{0,1:T(1,128)S(1)}, s32[64,1]{0,1:T(1,128)}, u32[]{:S(2)}) copy-start(s32[64,1]{0,1:T(1,128)} %param.3) | copy-start | bytes 772
  5.2 2.1 %collective-permute-start = (f32[1032,128]{1,0:T(8,128)S(1)}, f32[1032,128]{1,0:T(8,128)S(1)}, u32[]{:S(2)}, u32[]{:S(2)}) collective-permute-start(f32[1032,128]{1,0:T(8,128)S(1)} %get-tuple-element.17), channel_id=1, source_target_pairs={{0,1},{1,0},{2,3},{3,2},{4,5},{5,4},{6,7},{7,6},{8,9},{9,8},{10,11... | collective-permute-start | bytes 1585160 | tf_op jit(solution)/shard_map/ppermute | solution.py:233
  5.7 4.5 %collective-permute-start.9 = (f32[1032,128]{1,0:T(8,128)S(1)}, f32[1032,128]{1,0:T(8,128)S(1)}, u32[]{:S(2)}, u32[]{:S(2)}) collective-permute-start(f32[1032,128]{1,0:T(8,128)S(1)} %get-tuple-element.23), channel_id=1, source_target_pairs={{0,1},{1,0},{2,3},{3,2},{4,5},{5,4},{6,7},{7,6},{8,9},{9,8},{10,11... | collective-permute-start | bytes 1585160 | tf_op jit(solution)/shard_map/ppermute | solution.py:233
  7.3 7.3 %collective-permute-start.1 = (f32[520,128]{1,0:T(8,128)S(1)}, f32[520,128]{1,0:T(8,128)S(1)}, u32[]{:S(2)}, u32[]{:S(2)}) collective-permute-start(f32[520,128]{1,0:T(8,128)S(1)} %get-tuple-element.19), channel_id=1, source_target_pairs={{0,2},{1,5},{2,0},{3,7},{4,6},{5,1},{6,4},{7,3},{8,10},{9,13},{10,... | collective-permute-start | bytes 798728 | tf_op jit(solution)/shard_map/ppermute | solution.py:233
  10.3 7.7 %collective-permute-start.10 = (f32[520,128]{1,0:T(8,128)S(1)}, f32[520,128]{1,0:T(8,128)S(1)}, u32[]{:S(2)}, u32[]{:S(2)}) collective-permute-start(f32[520,128]{1,0:T(8,128)S(1)} %get-tuple-element.25), channel_id=1, source_target_pairs={{0,2},{1,5},{2,0},{3,7},{4,6},{5,1},{6,4},{7,3},{8,10},{9,13},{10,... | collective-permute-start | bytes 798728 | tf_op jit(solution)/shard_map/ppermute | solution.py:233
  14.7 5.8 %collective-permute-start.2 = (f32[264,128]{1,0:T(8,128)S(1)}, f32[264,128]{1,0:T(8,128)S(1)}, u32[]{:S(2)}, u32[]{:S(2)}) collective-permute-start(f32[264,128]{1,0:T(8,128)S(1)} %get-tuple-element.21), channel_id=1, source_target_pairs={{0,4},{1,3},{2,6},{3,1},{4,0},{5,7},{6,2},{7,5},{8,12},{9,11},{10,... | collective-permute-start | bytes 405512 | tf_op jit(solution)/shard_map/ppermute | solution.py:233
  18.1 5.4 %collective-permute-start.11 = (f32[264,128]{1,0:T(8,128)S(1)}, f32[264,128]{1,0:T(8,128)S(1)}, u32[]{:S(2)}, u32[]{:S(2)}) collective-permute-start(f32[264,128]{1,0:T(8,128)S(1)} %get-tuple-element.27), channel_id=1, source_target_pairs={{0,4},{1,3},{2,6},{3,1},{4,0},{5,7},{6,2},{7,5},{8,12},{9,11},{10,... | collective-permute-start | bytes 405512 | tf_op jit(solution)/shard_map/ppermute | solution.py:233
  20.5 5.6 %collective-permute-start.3 = (f32[264,128]{1,0:T(8,128)S(1)}, f32[264,128]{1,0:T(8,128)S(1)}, u32[]{:S(2)}, u32[]{:S(2)}) collective-permute-start(f32[264,128]{1,0:T(8,128)S(1)} %add.16), channel_id=1, source_target_pairs={{0,8},{1,17},{2,10},{3,19},{4,12},{5,21},{6,14},{7,23},{8,0},{9,25... | collective-permute-start | bytes 405512 | tf_op jit(solution)/shard_map/ppermute | solution.py:233
  23.5 6.4 %collective-permute-start.12 = (f32[264,128]{1,0:T(8,128)S(1)}, f32[264,128]{1,0:T(8,128)S(1)}, u32[]{:S(2)}, u32[]{:S(2)}) collective-permute-start(f32[264,128]{1,0:T(8,128)S(1)} %add.18), channel_id=1, source_target_pairs={{0,8},{1,17},{2,10},{3,19},{4,12},{5,21},{6,14},{7,23},{8,0},{9,25... | collective-permute-start | bytes 405512 | tf_op jit(solution)/shard_map/ppermute | solution.py:233
  26.2 6.8 %collective-permute-start.4 = (f32[264,128]{1,0:T(8,128)S(1)}, f32[264,128]{1,0:T(8,128)S(1)}, u32[]{:S(2)}, u32[]{:S(2)}) collective-permute-start(f32[264,128]{1,0:T(8,128)S(1)} %add.17.kept), channel_id=1, source_target_pairs={{0,16},{1,9},{2,18},{3,11},{4,20},{5,13},{6,22},{7,15},{8,24},{9,1... | collective-permute-start | bytes 405512 | tf_op jit(solution)/shard_map/ppermute | solution.py:233
  29.9 6.2 %collective-permute-start.13 = (f32[264,128]{1,0:T(8,128)S(1)}, f32[264,128]{1,0:T(8,128)S(1)}, u32[]{:S(2)}, u32[]{:S(2)}) collective-permute-start(f32[264,128]{1,0:T(8,128)S(1)} %add.19.kept.rest_0_), channel_id=1, source_target_pairs={{0,16},{1,9},{2,18},{3,11},{4,20},{5,13},{6,22},{7,15},{8,24},{9,1... | collective-permute-start | bytes 405512 | tf_op jit(solution)/shard_map/ppermute | solution.py:233
  33.1 5.9 %collective-permute-start.5 = (bf16[1,128,256]{2,1,0:T(8,128)(2,1)S(1)}, bf16[1,128,256]{2,1,0:T(8,128)(2,1)S(1)}, u32[]{:S(2)}, u32[]{:S(2)}) collective-permute-start(bf16[1,128,256]{2,1,0:T(8,128)(2,1)S(1)} %bitcast.6), channel_id=1, source_target_pairs={{0,1},{1,0},{2,3},{3,2},{4,5},{5,4},{6,7},{7,6},{8,9},{9,8},{10,11... | collective-permute-start | bytes 196616 | tf_op jit(solution)/shard_map/ppermute | solution.py:233
  33.2 8.0 %collective-permute-start.6 = (bf16[1,128,256]{2,1,0:T(8,128)(2,1)S(1)}, bf16[1,128,256]{2,1,0:T(8,128)(2,1)S(1)}, u32[]{:S(2)}, u32[]{:S(2)}) collective-permute-start(bf16[1,128,256]{2,1,0:T(8,128)(2,1)S(1)} %bitcast.7), channel_id=1, source_target_pairs={{0,6},{1,7},{2,4},{3,5},{4,2},{5,3},{6,0},{7,1},{8,14},{9,15},{10,... | collective-permute-start | bytes 196616 | tf_op jit(solution)/shard_map/ppermute | solution.py:233
  36.2 5.2 %collective-permute-start.15 = (bf16[1,128,256]{2,1,0:T(8,128)(2,1)S(1)}, bf16[1,128,256]{2,1,0:T(8,128)(2,1)S(1)}, u32[]{:S(2)}, u32[]{:S(2)}) collective-permute-start(bf16[1,128,256]{2,1,0:T(8,128)(2,1)S(1)} %bitcast.9), channel_id=1, source_target_pairs={{0,6},{1,7},{2,4},{3,5},{4,2},{5,3},{6,0},{7,1},{8,14},{9,15},{10,... | collective-permute-start | bytes 196616 | tf_op jit(solution)/shard_map/ppermute | solution.py:233
  39.0 1.3 %collective-permute-start.14 = (bf16[1,128,256]{2,1,0:T(8,128)(2,1)S(1)}, bf16[1,128,256]{2,1,0:T(8,128)(2,1)S(1)}, u32[]{:S(2)}, u32[]{:S(2)}) collective-permute-start(bf16[1,128,256]{2,1,0:T(8,128)(2,1)S(1)} %bitcast.10), channel_id=1, source_target_pairs={{0,1},{1,0},{2,3},{3,2},{4,5},{5,4},{6,7},{7,6},{8,9},{9,8},{10,11... | collective-permute-start | bytes 196616 | tf_op jit(solution)/shard_map/ppermute | solution.py:233
  39.0 6.5 %collective-permute-start.7 = (bf16[2,128,256]{2,1,0:T(8,128)(2,1)S(1)}, bf16[2,128,256]{2,1,0:T(8,128)(2,1)S(1)}, u32[]{:S(2)}, u32[]{:S(2)}) collective-permute-start(bf16[2,128,256]{2,1,0:T(8,128)(2,1)S(1)} %pad_maximum_fusion.near_by), channel_id=1, source_target_pairs={{0,2},{1,5},{2,0},{3,7},{4,6},{5,1},{6,4},{7,3},{8,10},{9,13},{10,... | collective-permute-start | bytes 393224 | tf_op jit(solution)/shard_map/ppermute | solution.py:233
  40.3 5.2 %collective-permute-start.16 = (bf16[2,128,256]{2,1,0:T(8,128)(2,1)S(1)}, bf16[2,128,256]{2,1,0:T(8,128)(2,1)S(1)}, u32[]{:S(2)}, u32[]{:S(2)}) collective-permute-start(bf16[2,128,256]{2,1,0:T(8,128)(2,1)S(1)} %pad_maximum_fusion.1.near_by), channel_id=1, source_target_pairs={{0,2},{1,5},{2,0},{3,7},{4,6},{5,1},{6,4},{7,3},{8,10},{9,13},{10,... | collective-permute-start | bytes 393224 | tf_op jit(solution)/shard_map/ppermute | solution.py:233
  45.5 1.5 %collective-permute-start.17 = (bf16[3,128,256]{2,1,0:T(8,128)(2,1)S(1)}, bf16[3,128,256]{2,1,0:T(8,128)(2,1)S(1)}, u32[]{:S(2)}, u32[]{:S(2)}) collective-permute-start(bf16[3,128,256]{2,1,0:T(8,128)(2,1)S(1)} %constant_dynamic-update-slice_fusion.2.taken), channel_id=1, source_target_pairs={{0,1},{1,0},{2,3},{3,2},{4,5},{5,4},{6,7},{7,6},{8,9},{9,8},{10,11... | collective-permute-start | bytes 589832 | tf_op jit(solution)/shard_map/ppermute | solution.py:233
  45.6 4.5 %collective-permute-start.8 = (bf16[3,128,256]{2,1,0:T(8,128)(2,1)S(1)}, bf16[3,128,256]{2,1,0:T(8,128)(2,1)S(1)}, u32[]{:S(2)}, u32[]{:S(2)}) collective-permute-start(bf16[3,128,256]{2,1,0:T(8,128)(2,1)S(1)} %constant_dynamic-update-slice_fusion.taken), channel_id=1, source_target_pairs={{0,1},{1,0},{2,3},{3,2},{4,5},{5,4},{6,7},{7,6},{8,9},{9,8},{10,11... | collective-permute-start | bytes 589832 | tf_op jit(solution)/shard_map/ppermute | solution.py:233

commit v3 on v2

--- a/solution.py
+++ b/solution.py
@@ -17,6 +17,7 @@
 VMEM = pl.BlockSpec(memory_space=pltpu.VMEM)
 SMEM = pl.BlockSpec(memory_space=pltpu.SMEM)
 ANY = pl.BlockSpec(memory_space=pl.ANY)
+HBM = pl.BlockSpec(memory_space=pltpu.HBM)
 
 
 def shares_of(width):
@@ -25,39 +26,49 @@
     return [(start, unit * share) for start, share in zip(starts, SHARES)]
 
 
+def role_of(index):
+    for shift in (16, 8, 4, 2, 1):
+        index = index ^ (index >> shift)
+    return index & 1
+
+
 def near(value):
     return pltpu.with_memory_space_constraint(value, pltpu.VMEM)
 
 
+def far_off(value):
+    return pltpu.with_memory_space_constraint(value, pltpu.HBM)
+
+
 def count_rows(devices):
     return CLUSTERS * pl.cdiv(devices, LANES)
 
 
-def local_sums_kernel(devices, where, deltas, labels_row, *rest):
-    chains = len(SHARES)
-    targets, helds, sems = rest[:2 * chains], rest[2 * chains:3 * chains], rest[-1]
-    clients, blocks, width = deltas.shape
+def local_sums_kernel(devices, first, where, deltas, labels_row, other, mine, held, labels_here, sems):
+    clients, blocks, _ = deltas.shape
     me = where[0]
-    core = me & 1
-    work = []
-    for chain, (first, columns) in enumerate(shares_of(width)):
-        for part in range(4):
-            half = (1 - core) if part < 2 else core
-            start = pl.multiple_of(first + (half * 2 + part % 2) * 2 * columns, LANES)
-            copy = pltpu.make_async_copy(
-                deltas.at[:, :, pl.ds(start, 2 * columns)], helds[chain].at[part], sems.at[chain, part])
-            copy.start()
-            work.append((copy, helds[chain].at[part], targets[2 * chain + part // 2], part % 2))
+    role = role_of(me)
+    columns = held.shape[3]
+    arrive = pltpu.make_async_copy(labels_row, labels_here, sems.at[4])
+    arrive.start()
+    copies = []
+    for part in range(4):
+        half = (1 - role) if part < 2 else role
+        start = pl.multiple_of(first + (half * 2 + part % 2) * columns, LANES)
+        copies.append(pltpu.make_async_copy(deltas.at[:, :, pl.ds(start, columns)], held.at[part], sems.at[part]))
+        copies[-1].start()
 
     rows, depth = CLUSTERS * blocks, clients * blocks
-    labels = labels_row[...]
     spread = (lax.broadcasted_iota(jnp.int32, (clients, depth), 1) // blocks
               == lax.broadcasted_iota(jnp.int32, (clients, depth), 0)).astype(jnp.bfloat16)
+    row = lax.broadcasted_iota(jnp.int32, (rows, depth), 0)
+    column = lax.broadcasted_iota(jnp.int32, (rows, depth), 1)
+    same_row = column % blocks == row % blocks
+    arrive.wait()
+    labels = labels_here[...]
     wide = jnp.dot(jnp.broadcast_to(labels, (16, clients)).astype(jnp.bfloat16), spread,
                    preferred_element_type=jnp.float32)[0:1].astype(jnp.int32)
-    row = lax.broadcasted_iota(jnp.int32, (rows, depth), 0)
-    column = lax.broadcasted_iota(jnp.int32, (rows, depth), 1)
-    pick = ((wide == row // blocks) & (column % blocks == row % blocks)).astype(jnp.bfloat16)
+    pick = ((wide == row // blocks) & same_row).astype(jnp.bfloat16)
 
     hits = (labels == lax.broadcasted_iota(jnp.int32, (CLUSTERS, clients), 0)).astype(jnp.float32)
     counts = jnp.sum(hits, axis=1, keepdims=True)
@@ -65,45 +76,43 @@
     tail = count_rows(devices)
     for tile in range(tail // CLUSTERS):
         table = jnp.where(lane + tile * LANES == me, counts, 0.0)
-        for target in targets:
-            at = target.shape[0] - tail + tile * CLUSTERS
-            target[at:at + CLUSTERS, :] = table
-
-    for copy, held, target, part in work:
-        copy.wait()
-        columns = held.shape[2]
-        sums = jnp.dot(pick, held[...].reshape(depth, columns), preferred_element_type=jnp.float32)
+        at = other.shape[0] - tail + tile * CLUSTERS
+        other[at:at + CLUSTERS, :] = table
+        mine[at:at + CLUSTERS, :] = table
+
+    for part in range(4):
+        copies[part].wait()
+        sums = jnp.dot(pick, held[part].reshape(depth, columns), preferred_element_type=jnp.float32)
+        target = other if part < 2 else mine
         for block in range(columns // LANES):
-            to = (part * columns // LANES + block) * rows
+            to = (part % 2 * columns // LANES + block) * rows
             target[to:to + rows, :] = sums[:, block * LANES:(block + 1) * LANES]
 
 
-def local_sums(devices, where, deltas, labels_row):
-    clients, blocks, width = deltas.shape
-    outs, helds = [], []
-    for _, columns in shares_of(width):
-        height = 4 * columns // LANES * CLUSTERS * blocks + count_rows(devices)
-        outs += [pltpu.VMEM((height, LANES), jnp.float32)] * 2
-        helds.append(pltpu.VMEM((4, clients, blocks, 2 * columns), jnp.bfloat16))
-    sums = pl.pallas_call(
-        functools.partial(local_sums_kernel, devices),
-        out_shape=outs,
-        in_specs=[SMEM, pl.BlockSpec(memory_space=pltpu.HBM), VMEM],
-        out_specs=[VMEM] * len(outs),
-        scratch_shapes=helds + [pltpu.SemaphoreType.DMA((len(SHARES), 4))],
-        compiler_params=pltpu.CompilerParams(vmem_limit_bytes=24 << 20),
+def local_sums(devices, first, columns, where, deltas, labels_row):
+    clients, blocks, _ = deltas.shape
+    height = 4 * columns // LANES * CLUSTERS * blocks + count_rows(devices)
+    out = pltpu.VMEM((height, LANES), jnp.float32)
+    return pl.pallas_call(
+        functools.partial(local_sums_kernel, devices, first),
+        out_shape=(out, out),
+        in_specs=[SMEM, HBM, HBM],
+        out_specs=(VMEM, VMEM),
+        scratch_shapes=[
+            pltpu.VMEM((4, clients, blocks, 2 * columns), jnp.bfloat16), pltpu.VMEM((1, clients), jnp.int32),
+            pltpu.SemaphoreType.DMA((5,))],
+        compiler_params=pltpu.CompilerParams(vmem_limit_bytes=16 << 20),
         name="local_sums",
-    )(where, pltpu.with_memory_space_constraint(deltas, pltpu.HBM), labels_row)
-    return list(zip(sums[::2], sums[1::2]))
-
-
-def bit_at(me, core, step):
-    return (me >> (1 + (core ^ step))) & 1
+    )(where, far_off(deltas), far_off(labels_row))
+
+
+def bit_at(me, role, step):
+    return (me >> (1 + (role ^ step))) & 1
 
 
 def split_kernel(tail, step, where, kept, arrived, send, keep):
     half = (kept.shape[0] - tail) // 2
-    bit = bit_at(where[0], where[0] & 1, step)
+    bit = bit_at(where[0], role_of(where[0]), step)
     for target, which in ((send, 1 - bit), (keep, bit)):
         rows = pl.ds(pl.multiple_of(which * half, CLUSTERS), half)
         target[0:half, :] = kept[rows, :] + arrived[rows, :]
@@ -173,17 +182,17 @@
 def give_back_kernel(first, tail, where, labels, near_by, taken, far, *rest):
     me = where[0]
     if tail:
-        kept, arrived, labels_row, returned, rank, laid, sem = rest
+        kept, arrived, labels_row, returned, rank, laid, sem, rank_here, rank_sem = rest
     else:
         _, returned, laid, sem = rest
     _, _, columns = near_by.shape
     clients, blocks, _ = returned.shape
-    core = me & 1
-    beside, opposite = 2 << core, 4 >> core
+    role = role_of(me)
+    beside, opposite = 2 << role, 4 >> role
     for source, slot, half, flip in (
-            (near_by, 0, core, 0), (near_by, 1, 1 - core, 0), (taken, 0, core, 6), (taken, 1, core, beside),
-            (taken, 2, 1 - core, beside), (far, 0, 1 - core, 6), (far, 1, 1 - core, opposite),
-            (far, 2, core, opposite)):
+            (near_by, 0, role, 0), (near_by, 1, 1 - role, 0), (taken, 0, role, 6), (taken, 1, role, beside),
+            (taken, 2, 1 - role, beside), (far, 0, 1 - role, 6), (far, 1, 1 - role, opposite),
+            (far, 2, role, opposite)):
         owner = me ^ flip
         piece = half * 4 + bit_at(owner, half, 0) * 2 + bit_at(owner, half, 1)
         to = pl.ds(pl.multiple_of(piece * columns, LANES), columns)
@@ -193,7 +202,10 @@
     for client in range(clients):
         pltpu.make_async_copy(laid.at[labels[client]], returned.at[client, :, across], sem).start()
     if tail:
-        rank[...] = ranks_of(me, table_of(tail, kept, arrived), labels_row[...])
+        rank_here[...] = ranks_of(me, table_of(tail, kept, arrived), labels_row[...])
+        ranks = pltpu.make_async_copy(rank_here, rank, rank_sem)
+        ranks.start()
+        ranks.wait()
     whole = returned.at[:, :, across]
     pltpu.make_async_copy(whole, whole, sem).wait()
 
@@ -201,19 +213,21 @@
 def give_back(first, where, labels, values, shape, returned=None, ranked=None):
     columns = values[0].shape[2]
     blocks = shape[1]
+    scratch = [pltpu.VMEM((CLUSTERS, blocks, 8 * columns), jnp.bfloat16), pltpu.SemaphoreType.DMA]
     out = [jax.ShapeDtypeStruct(shape, jnp.bfloat16)]
     if ranked is None:
         tail, more, more_specs, aliases = 0, (returned,), [ANY], {2 + len(values): 0}
     else:
         tail, kept, arrived, labels_row = ranked
-        more, more_specs, aliases = (near(kept), near(arrived), labels_row), [VMEM] * 3, {}
+        more, more_specs, aliases = (near(kept), near(arrived), near(labels_row)), [VMEM] * 3, {}
         out.append(jax.ShapeDtypeStruct(labels_row.shape, jnp.int32))
+        scratch += [pltpu.VMEM(labels_row.shape, jnp.int32), pltpu.SemaphoreType.DMA]
     return pl.pallas_call(
         functools.partial(give_back_kernel, first, tail),
         out_shape=out,
         in_specs=[SMEM, SMEM] + [VMEM] * len(values) + more_specs,
-        out_specs=[ANY, VMEM][:len(out)],
-        scratch_shapes=[pltpu.VMEM((CLUSTERS, blocks, 8 * columns), jnp.bfloat16), pltpu.SemaphoreType.DMA],
+        out_specs=[ANY] * len(out),
+        scratch_shapes=scratch,
         input_output_aliases=aliases,
         compiler_params=pltpu.CompilerParams(vmem_limit_bytes=8 << 20),
         cost_estimate=pl.CostEstimate(flops=COVER, bytes_accessed=0, transcendentals=0),
@@ -237,12 +251,13 @@
 
     def crossed(low, high, step):
         def flip(i):
-            return 1 << (high - 1 - step if i & 1 else low + step)
+            return 1 << (high - 1 - step if role_of(i) else low + step) | 1
 
         return flip
 
     kept = []
-    for other, mine in local_sums(devices, where, deltas, labels_row):
+    for first, columns in shares_of(width):
+        other, mine = local_sums(devices, first, columns, where, deltas, labels_row)
         kept.append(split(tail, 0, where, mine, send(other, cores)))
     for chain, (out, keep) in enumerate(kept):
         kept[chain] = split(tail, 1, where, keep, send(out, crossed(1, 3, 0)))
@@ -257,7 +272,7 @@
         own = finish(tail, blocks, *pair)[None]
         near_by = jnp.concatenate([own, send(own, cores)], axis=0)
         diagonal = send(own, lambda i: 6)
-        beside = send(near_by, lambda i: 2 << (i & 1))
+        beside = send(near_by, lambda i: 2 << role_of(i) | 1)
         taken = jnp.concatenate([diagonal, beside], axis=0)
         values.append((near_by, taken, send(taken, cores)))
 

time: 53.1 us -> 49.1 us (0.925)
  waiting for transfers between devices: 14.7 us -> 11 us
  Pallas kernels: 9.88 us -> 10.7 us
  local copies, waits for them, and re-layouts: 0.68 us -> 0.04 us
    ppermute x18, waiting for transfers between devices: 14.7 us -> 11 us  [send(): return lax.ppermute(value, AXES, [(i, i ^ flip(i)) for i in range(devices)])]
    pallas_call x1 -> x2, Pallas kernels: 3.85 us -> 5.14 us  [local_sums(): pl.pallas_call(functools.partial(local_sums_kernel, devices, first), out_...]
    unnamed x4, local copies, waits for them, and re-layouts: 0.66 us -> 0.02 us
  transfers between devices with their start and end apart: 18 -> 18, of which waited for: 11 -> 11; matrix products, arithmetic and copies ran while one was open for 0% -> 0% of each run, Pallas kernels for 7% -> 11%
where the time goes in v3:
time: 49.1 us; the launch traced here: 48.9 us
  starting transfers between devices  26.3 us (54%)
  waiting for transfers between devices  11 us (22%)
  Pallas kernels  10.7 us (22%)
  between operations  0.74 us (2%)
    ppermute x18, starting transfers between devices, send(): return lax.ppermute(value, AXES, [(i, i ^ flip(i)) for i in range(devices)])  26.3 us
    ppermute x18, waiting for transfers between devices, send(): return lax.ppermute(value, AXES, [(i, i ^ flip(i)) for i in range(devices)])  11 us
    pallas_call x2, Pallas kernels, give_back(): pl.pallas_call(functools.partial(give_back_kernel, first, tail), out_shap...  5.15 us
    pallas_call x2, Pallas kernels, local_sums(): pl.pallas_call(functools.partial(local_sums_kernel, devices, first), out_...  5.14 us
  transfers between devices with their start and end apart: 18, of which 11 were waited for; matrix products, arithmetic and copies ran while one was open for 0% of the time, Pallas kernels for 11%

profile of v3, /device:TPU:0, one launch (start us, length us, event | category | flops | bytes accessed | tf_op | source)
XLA Modules:
  0.0 48.9 jit_solution(13305993284105307645)
XLA Ops:
  0.6 2.6 %local_sums.3 = (f32[1032,128]{1,0:T(8,128)S(1)}, f32[1032,128]{1,0:T(8,128)S(1)}) custom-call(s32[1]{0:T(128)} %bitcast.where, bf16[64,16,4096]{2,1,0:T(8,128)(2,1)} %deltas.3, s32[1,64]{1,0:T(1,128)} %bitcast.12), custom_call_target="tpu_custom_call" | custom-call | tf_op jit(solution)/shard_map/local_sums/pallas_call | solution.py:96
  3.8 2.6 %local_sums.2 = (f32[1032,128]{1,0:T(8,128)S(1)}, f32[1032,128]{1,0:T(8,128)S(1)}) custom-call(s32[1]{0:T(128)} %bitcast.where, bf16[64,16,4096]{2,1,0:T(8,128)(2,1)} %deltas.3, s32[1,64]{1,0:T(1,128)} %bitcast.13), custom_call_target="tpu_custom_call" | custom-call | tf_op jit(solution)/shard_map/local_sums/pallas_call | solution.py:96
  6.5 2.7 %collective-permute-start.10 = (f32[520,128]{1,0:T(8,128)S(1)}, f32[520,128]{1,0:T(8,128)S(1)}, u32[]{:S(2)}, u32[]{:S(2)}) collective-permute-start(f32[520,128]{1,0:T(8,128)S(1)} %get-tuple-element.25), channel_id=1, source_target_pairs={{0,3},{1,4},{2,7},{3,0},{4,1},{5,6},{6,5},{7,2},{8,13},{9,10},{10,... | collective-permute-start | bytes 798728 | tf_op jit(solution)/shard_map/ppermute | solution.py:247
  9.3 1.8 %collective-permute-start.1 = (f32[520,128]{1,0:T(8,128)S(1)}, f32[520,128]{1,0:T(8,128)S(1)}, u32[]{:S(2)}, u32[]{:S(2)}) collective-permute-start(f32[520,128]{1,0:T(8,128)S(1)} %get-tuple-element.19), channel_id=1, source_target_pairs={{0,3},{1,4},{2,7},{3,0},{4,1},{5,6},{6,5},{7,2},{8,13},{9,10},{10,... | collective-permute-start | bytes 798728 | tf_op jit(solution)/shard_map/ppermute | solution.py:247
  11.1 2.2 %collective-permute-done.10.arrived = f32[520,128]{1,0:T(8,128)S(1)} collective-permute-done((f32[520,128]{1,0:T(8,128)S(1)}, f32[520,128]{1,0:T(8,128)S(1)}, u32[]{:S(2)}, u32[]{:S(2)}) %collective-permute-start.10) | collective-permute-done | bytes 266272 | tf_op jit(solution)/shard_map/ppermute | solution.py:247
  13.3 2.1 %collective-permute-start.11 = (f32[264,128]{1,0:T(8,128)S(1)}, f32[264,128]{1,0:T(8,128)S(1)}, u32[]{:S(2)}, u32[]{:S(2)}) collective-permute-start(f32[264,128]{1,0:T(8,128)S(1)} %get-tuple-element.27), channel_id=1, source_target_pairs={{0,5},{1,2},{2,1},{3,6},{4,7},{5,0},{6,3},{7,4},{8,11},{9,12},{10,... | collective-permute-start | bytes 405512 | tf_op jit(solution)/shard_map/ppermute | solution.py:247
  15.5 0.7 %collective-permute-done.1.arrived = f32[520,128]{1,0:T(8,128)S(1)} collective-permute-done((f32[520,128]{1,0:T(8,128)S(1)}, f32[520,128]{1,0:T(8,128)S(1)}, u32[]{:S(2)}, u32[]{:S(2)}) %collective-permute-start.1) | collective-permute-done | bytes 266272 | tf_op jit(solution)/shard_map/ppermute | solution.py:247
  16.2 1.9 %collective-permute-start.2 = (f32[264,128]{1,0:T(8,128)S(1)}, f32[264,128]{1,0:T(8,128)S(1)}, u32[]{:S(2)}, u32[]{:S(2)}) collective-permute-start(f32[264,128]{1,0:T(8,128)S(1)} %get-tuple-element.21), channel_id=1, source_target_pairs={{0,5},{1,2},{2,1},{3,6},{4,7},{5,0},{6,3},{7,4},{8,11},{9,12},{10,... | collective-permute-start | bytes 405512 | tf_op jit(solution)/shard_map/ppermute | solution.py:247
  18.3 1.7 %collective-permute-start.12 = (f32[264,128]{1,0:T(8,128)S(1)}, f32[264,128]{1,0:T(8,128)S(1)}, u32[]{:S(2)}, u32[]{:S(2)}) collective-permute-start(f32[264,128]{1,0:T(8,128)S(1)} %add.18), channel_id=1, source_target_pairs={{0,9},{1,16},{2,19},{3,10},{4,21},{5,12},{6,15},{7,22},{8,25},{9,0... | collective-permute-start | bytes 405512 | tf_op jit(solution)/shard_map/ppermute | solution.py:247
  20.0 0.8 %collective-permute-done.2 = f32[264,128]{1,0:T(8,128)S(1)} collective-permute-done((f32[264,128]{1,0:T(8,128)S(1)}, f32[264,128]{1,0:T(8,128)S(1)}, u32[]{:S(2)}, u32[]{:S(2)}) %collective-permute-start.2) | collective-permute-done | bytes 135200 | tf_op jit(solution)/shard_map/ppermute | solution.py:247
  20.8 1.9 %collective-permute-start.3 = (f32[264,128]{1,0:T(8,128)S(1)}, f32[264,128]{1,0:T(8,128)S(1)}, u32[]{:S(2)}, u32[]{:S(2)}) collective-permute-start(f32[264,128]{1,0:T(8,128)S(1)} %add.16), channel_id=1, source_target_pairs={{0,9},{1,16},{2,19},{3,10},{4,21},{5,12},{6,15},{7,22},{8,25},{9,0... | collective-permute-start | bytes 405512 | tf_op jit(solution)/shard_map/ppermute | solution.py:247
  22.7 0.8 %collective-permute-done.12 = f32[264,128]{1,0:T(8,128)S(1)} collective-permute-done((f32[264,128]{1,0:T(8,128)S(1)}, f32[264,128]{1,0:T(8,128)S(1)}, u32[]{:S(2)}, u32[]{:S(2)}) %collective-permute-start.12) | collective-permute-done | bytes 135200 | tf_op jit(solution)/shard_map/ppermute | solution.py:247
  23.5 3.2 %collective-permute-start.13 = (f32[264,128]{1,0:T(8,128)S(1)}, f32[264,128]{1,0:T(8,128)S(1)}, u32[]{:S(2)}, u32[]{:S(2)}) collective-permute-start(f32[264,128]{1,0:T(8,128)S(1)} %add.19.kept.rest_0_), channel_id=1, source_target_pairs={{0,17},{1,8},{2,11},{3,18},{4,13},{5,20},{6,23},{7,14},{8,1},{9,24... | collective-permute-start | bytes 405512 | tf_op jit(solution)/shard_map/ppermute | solution.py:247
  26.8 2.8 %collective-permute-start.4 = (f32[264,128]{1,0:T(8,128)S(1)}, f32[264,128]{1,0:T(8,128)S(1)}, u32[]{:S(2)}, u32[]{:S(2)}) collective-permute-start(f32[264,128]{1,0:T(8,128)S(1)} %add.17.kept), channel_id=1, source_target_pairs={{0,17},{1,8},{2,11},{3,18},{4,13},{5,20},{6,23},{7,14},{8,1},{9,24... | collective-permute-start | bytes 405512 | tf_op jit(solution)/shard_map/ppermute | solution.py:247
  29.6 2.1 %collective-permute-done.13.arrived.rest_1_ = f32[264,128]{1,0:T(8,128)S(1)} collective-permute-done((f32[264,128]{1,0:T(8,128)S(1)}, f32[264,128]{1,0:T(8,128)S(1)}, u32[]{:S(2)}, u32[]{:S(2)}) %collective-permute-start.13) | collective-permute-done | bytes 135200 | tf_op jit(solution)/shard_map/ppermute | solution.py:247
  32.2 2.4 %collective-permute-start.15 = (bf16[1,128,256]{2,1,0:T(8,128)(2,1)S(1)}, bf16[1,128,256]{2,1,0:T(8,128)(2,1)S(1)}, u32[]{:S(2)}, u32[]{:S(2)}) collective-permute-start(bf16[1,128,256]{2,1,0:T(8,128)(2,1)S(1)} %bitcast.7), channel_id=1, source_target_pairs={{0,6},{1,7},{2,4},{3,5},{4,2},{5,3},{6,0},{7,1},{8,14},{9,15},{10,... | collective-permute-start | bytes 196616 | tf_op jit(solution)/shard_map/ppermute | solution.py:247
  35.0 2.3 %collective-permute-start.6 = (bf16[1,128,256]{2,1,0:T(8,128)(2,1)S(1)}, bf16[1,128,256]{2,1,0:T(8,128)(2,1)S(1)}, u32[]{:S(2)}, u32[]{:S(2)}) collective-permute-start(bf16[1,128,256]{2,1,0:T(8,128)(2,1)S(1)} %bitcast.9), channel_id=1, source_target_pairs={{0,6},{1,7},{2,4},{3,5},{4,2},{5,3},{6,0},{7,1},{8,14},{9,15},{10,... | collective-permute-start | bytes 196616 | tf_op jit(solution)/shard_map/ppermute | solution.py:247
  37.5 1.0 %collective-permute-done.5 = bf16[1,128,256]{2,1,0:T(8,128)(2,1)S(1)} collective-permute-done((bf16[1,128,256]{2,1,0:T(8,128)(2,1)S(1)}, bf16[1,128,256]{2,1,0:T(8,128)(2,1)S(1)}, u32[]{:S(2)}, u32[]{:S(2)}) %collective-permute-start.5) | collective-permute-done | bytes 65568 | tf_op jit(solution)/shard_map/ppermute | solution.py:247
  38.5 0.7 %collective-permute-start.7 = (bf16[2,128,256]{2,1,0:T(8,128)(2,1)S(1)}, bf16[2,128,256]{2,1,0:T(8,128)(2,1)S(1)}, u32[]{:S(2)}, u32[]{:S(2)}) collective-permute-start(bf16[2,128,256]{2,1,0:T(8,128)(2,1)S(1)} %pad_maximum_fusion.near_by), channel_id=1, source_target_pairs={{0,3},{1,4},{2,7},{3,0},{4,1},{5,6},{6,5},{7,2},{8,13},{9,10},{10,... | collective-permute-start | bytes 393224 | tf_op jit(solution)/shard_map/ppermute | solution.py:247
  39.2 1.0 %collective-permute-done.6 = bf16[1,128,256]{2,1,0:T(8,128)(2,1)S(1)} collective-permute-done((bf16[1,128,256]{2,1,0:T(8,128)(2,1)S(1)}, bf16[1,128,256]{2,1,0:T(8,128)(2,1)S(1)}, u32[]{:S(2)}, u32[]{:S(2)}) %collective-permute-start.6) | collective-permute-done | bytes 65568 | tf_op jit(solution)/shard_map/ppermute | solution.py:247
  40.2 1.5 %collective-permute-done.16 = bf16[2,128,256]{2,1,0:T(8,128)(2,1)S(1)} collective-permute-done((bf16[2,128,256]{2,1,0:T(8,128)(2,1)S(1)}, bf16[2,128,256]{2,1,0:T(8,128)(2,1)S(1)}, u32[]{:S(2)}, u32[]{:S(2)}) %collective-permute-start.16) | collective-permute-done | bytes 131104 | tf_op jit(solution)/shard_map/ppermute | solution.py:247
  41.7 0.9 %collective-permute-start.17 = (bf16[3,128,256]{2,1,0:T(8,128)(2,1)S(1)}, bf16[3,128,256]{2,1,0:T(8,128)(2,1)S(1)}, u32[]{:S(2)}, u32[]{:S(2)}) collective-permute-start(bf16[3,128,256]{2,1,0:T(8,128)(2,1)S(1)} %constant_dynamic-update-slice_fusion.2.taken), channel_id=1, source_target_pairs={{0,1},{1,0},{2,3},{3,2},{4,5},{5,4},{6,7},{7,6},{8,9},{9,8},{10,11... | collective-permute-start | bytes 589832 | tf_op jit(solution)/shard_map/ppermute | solution.py:247
  43.7 2.6 %give_back.2 = (bf16[64,16,4096]{2,1,0:T(8,128)(2,1)}, s32[1,64]{1,0:T(1,128)}) custom-call(s32[1]{0:T(128)} %bitcast.where, s32[64]{0:T(128)S(1)} %bitcast.14, bf16[2,128,256]{2,1,0:T(8,128)(2,1)S(1)} %pad_maximum_fusion.1.near_by, bf16[3,128,256]{2,1,0:T(8,128)(2,1)S(1)} %constant_dynamic-update-slice_fusion.2.taken, ...), custom_call_target="tpu_custom_call" | custom-call | flops 67108864 | tf_op jit(solution)/shard_map/give_back/pallas_call | solution.py:225
  46.3 2.6 %give_back.3 = bf16[64,16,4096]{2,1,0:T(8,128)(2,1)} custom-call(s32[1]{0:T(128)} %bitcast.where, s32[64]{0:T(128)S(1)} %bitcast.16, bf16[2,128,256]{2,1,0:T(8,128)(2,1)S(1)} %pad_maximum_fusion.near_by, bf16[3,128,256]{2,1,0:T(8,128)(2,1)S(1)} %constant_dynamic-update-slice_fusion.taken, ...), custom_call_target="tpu_custom_call", output_to_operand_aliasing={{}: (5, {})} | custom-call | flops 67108864 | tf_op jit(solution)/shard_map/give_back/pallas_call | solution.py:225
  (34 shorter events, 3.4 us)
Async XLA Ops:
  3.2 40.5 %copy-start = (s32[64,1]{0,1:T(1,128)S(1)}, s32[64,1]{0,1:T(1,128)}, u32[]{:S(2)}) copy-start(s32[64,1]{0,1:T(1,128)} %param.3) | copy-start | bytes 772
  3.2 3.2 %collective-permute-start.9 = (f32[1032,128]{1,0:T(8,128)S(1)}, f32[1032,128]{1,0:T(8,128)S(1)}, u32[]{:S(2)}, u32[]{:S(2)}) collective-permute-start(f32[1032,128]{1,0:T(8,128)S(1)} %get-tuple-element.23), channel_id=1, source_target_pairs={{0,1},{1,0},{2,3},{3,2},{4,5},{5,4},{6,7},{7,6},{8,9},{9,8},{10,11... | collective-permute-start | bytes 1585160 | tf_op jit(solution)/shard_map/ppermute | solution.py:247
  6.4 2.8 %collective-permute-start = (f32[1032,128]{1,0:T(8,128)S(1)}, f32[1032,128]{1,0:T(8,128)S(1)}, u32[]{:S(2)}, u32[]{:S(2)}) collective-permute-start(f32[1032,128]{1,0:T(8,128)S(1)} %get-tuple-element.17), channel_id=1, source_target_pairs={{0,1},{1,0},{2,3},{3,2},{4,5},{5,4},{6,7},{7,6},{8,9},{9,8},{10,11... | collective-permute-start | bytes 1585160 | tf_op jit(solution)/shard_map/ppermute | solution.py:247
  6.5 6.8 %collective-permute-start.10 = (f32[520,128]{1,0:T(8,128)S(1)}, f32[520,128]{1,0:T(8,128)S(1)}, u32[]{:S(2)}, u32[]{:S(2)}) collective-permute-start(f32[520,128]{1,0:T(8,128)S(1)} %get-tuple-element.25), channel_id=1, source_target_pairs={{0,3},{1,4},{2,7},{3,0},{4,1},{5,6},{6,5},{7,2},{8,13},{9,10},{10,... | collective-permute-start | bytes 798728 | tf_op jit(solution)/shard_map/ppermute | solution.py:247
  9.3 6.9 %collective-permute-start.1 = (f32[520,128]{1,0:T(8,128)S(1)}, f32[520,128]{1,0:T(8,128)S(1)}, u32[]{:S(2)}, u32[]{:S(2)}) collective-permute-start(f32[520,128]{1,0:T(8,128)S(1)} %get-tuple-element.19), channel_id=1, source_target_pairs={{0,3},{1,4},{2,7},{3,0},{4,1},{5,6},{6,5},{7,2},{8,13},{9,10},{10,... | collective-permute-start | bytes 798728 | tf_op jit(solution)/shard_map/ppermute | solution.py:247
  13.3 4.9 %collective-permute-start.11 = (f32[264,128]{1,0:T(8,128)S(1)}, f32[264,128]{1,0:T(8,128)S(1)}, u32[]{:S(2)}, u32[]{:S(2)}) collective-permute-start(f32[264,128]{1,0:T(8,128)S(1)} %get-tuple-element.27), channel_id=1, source_target_pairs={{0,5},{1,2},{2,1},{3,6},{4,7},{5,0},{6,3},{7,4},{8,11},{9,12},{10,... | collective-permute-start | bytes 405512 | tf_op jit(solution)/shard_map/ppermute | solution.py:247
  16.2 4.6 %collective-permute-start.2 = (f32[264,128]{1,0:T(8,128)S(1)}, f32[264,128]{1,0:T(8,128)S(1)}, u32[]{:S(2)}, u32[]{:S(2)}) collective-permute-start(f32[264,128]{1,0:T(8,128)S(1)} %get-tuple-element.21), channel_id=1, source_target_pairs={{0,5},{1,2},{2,1},{3,6},{4,7},{5,0},{6,3},{7,4},{8,11},{9,12},{10,... | collective-permute-start | bytes 405512 | tf_op jit(solution)/shard_map/ppermute | solution.py:247
  18.3 5.2 %collective-permute-start.12 = (f32[264,128]{1,0:T(8,128)S(1)}, f32[264,128]{1,0:T(8,128)S(1)}, u32[]{:S(2)}, u32[]{:S(2)}) collective-permute-start(f32[264,128]{1,0:T(8,128)S(1)} %add.18), channel_id=1, source_target_pairs={{0,9},{1,16},{2,19},{3,10},{4,21},{5,12},{6,15},{7,22},{8,25},{9,0... | collective-permute-start | bytes 405512 | tf_op jit(solution)/shard_map/ppermute | solution.py:247
  20.8 5.9 %collective-permute-start.3 = (f32[264,128]{1,0:T(8,128)S(1)}, f32[264,128]{1,0:T(8,128)S(1)}, u32[]{:S(2)}, u32[]{:S(2)}) collective-permute-start(f32[264,128]{1,0:T(8,128)S(1)} %add.16), channel_id=1, source_target_pairs={{0,9},{1,16},{2,19},{3,10},{4,21},{5,12},{6,15},{7,22},{8,25},{9,0... | collective-permute-start | bytes 405512 | tf_op jit(solution)/shard_map/ppermute | solution.py:247
  23.5 8.1 %collective-permute-start.13 = (f32[264,128]{1,0:T(8,128)S(1)}, f32[264,128]{1,0:T(8,128)S(1)}, u32[]{:S(2)}, u32[]{:S(2)}) collective-permute-start(f32[264,128]{1,0:T(8,128)S(1)} %add.19.kept.rest_0_), channel_id=1, source_target_pairs={{0,17},{1,8},{2,11},{3,18},{4,13},{5,20},{6,23},{7,14},{8,1},{9,24... | collective-permute-start | bytes 405512 | tf_op jit(solution)/shard_map/ppermute | solution.py:247
  26.8 8.1 %collective-permute-start.4 = (f32[264,128]{1,0:T(8,128)S(1)}, f32[264,128]{1,0:T(8,128)S(1)}, u32[]{:S(2)}, u32[]{:S(2)}) collective-permute-start(f32[264,128]{1,0:T(8,128)S(1)} %add.17.kept), channel_id=1, source_target_pairs={{0,17},{1,8},{2,11},{3,18},{4,13},{5,20},{6,23},{7,14},{8,1},{9,24... | collective-permute-start | bytes 405512 | tf_op jit(solution)/shard_map/ppermute | solution.py:247
  31.8 5.5 %collective-permute-start.14 = (bf16[1,128,256]{2,1,0:T(8,128)(2,1)S(1)}, bf16[1,128,256]{2,1,0:T(8,128)(2,1)S(1)}, u32[]{:S(2)}, u32[]{:S(2)}) collective-permute-start(bf16[1,128,256]{2,1,0:T(8,128)(2,1)S(1)} %bitcast.6), channel_id=1, source_target_pairs={{0,1},{1,0},{2,3},{3,2},{4,5},{5,4},{6,7},{7,6},{8,9},{9,8},{10,11... | collective-permute-start | bytes 196616 | tf_op jit(solution)/shard_map/ppermute | solution.py:247
  32.2 7.0 %collective-permute-start.15 = (bf16[1,128,256]{2,1,0:T(8,128)(2,1)S(1)}, bf16[1,128,256]{2,1,0:T(8,128)(2,1)S(1)}, u32[]{:S(2)}, u32[]{:S(2)}) collective-permute-start(bf16[1,128,256]{2,1,0:T(8,128)(2,1)S(1)} %bitcast.7), channel_id=1, source_target_pairs={{0,6},{1,7},{2,4},{3,5},{4,2},{5,3},{6,0},{7,1},{8,14},{9,15},{10,... | collective-permute-start | bytes 196616 | tf_op jit(solution)/shard_map/ppermute | solution.py:247
  35.0 5.2 %collective-permute-start.6 = (bf16[1,128,256]{2,1,0:T(8,128)(2,1)S(1)}, bf16[1,128,256]{2,1,0:T(8,128)(2,1)S(1)}, u32[]{:S(2)}, u32[]{:S(2)}) collective-permute-start(bf16[1,128,256]{2,1,0:T(8,128)(2,1)S(1)} %bitcast.9), channel_id=1, source_target_pairs={{0,6},{1,7},{2,4},{3,5},{4,2},{5,3},{6,0},{7,1},{8,14},{9,15},{10,... | collective-permute-start | bytes 196616 | tf_op jit(solution)/shard_map/ppermute | solution.py:247
  37.2 1.3 %collective-permute-start.5 = (bf16[1,128,256]{2,1,0:T(8,128)(2,1)S(1)}, bf16[1,128,256]{2,1,0:T(8,128)(2,1)S(1)}, u32[]{:S(2)}, u32[]{:S(2)}) collective-permute-start(bf16[1,128,256]{2,1,0:T(8,128)(2,1)S(1)} %bitcast.10), channel_id=1, source_target_pairs={{0,1},{1,0},{2,3},{3,2},{4,5},{5,4},{6,7},{7,6},{8,9},{9,8},{10,11... | collective-permute-start | bytes 196616 | tf_op jit(solution)/shard_map/ppermute | solution.py:247
  37.3 4.5 %collective-permute-start.16 = (bf16[2,128,256]{2,1,0:T(8,128)(2,1)S(1)}, bf16[2,128,256]{2,1,0:T(8,128)(2,1)S(1)}, u32[]{:S(2)}, u32[]{:S(2)}) collective-permute-start(bf16[2,128,256]{2,1,0:T(8,128)(2,1)S(1)} %pad_maximum_fusion.1.near_by), channel_id=1, source_target_pairs={{0,3},{1,4},{2,7},{3,0},{4,1},{5,6},{6,5},{7,2},{8,13},{9,10},{10,... | collective-permute-start | bytes 393224 | tf_op jit(solution)/shard_map/ppermute | solution.py:247
  38.5 4.6 %collective-permute-start.7 = (bf16[2,128,256]{2,1,0:T(8,128)(2,1)S(1)}, bf16[2,128,256]{2,1,0:T(8,128)(2,1)S(1)}, u32[]{:S(2)}, u32[]{:S(2)}) collective-permute-start(bf16[2,128,256]{2,1,0:T(8,128)(2,1)S(1)} %pad_maximum_fusion.near_by), channel_id=1, source_target_pairs={{0,3},{1,4},{2,7},{3,0},{4,1},{5,6},{6,5},{7,2},{8,13},{9,10},{10,... | collective-permute-start | bytes 393224 | tf_op jit(solution)/shard_map/ppermute | solution.py:247
  41.7 2.0 %collective-permute-start.17 = (bf16[3,128,256]{2,1,0:T(8,128)(2,1)S(1)}, bf16[3,128,256]{2,1,0:T(8,128)(2,1)S(1)}, u32[]{:S(2)}, u32[]{:S(2)}) collective-permute-start(bf16[3,128,256]{2,1,0:T(8,128)(2,1)S(1)} %constant_dynamic-update-slice_fusion.2.taken), channel_id=1, source_target_pairs={{0,1},{1,0},{2,3},{3,2},{4,5},{5,4},{6,7},{7,6},{8,9},{9,8},{10,11... | collective-permute-start | bytes 589832 | tf_op jit(solution)/shard_map/ppermute | solution.py:247
  43.2 3.2 %collective-permute-start.8 = (bf16[3,128,256]{2,1,0:T(8,128)(2,1)S(1)}, bf16[3,128,256]{2,1,0:T(8,128)(2,1)S(1)}, u32[]{:S(2)}, u32[]{:S(2)}) collective-permute-start(bf16[3,128,256]{2,1,0:T(8,128)(2,1)S(1)} %constant_dynamic-update-slice_fusion.taken), channel_id=1, source_target_pairs={{0,1},{1,0},{2,3},{3,2},{4,5},{5,4},{6,7},{7,6},{8,9},{9,8},{10,11... | collective-permute-start | bytes 589832 | tf_op jit(solution)/shard_map/ppermute | solution.py:247

commit v4 on v3

--- a/solution.py
+++ b/solution.py
@@ -11,7 +11,7 @@
 CLUSTERS = 8
 LANES = 128
 AXES = ("dp", "group")
-SHARES = (2, 2)
+CHAINS = 2
 COVER = 1 << 26
 
 VMEM = pl.BlockSpec(memory_space=pltpu.VMEM)
@@ -20,12 +20,6 @@
 HBM = pl.BlockSpec(memory_space=pltpu.HBM)
 
 
-def shares_of(width):
-    unit = width // (8 * sum(SHARES))
-    starts = [8 * unit * sum(SHARES[:at]) for at in range(len(SHARES))]
-    return [(start, unit * share) for start, share in zip(starts, SHARES)]
-
-
 def role_of(index):
     for shift in (16, 8, 4, 2, 1):
         index = index ^ (index >> shift)
@@ -44,19 +38,32 @@
     return CLUSTERS * pl.cdiv(devices, LANES)
 
 
-def local_sums_kernel(devices, first, where, deltas, labels_row, other, mine, held, labels_here, sems):
+def bit_at(me, role, step):
+    return (me >> (1 + (role ^ step))) & 1
+
+
+def quarter_of(index):
+    return (index >> 1) & 3
+
+
+def local_sums_kernel(devices, chain, where, deltas, labels_row, other, mine, held, labels_here, sems):
     clients, blocks, _ = deltas.shape
     me = where[0]
     role = role_of(me)
     columns = held.shape[3]
-    arrive = pltpu.make_async_copy(labels_row, labels_here, sems.at[4])
+    piece = columns // 2
+    arrive = pltpu.make_async_copy(labels_row, labels_here, sems.at[8])
     arrive.start()
     copies = []
     for part in range(4):
         half = (1 - role) if part < 2 else role
-        start = pl.multiple_of(first + (half * 2 + part % 2) * columns, LANES)
-        copies.append(pltpu.make_async_copy(deltas.at[:, :, pl.ds(start, columns)], held.at[part], sems.at[part]))
-        copies[-1].start()
+        for second in range(2):
+            owner = (part % 2) << (1 + half) | second << (2 - half)
+            start = pl.multiple_of(((quarter_of(owner) * CHAINS + chain) * 2 + half) * piece, LANES)
+            copies.append(pltpu.make_async_copy(
+                deltas.at[:, :, pl.ds(start, piece)], held.at[part, :, :, second * piece:(second + 1) * piece],
+                sems.at[part * 2 + second]))
+            copies[-1].start()
 
     rows, depth = CLUSTERS * blocks, clients * blocks
     spread = (lax.broadcasted_iota(jnp.int32, (clients, depth), 1) // blocks
@@ -81,7 +88,8 @@
         mine[at:at + CLUSTERS, :] = table
 
     for part in range(4):
-        copies[part].wait()
+        copies[2 * part].wait()
+        copies[2 * part + 1].wait()
         sums = jnp.dot(pick, held[part].reshape(depth, columns), preferred_element_type=jnp.float32)
         target = other if part < 2 else mine
         for block in range(columns // LANES):
@@ -89,25 +97,22 @@
             target[to:to + rows, :] = sums[:, block * LANES:(block + 1) * LANES]
 
 
-def local_sums(devices, first, columns, where, deltas, labels_row):
-    clients, blocks, _ = deltas.shape
+def local_sums(devices, chain, where, deltas, labels_row):
+    clients, blocks, width = deltas.shape
+    columns = width // (8 * CHAINS)
     height = 4 * columns // LANES * CLUSTERS * blocks + count_rows(devices)
     out = pltpu.VMEM((height, LANES), jnp.float32)
     return pl.pallas_call(
-        functools.partial(local_sums_kernel, devices, first),
+        functools.partial(local_sums_kernel, devices, chain),
         out_shape=(out, out),
         in_specs=[SMEM, HBM, HBM],
         out_specs=(VMEM, VMEM),
         scratch_shapes=[
             pltpu.VMEM((4, clients, blocks, 2 * columns), jnp.bfloat16), pltpu.VMEM((1, clients), jnp.int32),
-            pltpu.SemaphoreType.DMA((5,))],
+            pltpu.SemaphoreType.DMA((9,))],
         compiler_params=pltpu.CompilerParams(vmem_limit_bytes=16 << 20),
         name="local_sums",
     )(where, far_off(deltas), far_off(labels_row))
-
-
-def bit_at(me, role, step):
-    return (me >> (1 + (role ^ step))) & 1
 
 
 def split_kernel(tail, step, where, kept, arrived, send, keep):
@@ -179,64 +184,83 @@
     return jnp.sum(jnp.where(hits, before + local, 0.0), axis=0, keepdims=True).astype(jnp.int32)
 
 
-def give_back_kernel(first, tail, where, labels, near_by, taken, far, *rest):
+def own_places(me):
+    return [(quarter_of(me), [
+        (chain, other, chain, role_of(me) ^ other) for chain in range(CHAINS) for other in range(2)])]
+
+
+def rest_places(me):
+    role = role_of(me)
+    kinds = [
+        (me ^ 6, [(0, 0, role), (1, 0, 1 - role)]),
+        (me ^ (2 << role), [(0, 1, role), (0, 2, 1 - role)]),
+        (me ^ (4 >> role), [(1, 1, 1 - role), (1, 2, role)]),
+    ]
+    return [(quarter_of(chip), [
+        (2 * chain + array, slot, chain, half) for chain in range(CHAINS) for array, slot, half in pieces])
+        for chip, pieces in kinds]
+
+
+def give_back_kernel(places, arrays, tail, where, labels, *rest):
     me = where[0]
+    models, rest = rest[:arrays], rest[arrays:]
     if tail:
         kept, arrived, labels_row, returned, rank, laid, sem, rank_here, rank_sem = rest
     else:
         _, returned, laid, sem = rest
-    _, _, columns = near_by.shape
+    columns = models[0].shape[2]
     clients, blocks, _ = returned.shape
-    role = role_of(me)
-    beside, opposite = 2 << role, 4 >> role
-    for source, slot, half, flip in (
-            (near_by, 0, role, 0), (near_by, 1, 1 - role, 0), (taken, 0, role, 6), (taken, 1, role, beside),
-            (taken, 2, 1 - role, beside), (far, 0, 1 - role, 6), (far, 1, 1 - role, opposite),
-            (far, 2, role, opposite)):
-        owner = me ^ flip
-        piece = half * 4 + bit_at(owner, half, 0) * 2 + bit_at(owner, half, 1)
-        to = pl.ds(pl.multiple_of(piece * columns, LANES), columns)
-        for cluster in range(CLUSTERS):
-            laid[cluster, :, to] = source[slot, cluster * blocks:(cluster + 1) * blocks, :]
-    across = pl.ds(first, 8 * columns)
-    for client in range(clients):
-        pltpu.make_async_copy(laid.at[labels[client]], returned.at[client, :, across], sem).start()
+    ends, offset = [], 0
+    for at, (quarter, pieces) in enumerate(places(me)):
+        size = len(pieces) * columns
+        first = pieces[0][2]
+        for array, slot, chain, half in pieces:
+            to = offset + ((chain - first) * 2 + half) * columns
+            to = pl.ds(pl.multiple_of(to, LANES), columns)
+            for cluster in range(CLUSTERS):
+                laid[cluster, :, to] = models[array][slot, cluster * blocks:(cluster + 1) * blocks, :]
+        across = pl.ds(pl.multiple_of((quarter * CHAINS + first) * 2 * columns, LANES), size)
+        for client in range(clients):
+            pltpu.make_async_copy(
+                laid.at[labels[client], :, offset:offset + size], returned.at[client, :, across], sem.at[at]).start()
+        whole = returned.at[:, :, across]
+        ends.append(pltpu.make_async_copy(whole, whole, sem.at[at]))
+        offset += size
     if tail:
         rank_here[...] = ranks_of(me, table_of(tail, kept, arrived), labels_row[...])
-        ranks = pltpu.make_async_copy(rank_here, rank, rank_sem)
-        ranks.start()
-        ranks.wait()
-    whole = returned.at[:, :, across]
-    pltpu.make_async_copy(whole, whole, sem).wait()
-
-
-def give_back(first, where, labels, values, shape, returned=None, ranked=None):
-    columns = values[0].shape[2]
-    blocks = shape[1]
-    scratch = [pltpu.VMEM((CLUSTERS, blocks, 8 * columns), jnp.bfloat16), pltpu.SemaphoreType.DMA]
+        ends.append(pltpu.make_async_copy(rank_here, rank, rank_sem))
+        ends[-1].start()
+    for end in ends:
+        end.wait()
+
+
+def give_back(places, where, labels, models, shape, returned=None, ranked=None):
+    columns = models[0].shape[2]
+    slots = sum(array.shape[0] for array in models)
+    scratch = [pltpu.VMEM((CLUSTERS, shape[1], slots * columns), jnp.bfloat16), pltpu.SemaphoreType.DMA((3,))]
     out = [jax.ShapeDtypeStruct(shape, jnp.bfloat16)]
     if ranked is None:
-        tail, more, more_specs, aliases = 0, (returned,), [ANY], {2 + len(values): 0}
+        tail, more, more_specs, aliases = 0, (returned,), [ANY], {2 + len(models): 0}
     else:
         tail, kept, arrived, labels_row = ranked
         more, more_specs, aliases = (near(kept), near(arrived), near(labels_row)), [VMEM] * 3, {}
         out.append(jax.ShapeDtypeStruct(labels_row.shape, jnp.int32))
         scratch += [pltpu.VMEM(labels_row.shape, jnp.int32), pltpu.SemaphoreType.DMA]
     return pl.pallas_call(
-        functools.partial(give_back_kernel, first, tail),
+        functools.partial(give_back_kernel, places, len(models), tail),
         out_shape=out,
-        in_specs=[SMEM, SMEM] + [VMEM] * len(values) + more_specs,
+        in_specs=[SMEM, SMEM] + [VMEM] * len(models) + more_specs,
         out_specs=[ANY] * len(out),
         scratch_shapes=scratch,
         input_output_aliases=aliases,
         compiler_params=pltpu.CompilerParams(vmem_limit_bytes=8 << 20),
         cost_estimate=pl.CostEstimate(flops=COVER, bytes_accessed=0, transcendentals=0),
         name="give_back",
-    )(where, labels, *[near(value) for value in values], *more)
+    )(where, labels, *[near(array) for array in models], *more)
 
 
 def on_device(devices, deltas, labels):
-    clients, blocks, width = deltas.shape
+    clients, blocks, _ = deltas.shape
     where = lax.axis_index(AXES).astype(jnp.int32).reshape(1)
     labels_row = labels.reshape(1, clients)
     labels_list = labels.reshape(clients)
@@ -256,8 +280,8 @@
         return flip
 
     kept = []
-    for first, columns in shares_of(width):
-        other, mine = local_sums(devices, first, columns, where, deltas, labels_row)
+    for chain in range(CHAINS):
+        other, mine = local_sums(devices, chain, where, deltas, labels_row)
         kept.append(split(tail, 0, where, mine, send(other, cores)))
     for chain, (out, keep) in enumerate(kept):
         kept[chain] = split(tail, 1, where, keep, send(out, crossed(1, 3, 0)))
@@ -267,20 +291,18 @@
         for chain, (keep, arrived) in enumerate(kept):
             total = keep + arrived
             kept[chain] = (total, send(total, crossed(3, bits, step)))
-    values = []
+    pairs, rests = [], []
     for pair in kept:
         own = finish(tail, blocks, *pair)[None]
-        near_by = jnp.concatenate([own, send(own, cores)], axis=0)
         diagonal = send(own, lambda i: 6)
-        beside = send(near_by, lambda i: 2 << role_of(i) | 1)
+        pairs.append(jnp.concatenate([own, send(own, cores)], axis=0))
+        beside = send(pairs[-1], lambda i: 2 << role_of(i) | 1)
         taken = jnp.concatenate([diagonal, beside], axis=0)
-        values.append((near_by, taken, send(taken, cores)))
+        rests.append([taken, send(taken, cores)])
 
     give = functools.partial(give_back, where=where, labels=labels_list, shape=deltas.shape)
-    starts = [first for first, _ in shares_of(width)]
-    returned, rank = give(starts[0], values=values[0], ranked=(tail, *kept[0], labels_row))
-    for chain in range(1, len(SHARES)):
-        returned, = give(starts[chain], values=values[chain], returned=returned)
+    returned, rank = give(own_places, models=pairs, ranked=(tail, *kept[0], labels_row))
+    returned, = give(rest_places, models=rests[0] + rests[1], returned=returned)
     return returned, rank.reshape(clients)
 
 

time: 49.1 us -> 48.8 us (level)
  waiting for transfers between devices: 11 us -> 10.4 us
    ppermute x18, waiting for transfers between devices: 11 us -> 10.4 us  [send(): return lax.ppermute(value, AXES, [(i, i ^ flip(i)) for i in range(devices)])]
  transfers between devices with their start and end apart: 18 -> 18, of which waited for: 11 -> 10; matrix products, arithmetic and copies ran while one was open for 0% -> 0% of each run, Pallas kernels for 11% -> 10%
where the time goes in v4:
time: 48.8 us; the launch traced here: 48.6 us
  starting transfers between devices  26.6 us (55%)
  Pallas kernels  10.7 us (22%)
  waiting for transfers between devices  10.4 us (21%)
  between operations  0.75 us (2%)
    ppermute x18, starting transfers between devices, send(): return lax.ppermute(value, AXES, [(i, i ^ flip(i)) for i in range(devices)])  26.6 us
    ppermute x18, waiting for transfers between devices, send(): return lax.ppermute(value, AXES, [(i, i ^ flip(i)) for i in range(devices)])  10.4 us
    pallas_call x2, Pallas kernels, local_sums(): pl.pallas_call(functools.partial(local_sums_kernel, devices, chain), out_...  5.23 us
    pallas_call x2, Pallas kernels, give_back(): pl.pallas_call(functools.partial(give_back_kernel, places, len(models), t...  5.06 us
  transfers between devices with their start and end apart: 18, of which 10 were waited for; matrix products, arithmetic and copies ran while one was open for 0% of the time, Pallas kernels for 10%

profile of v4, /device:TPU:0, one launch (start us, length us, event | category | flops | bytes accessed | tf_op | source)
XLA Modules:
  0.0 48.6 jit_solution(2331245409081989574)
XLA Ops:
  0.6 2.6 %local_sums.3 = (f32[1032,128]{1,0:T(8,128)S(1)}, f32[1032,128]{1,0:T(8,128)S(1)}) custom-call(s32[1]{0:T(128)} %bitcast.where, bf16[64,16,4096]{2,1,0:T(8,128)(2,1)} %deltas.3, s32[1,64]{1,0:T(1,128)} %bitcast.12), custom_call_target="tpu_custom_call" | custom-call | tf_op jit(solution)/shard_map/local_sums/pallas_call | solution.py:105
  3.3 0.6 %collective-permute-start.9 = (f32[1032,128]{1,0:T(8,128)S(1)}, f32[1032,128]{1,0:T(8,128)S(1)}, u32[]{:S(2)}, u32[]{:S(2)}) collective-permute-start(f32[1032,128]{1,0:T(8,128)S(1)} %get-tuple-element.23), channel_id=1, source_target_pairs={{0,1},{1,0},{2,3},{3,2},{4,5},{5,4},{6,7},{7,6},{8,9},{9,8},{10,11... | collective-permute-start | bytes 1585160 | tf_op jit(solution)/shard_map/ppermute | solution.py:271
  3.8 2.6 %local_sums.2 = (f32[1032,128]{1,0:T(8,128)S(1)}, f32[1032,128]{1,0:T(8,128)S(1)}) custom-call(s32[1]{0:T(128)} %bitcast.where, bf16[64,16,4096]{2,1,0:T(8,128)(2,1)} %deltas.3, s32[1,64]{1,0:T(1,128)} %bitcast.13), custom_call_target="tpu_custom_call" | custom-call | tf_op jit(solution)/shard_map/local_sums/pallas_call | solution.py:105
  6.6 2.7 %collective-permute-start.10 = (f32[520,128]{1,0:T(8,128)S(1)}, f32[520,128]{1,0:T(8,128)S(1)}, u32[]{:S(2)}, u32[]{:S(2)}) collective-permute-start(f32[520,128]{1,0:T(8,128)S(1)} %get-tuple-element.25), channel_id=1, source_target_pairs={{0,3},{1,4},{2,7},{3,0},{4,1},{5,6},{6,5},{7,2},{8,13},{9,10},{10,... | collective-permute-start | bytes 798728 | tf_op jit(solution)/shard_map/ppermute | solution.py:271
  9.3 1.8 %collective-permute-start.1 = (f32[520,128]{1,0:T(8,128)S(1)}, f32[520,128]{1,0:T(8,128)S(1)}, u32[]{:S(2)}, u32[]{:S(2)}) collective-permute-start(f32[520,128]{1,0:T(8,128)S(1)} %get-tuple-element.19), channel_id=1, source_target_pairs={{0,3},{1,4},{2,7},{3,0},{4,1},{5,6},{6,5},{7,2},{8,13},{9,10},{10,... | collective-permute-start | bytes 798728 | tf_op jit(solution)/shard_map/ppermute | solution.py:271
  11.1 2.2 %collective-permute-done.10.arrived = f32[520,128]{1,0:T(8,128)S(1)} collective-permute-done((f32[520,128]{1,0:T(8,128)S(1)}, f32[520,128]{1,0:T(8,128)S(1)}, u32[]{:S(2)}, u32[]{:S(2)}) %collective-permute-start.10) | collective-permute-done | bytes 266272 | tf_op jit(solution)/shard_map/ppermute | solution.py:271
  13.4 2.1 %collective-permute-start.11 = (f32[264,128]{1,0:T(8,128)S(1)}, f32[264,128]{1,0:T(8,128)S(1)}, u32[]{:S(2)}, u32[]{:S(2)}) collective-permute-start(f32[264,128]{1,0:T(8,128)S(1)} %get-tuple-element.27), channel_id=1, source_target_pairs={{0,5},{1,2},{2,1},{3,6},{4,7},{5,0},{6,3},{7,4},{8,11},{9,12},{10,... | collective-permute-start | bytes 405512 | tf_op jit(solution)/shard_map/ppermute | solution.py:271
  15.5 0.7 %collective-permute-done.1.arrived = f32[520,128]{1,0:T(8,128)S(1)} collective-permute-done((f32[520,128]{1,0:T(8,128)S(1)}, f32[520,128]{1,0:T(8,128)S(1)}, u32[]{:S(2)}, u32[]{:S(2)}) %collective-permute-start.1) | collective-permute-done | bytes 266272 | tf_op jit(solution)/shard_map/ppermute | solution.py:271
  16.3 1.9 %collective-permute-start.2 = (f32[264,128]{1,0:T(8,128)S(1)}, f32[264,128]{1,0:T(8,128)S(1)}, u32[]{:S(2)}, u32[]{:S(2)}) collective-permute-start(f32[264,128]{1,0:T(8,128)S(1)} %get-tuple-element.21), channel_id=1, source_target_pairs={{0,5},{1,2},{2,1},{3,6},{4,7},{5,0},{6,3},{7,4},{8,11},{9,12},{10,... | collective-permute-start | bytes 405512 | tf_op jit(solution)/shard_map/ppermute | solution.py:271
  18.4 1.7 %collective-permute-start.12 = (f32[264,128]{1,0:T(8,128)S(1)}, f32[264,128]{1,0:T(8,128)S(1)}, u32[]{:S(2)}, u32[]{:S(2)}) collective-permute-start(f32[264,128]{1,0:T(8,128)S(1)} %add.18), channel_id=1, source_target_pairs={{0,9},{1,16},{2,19},{3,10},{4,21},{5,12},{6,15},{7,22},{8,25},{9,0... | collective-permute-start | bytes 405512 | tf_op jit(solution)/shard_map/ppermute | solution.py:271
  20.1 0.8 %collective-permute-done.2 = f32[264,128]{1,0:T(8,128)S(1)} collective-permute-done((f32[264,128]{1,0:T(8,128)S(1)}, f32[264,128]{1,0:T(8,128)S(1)}, u32[]{:S(2)}, u32[]{:S(2)}) %collective-permute-start.2) | collective-permute-done | bytes 135200 | tf_op jit(solution)/shard_map/ppermute | solution.py:271
  20.9 1.9 %collective-permute-start.3 = (f32[264,128]{1,0:T(8,128)S(1)}, f32[264,128]{1,0:T(8,128)S(1)}, u32[]{:S(2)}, u32[]{:S(2)}) collective-permute-start(f32[264,128]{1,0:T(8,128)S(1)} %add.16), channel_id=1, source_target_pairs={{0,9},{1,16},{2,19},{3,10},{4,21},{5,12},{6,15},{7,22},{8,25},{9,0... | collective-permute-start | bytes 405512 | tf_op jit(solution)/shard_map/ppermute | solution.py:271
  22.8 0.8 %collective-permute-done.12 = f32[264,128]{1,0:T(8,128)S(1)} collective-permute-done((f32[264,128]{1,0:T(8,128)S(1)}, f32[264,128]{1,0:T(8,128)S(1)}, u32[]{:S(2)}, u32[]{:S(2)}) %collective-permute-start.12) | collective-permute-done | bytes 135200 | tf_op jit(solution)/shard_map/ppermute | solution.py:271
  23.6 3.2 %collective-permute-start.13 = (f32[264,128]{1,0:T(8,128)S(1)}, f32[264,128]{1,0:T(8,128)S(1)}, u32[]{:S(2)}, u32[]{:S(2)}) collective-permute-start(f32[264,128]{1,0:T(8,128)S(1)} %add.19.kept), channel_id=1, source_target_pairs={{0,17},{1,8},{2,11},{3,18},{4,13},{5,20},{6,23},{7,14},{8,1},{9,24... | collective-permute-start | bytes 405512 | tf_op jit(solution)/shard_map/ppermute | solution.py:271
  26.9 2.8 %collective-permute-start.4 = (f32[264,128]{1,0:T(8,128)S(1)}, f32[264,128]{1,0:T(8,128)S(1)}, u32[]{:S(2)}, u32[]{:S(2)}) collective-permute-start(f32[264,128]{1,0:T(8,128)S(1)} %add.17.kept.rest_2_), channel_id=1, source_target_pairs={{0,17},{1,8},{2,11},{3,18},{4,13},{5,20},{6,23},{7,14},{8,1},{9,24... | collective-permute-start | bytes 405512 | tf_op jit(solution)/shard_map/ppermute | solution.py:271
  29.7 2.0 %collective-permute-done.13.arrived = f32[264,128]{1,0:T(8,128)S(1)} collective-permute-done((f32[264,128]{1,0:T(8,128)S(1)}, f32[264,128]{1,0:T(8,128)S(1)}, u32[]{:S(2)}, u32[]{:S(2)}) %collective-permute-start.13) | collective-permute-done | bytes 135200 | tf_op jit(solution)/shard_map/ppermute | solution.py:271
  32.3 2.4 %collective-permute-start.14 = (bf16[1,128,256]{2,1,0:T(8,128)(2,1)S(1)}, bf16[1,128,256]{2,1,0:T(8,128)(2,1)S(1)}, u32[]{:S(2)}, u32[]{:S(2)}) collective-permute-start(bf16[1,128,256]{2,1,0:T(8,128)(2,1)S(1)} %bitcast.7), channel_id=1, source_target_pairs={{0,6},{1,7},{2,4},{3,5},{4,2},{5,3},{6,0},{7,1},{8,14},{9,15},{10,... | collective-permute-start | bytes 196616 | tf_op jit(solution)/shard_map/ppermute | solution.py:271
  35.1 2.3 %collective-permute-start.5 = (bf16[1,128,256]{2,1,0:T(8,128)(2,1)S(1)}, bf16[1,128,256]{2,1,0:T(8,128)(2,1)S(1)}, u32[]{:S(2)}, u32[]{:S(2)}) collective-permute-start(bf16[1,128,256]{2,1,0:T(8,128)(2,1)S(1)} %bitcast.10), channel_id=1, source_target_pairs={{0,6},{1,7},{2,4},{3,5},{4,2},{5,3},{6,0},{7,1},{8,14},{9,15},{10,... | collective-permute-start | bytes 196616 | tf_op jit(solution)/shard_map/ppermute | solution.py:271
  37.7 1.6 %collective-permute-start.7 = (bf16[2,128,256]{2,1,0:T(8,128)(2,1)S(1)}, bf16[2,128,256]{2,1,0:T(8,128)(2,1)S(1)}, u32[]{:S(2)}, u32[]{:S(2)}) collective-permute-start(bf16[2,128,256]{2,1,0:T(8,128)(2,1)S(1)} %pad_maximum_fusion.rest_0_), channel_id=1, source_target_pairs={{0,3},{1,4},{2,7},{3,0},{4,1},{5,6},{6,5},{7,2},{8,13},{9,10},{10,... | collective-permute-start | bytes 393224 | tf_op jit(solution)/shard_map/ppermute | solution.py:271
  39.4 1.2 %collective-permute-done.5 = bf16[1,128,256]{2,1,0:T(8,128)(2,1)S(1)} collective-permute-done((bf16[1,128,256]{2,1,0:T(8,128)(2,1)S(1)}, bf16[1,128,256]{2,1,0:T(8,128)(2,1)S(1)}, u32[]{:S(2)}, u32[]{:S(2)}) %collective-permute-start.5) | collective-permute-done | bytes 65568 | tf_op jit(solution)/shard_map/ppermute | solution.py:271
  40.5 1.4 %collective-permute-done.16 = bf16[2,128,256]{2,1,0:T(8,128)(2,1)S(1)} collective-permute-done((bf16[2,128,256]{2,1,0:T(8,128)(2,1)S(1)}, bf16[2,128,256]{2,1,0:T(8,128)(2,1)S(1)}, u32[]{:S(2)}, u32[]{:S(2)}) %collective-permute-start.16) | collective-permute-done | bytes 131104 | tf_op jit(solution)/shard_map/ppermute | solution.py:271
  42.4 0.9 %collective-permute-done.7 = bf16[2,128,256]{2,1,0:T(8,128)(2,1)S(1)} collective-permute-done((bf16[2,128,256]{2,1,0:T(8,128)(2,1)S(1)}, bf16[2,128,256]{2,1,0:T(8,128)(2,1)S(1)}, u32[]{:S(2)}, u32[]{:S(2)}) %collective-permute-start.7) | collective-permute-done | bytes 131104 | tf_op jit(solution)/shard_map/ppermute | solution.py:271
  43.5 1.9 %give_back.2 = (bf16[64,16,4096]{2,1,0:T(8,128)(2,1)}, s32[1,64]{1,0:T(1,128)}) custom-call(s32[1]{0:T(128)} %bitcast.where, s32[64]{0:T(128)S(1)} %bitcast.14, bf16[2,128,256]{2,1,0:T(8,128)(2,1)S(1)} %pad_maximum_fusion.rest_0_, bf16[2,128,256]{2,1,0:T(8,128)(2,1)S(1)} %pad_maximum_fusion.1.rest_1_, f32[264,128]{1,0:T(8,128)S(1)} %add.17.kept.rest_2_, ...), custom_call_target="tpu_custom_call" | custom-call | flops 67108864 | tf_op jit(solution)/shard_map/give_back/pallas_call | solution.py:249
  45.5 3.2 %give_back.3 = bf16[64,16,4096]{2,1,0:T(8,128)(2,1)} custom-call(s32[1]{0:T(128)} %bitcast.where, s32[64]{0:T(128)S(1)} %bitcast.16, bf16[3,128,256]{2,1,0:T(8,128)(2,1)S(1)} %constant_dynamic-update-slice_fusion.rest_0_, bf16[3,128,256]{2,1,0:T(8,128)(2,1)S(1)} %collective-permute-done.8.rest_1_, ...), custom_call_target="tpu_custom_call", output_to_operand_aliasing={{}: (6, {})} | custom-call | flops 67108864 | tf_op jit(solution)/shard_map/give_back/pallas_call | solution.py:249
  (34 shorter events, 2.5 us)
Async XLA Ops:
  3.3 40.3 %copy-start = (s32[64,1]{0,1:T(1,128)S(1)}, s32[64,1]{0,1:T(1,128)}, u32[]{:S(2)}) copy-start(s32[64,1]{0,1:T(1,128)} %param.3) | copy-start | bytes 772
  3.3 3.3 %collective-permute-start.9 = (f32[1032,128]{1,0:T(8,128)S(1)}, f32[1032,128]{1,0:T(8,128)S(1)}, u32[]{:S(2)}, u32[]{:S(2)}) collective-permute-start(f32[1032,128]{1,0:T(8,128)S(1)} %get-tuple-element.23), channel_id=1, source_target_pairs={{0,1},{1,0},{2,3},{3,2},{4,5},{5,4},{6,7},{7,6},{8,9},{9,8},{10,11... | collective-permute-start | bytes 1585160 | tf_op jit(solution)/shard_map/ppermute | solution.py:271
  6.4 2.8 %collective-permute-start = (f32[1032,128]{1,0:T(8,128)S(1)}, f32[1032,128]{1,0:T(8,128)S(1)}, u32[]{:S(2)}, u32[]{:S(2)}) collective-permute-start(f32[1032,128]{1,0:T(8,128)S(1)} %get-tuple-element.17), channel_id=1, source_target_pairs={{0,1},{1,0},{2,3},{3,2},{4,5},{5,4},{6,7},{7,6},{8,9},{9,8},{10,11... | collective-permute-start | bytes 1585160 | tf_op jit(solution)/shard_map/ppermute | solution.py:271
  6.6 6.8 %collective-permute-start.10 = (f32[520,128]{1,0:T(8,128)S(1)}, f32[520,128]{1,0:T(8,128)S(1)}, u32[]{:S(2)}, u32[]{:S(2)}) collective-permute-start(f32[520,128]{1,0:T(8,128)S(1)} %get-tuple-element.25), channel_id=1, source_target_pairs={{0,3},{1,4},{2,7},{3,0},{4,1},{5,6},{6,5},{7,2},{8,13},{9,10},{10,... | collective-permute-start | bytes 798728 | tf_op jit(solution)/shard_map/ppermute | solution.py:271
  9.3 6.9 %collective-permute-start.1 = (f32[520,128]{1,0:T(8,128)S(1)}, f32[520,128]{1,0:T(8,128)S(1)}, u32[]{:S(2)}, u32[]{:S(2)}) collective-permute-start(f32[520,128]{1,0:T(8,128)S(1)} %get-tuple-element.19), channel_id=1, source_target_pairs={{0,3},{1,4},{2,7},{3,0},{4,1},{5,6},{6,5},{7,2},{8,13},{9,10},{10,... | collective-permute-start | bytes 798728 | tf_op jit(solution)/shard_map/ppermute | solution.py:271
  13.4 4.9 %collective-permute-start.11 = (f32[264,128]{1,0:T(8,128)S(1)}, f32[264,128]{1,0:T(8,128)S(1)}, u32[]{:S(2)}, u32[]{:S(2)}) collective-permute-start(f32[264,128]{1,0:T(8,128)S(1)} %get-tuple-element.27), channel_id=1, source_target_pairs={{0,5},{1,2},{2,1},{3,6},{4,7},{5,0},{6,3},{7,4},{8,11},{9,12},{10,... | collective-permute-start | bytes 405512 | tf_op jit(solution)/shard_map/ppermute | solution.py:271
  16.3 4.6 %collective-permute-start.2 = (f32[264,128]{1,0:T(8,128)S(1)}, f32[264,128]{1,0:T(8,128)S(1)}, u32[]{:S(2)}, u32[]{:S(2)}) collective-permute-start(f32[264,128]{1,0:T(8,128)S(1)} %get-tuple-element.21), channel_id=1, source_target_pairs={{0,5},{1,2},{2,1},{3,6},{4,7},{5,0},{6,3},{7,4},{8,11},{9,12},{10,... | collective-permute-start | bytes 405512 | tf_op jit(solution)/shard_map/ppermute | solution.py:271
  18.4 5.2 %collective-permute-start.12 = (f32[264,128]{1,0:T(8,128)S(1)}, f32[264,128]{1,0:T(8,128)S(1)}, u32[]{:S(2)}, u32[]{:S(2)}) collective-permute-start(f32[264,128]{1,0:T(8,128)S(1)} %add.18), channel_id=1, source_target_pairs={{0,9},{1,16},{2,19},{3,10},{4,21},{5,12},{6,15},{7,22},{8,25},{9,0... | collective-permute-start | bytes 405512 | tf_op jit(solution)/shard_map/ppermute | solution.py:271
  20.9 5.9 %collective-permute-start.3 = (f32[264,128]{1,0:T(8,128)S(1)}, f32[264,128]{1,0:T(8,128)S(1)}, u32[]{:S(2)}, u32[]{:S(2)}) collective-permute-start(f32[264,128]{1,0:T(8,128)S(1)} %add.16), channel_id=1, source_target_pairs={{0,9},{1,16},{2,19},{3,10},{4,21},{5,12},{6,15},{7,22},{8,25},{9,0... | collective-permute-start | bytes 405512 | tf_op jit(solution)/shard_map/ppermute | solution.py:271
  23.6 8.1 %collective-permute-start.13 = (f32[264,128]{1,0:T(8,128)S(1)}, f32[264,128]{1,0:T(8,128)S(1)}, u32[]{:S(2)}, u32[]{:S(2)}) collective-permute-start(f32[264,128]{1,0:T(8,128)S(1)} %add.19.kept), channel_id=1, source_target_pairs={{0,17},{1,8},{2,11},{3,18},{4,13},{5,20},{6,23},{7,14},{8,1},{9,24... | collective-permute-start | bytes 405512 | tf_op jit(solution)/shard_map/ppermute | solution.py:271
  26.9 8.1 %collective-permute-start.4 = (f32[264,128]{1,0:T(8,128)S(1)}, f32[264,128]{1,0:T(8,128)S(1)}, u32[]{:S(2)}, u32[]{:S(2)}) collective-permute-start(f32[264,128]{1,0:T(8,128)S(1)} %add.17.kept.rest_2_), channel_id=1, source_target_pairs={{0,17},{1,8},{2,11},{3,18},{4,13},{5,20},{6,23},{7,14},{8,1},{9,24... | collective-permute-start | bytes 405512 | tf_op jit(solution)/shard_map/ppermute | solution.py:271
  31.8 5.6 %collective-permute-start.15 = (bf16[1,128,256]{2,1,0:T(8,128)(2,1)S(1)}, bf16[1,128,256]{2,1,0:T(8,128)(2,1)S(1)}, u32[]{:S(2)}, u32[]{:S(2)}) collective-permute-start(bf16[1,128,256]{2,1,0:T(8,128)(2,1)S(1)} %bitcast.6), channel_id=1, source_target_pairs={{0,1},{1,0},{2,3},{3,2},{4,5},{5,4},{6,7},{7,6},{8,9},{9,8},{10,11... | collective-permute-start | bytes 196616 | tf_op jit(solution)/shard_map/ppermute | solution.py:271
  32.3 7.0 %collective-permute-start.14 = (bf16[1,128,256]{2,1,0:T(8,128)(2,1)S(1)}, bf16[1,128,256]{2,1,0:T(8,128)(2,1)S(1)}, u32[]{:S(2)}, u32[]{:S(2)}) collective-permute-start(bf16[1,128,256]{2,1,0:T(8,128)(2,1)S(1)} %bitcast.7), channel_id=1, source_target_pairs={{0,6},{1,7},{2,4},{3,5},{4,2},{5,3},{6,0},{7,1},{8,14},{9,15},{10,... | collective-permute-start | bytes 196616 | tf_op jit(solution)/shard_map/ppermute | solution.py:271
  35.0 2.6 %collective-permute-start.6 = (bf16[1,128,256]{2,1,0:T(8,128)(2,1)S(1)}, bf16[1,128,256]{2,1,0:T(8,128)(2,1)S(1)}, u32[]{:S(2)}, u32[]{:S(2)}) collective-permute-start(bf16[1,128,256]{2,1,0:T(8,128)(2,1)S(1)} %bitcast.9), channel_id=1, source_target_pairs={{0,1},{1,0},{2,3},{3,2},{4,5},{5,4},{6,7},{7,6},{8,9},{9,8},{10,11... | collective-permute-start | bytes 196616 | tf_op jit(solution)/shard_map/ppermute | solution.py:271
  35.1 5.4 %collective-permute-start.5 = (bf16[1,128,256]{2,1,0:T(8,128)(2,1)S(1)}, bf16[1,128,256]{2,1,0:T(8,128)(2,1)S(1)}, u32[]{:S(2)}, u32[]{:S(2)}) collective-permute-start(bf16[1,128,256]{2,1,0:T(8,128)(2,1)S(1)} %bitcast.10), channel_id=1, source_target_pairs={{0,6},{1,7},{2,4},{3,5},{4,2},{5,3},{6,0},{7,1},{8,14},{9,15},{10,... | collective-permute-start | bytes 196616 | tf_op jit(solution)/shard_map/ppermute | solution.py:271
  37.4 4.5 %collective-permute-start.16 = (bf16[2,128,256]{2,1,0:T(8,128)(2,1)S(1)}, bf16[2,128,256]{2,1,0:T(8,128)(2,1)S(1)}, u32[]{:S(2)}, u32[]{:S(2)}) collective-permute-start(bf16[2,128,256]{2,1,0:T(8,128)(2,1)S(1)} %pad_maximum_fusion.1.rest_1_), channel_id=1, source_target_pairs={{0,3},{1,4},{2,7},{3,0},{4,1},{5,6},{6,5},{7,2},{8,13},{9,10},{10,... | collective-permute-start | bytes 393224 | tf_op jit(solution)/shard_map/ppermute | solution.py:271
  37.7 5.6 %collective-permute-start.7 = (bf16[2,128,256]{2,1,0:T(8,128)(2,1)S(1)}, bf16[2,128,256]{2,1,0:T(8,128)(2,1)S(1)}, u32[]{:S(2)}, u32[]{:S(2)}) collective-permute-start(bf16[2,128,256]{2,1,0:T(8,128)(2,1)S(1)} %pad_maximum_fusion.rest_0_), channel_id=1, source_target_pairs={{0,3},{1,4},{2,7},{3,0},{4,1},{5,6},{6,5},{7,2},{8,13},{9,10},{10,... | collective-permute-start | bytes 393224 | tf_op jit(solution)/shard_map/ppermute | solution.py:271
  41.9 3.5 %collective-permute-start.17 = (bf16[3,128,256]{2,1,0:T(8,128)(2,1)S(1)}, bf16[3,128,256]{2,1,0:T(8,128)(2,1)S(1)}, u32[]{:S(2)}, u32[]{:S(2)}) collective-permute-start(bf16[3,128,256]{2,1,0:T(8,128)(2,1)S(1)} %constant_dynamic-update-slice_fusion.2.rest_2_), channel_id=1, source_target_pairs={{0,1},{1,0},{2,3},{3,2},{4,5},{5,4},{6,7},{7,6},{8,9},{9,8},{10,11... | collective-permute-start | bytes 589832 | tf_op jit(solution)/shard_map/ppermute | solution.py:271
  43.3 2.1 %collective-permute-start.8 = (bf16[3,128,256]{2,1,0:T(8,128)(2,1)S(1)}, bf16[3,128,256]{2,1,0:T(8,128)(2,1)S(1)}, u32[]{:S(2)}, u32[]{:S(2)}) collective-permute-start(bf16[3,128,256]{2,1,0:T(8,128)(2,1)S(1)} %constant_dynamic-update-slice_fusion.rest_0_), channel_id=1, source_target_pairs={{0,1},{1,0},{2,3},{3,2},{4,5},{5,4},{6,7},{7,6},{8,9},{9,8},{10,11... | collective-permute-start | bytes 589832 | tf_op jit(solution)/shard_map/ppermute | solution.py:271

commit v5 on v4

--- a/solution.py
+++ b/solution.py
@@ -168,6 +168,25 @@
         compiler_params=pltpu.CompilerParams(vmem_limit_bytes=8 << 20),
         name="finish",
     )(near(kept), near(arrived))
+
+
+def join_kernel(*refs):
+    at = 0
+    for part in refs[:-1]:
+        refs[-1][at:at + part.shape[0]] = part[...]
+        at += part.shape[0]
+
+
+def join(*parts):
+    slots = sum(part.shape[0] for part in parts)
+    return pl.pallas_call(
+        join_kernel,
+        out_shape=pltpu.VMEM((slots,) + parts[0].shape[1:], parts[0].dtype),
+        in_specs=[VMEM] * len(parts),
+        out_specs=VMEM,
+        compiler_params=pltpu.CompilerParams(vmem_limit_bytes=8 << 20),
+        name="join",
+    )(*[near(part) for part in parts])
 
 
 def ranks_of(me, table, labels):
@@ -295,9 +314,9 @@
     for pair in kept:
         own = finish(tail, blocks, *pair)[None]
         diagonal = send(own, lambda i: 6)
-        pairs.append(jnp.concatenate([own, send(own, cores)], axis=0))
+        pairs.append(join(own, send(own, cores)))
         beside = send(pairs[-1], lambda i: 2 << role_of(i) | 1)
-        taken = jnp.concatenate([diagonal, beside], axis=0)
+        taken = join(diagonal, beside)
         rests.append([taken, send(taken, cores)])
 
     give = functools.partial(give_back, where=where, labels=labels_list, shape=deltas.shape)

time: 48.8 us -> 50.5 us (1.035)
  waiting for transfers between devices: 10.4 us -> 13.8 us
  starting transfers between devices: 26.6 us -> 24.8 us
    ppermute x18, waiting for transfers between devices: 10.4 us -> 13.8 us  [send(): return lax.ppermute(value, AXES, [(i, i ^ flip(i)) for i in range(devices)])]
    ppermute x18, starting transfers between devices: 26.6 us -> 24.8 us  [send(): return lax.ppermute(value, AXES, [(i, i ^ flip(i)) for i in range(devices)])]
  transfers between devices with their start and end apart: 18 -> 18, of which waited for: 10 -> 9; matrix products, arithmetic and copies ran while one was open for 0% -> 0% of each run, Pallas kernels for 10% -> 10%
where the time goes in v5:
time: 50.5 us; the launch traced here: 50.2 us
  starting transfers between devices  24.8 us (49%)
  waiting for transfers between devices  13.8 us (27%)
  Pallas kernels  10.8 us (21%)
  between operations  0.78 us (2%)
    ppermute x18, starting transfers between devices, send(): return lax.ppermute(value, AXES, [(i, i ^ flip(i)) for i in range(devices)])  24.8 us
    ppermute x18, waiting for transfers between devices, send(): return lax.ppermute(value, AXES, [(i, i ^ flip(i)) for i in range(devices)])  13.8 us
    pallas_call x2, Pallas kernels, local_sums(): pl.pallas_call(functools.partial(local_sums_kernel, devices, chain), out_...  5.23 us
    pallas_call x2, Pallas kernels, give_back(): pl.pallas_call(functools.partial(give_back_kernel, places, len(models), t...  5.06 us
  transfers between devices with their start and end apart: 18, of which 9 were waited for; matrix products, arithmetic and copies ran while one was open for 0% of the time, Pallas kernels for 10%

profile of v5, /device:TPU:0, one launch (start us, length us, event | category | flops | bytes accessed | tf_op | source)
XLA Modules:
  0.0 50.2 jit_solution(15532471727009216066)
XLA Ops:
  0.6 2.6 %local_sums.3 = (f32[1032,128]{1,0:T(8,128)S(1)}, f32[1032,128]{1,0:T(8,128)S(1)}) custom-call(s32[1]{0:T(128)} %bitcast.where, bf16[64,16,4096]{2,1,0:T(8,128)(2,1)} %deltas.3, s32[1,64]{1,0:T(1,128)} %bitcast.12), custom_call_target="tpu_custom_call" | custom-call | tf_op jit(solution)/shard_map/local_sums/pallas_call | solution.py:105
  3.8 2.6 %local_sums.2 = (f32[1032,128]{1,0:T(8,128)S(1)}, f32[1032,128]{1,0:T(8,128)S(1)}) custom-call(s32[1]{0:T(128)} %bitcast.where, bf16[64,16,4096]{2,1,0:T(8,128)(2,1)} %deltas.3, s32[1,64]{1,0:T(1,128)} %bitcast.13), custom_call_target="tpu_custom_call" | custom-call | tf_op jit(solution)/shard_map/local_sums/pallas_call | solution.py:105
  6.6 2.7 %collective-permute-start.10 = (f32[520,128]{1,0:T(8,128)S(1)}, f32[520,128]{1,0:T(8,128)S(1)}, u32[]{:S(2)}, u32[]{:S(2)}) collective-permute-start(f32[520,128]{1,0:T(8,128)S(1)} %get-tuple-element.25), channel_id=1, source_target_pairs={{0,3},{1,4},{2,7},{3,0},{4,1},{5,6},{6,5},{7,2},{8,13},{9,10},{10,... | collective-permute-start | bytes 798728 | tf_op jit(solution)/shard_map/ppermute | solution.py:290
  9.3 1.8 %collective-permute-start.1 = (f32[520,128]{1,0:T(8,128)S(1)}, f32[520,128]{1,0:T(8,128)S(1)}, u32[]{:S(2)}, u32[]{:S(2)}) collective-permute-start(f32[520,128]{1,0:T(8,128)S(1)} %get-tuple-element.19), channel_id=1, source_target_pairs={{0,3},{1,4},{2,7},{3,0},{4,1},{5,6},{6,5},{7,2},{8,13},{9,10},{10,... | collective-permute-start | bytes 798728 | tf_op jit(solution)/shard_map/ppermute | solution.py:290
  11.1 2.2 %collective-permute-done.10.arrived = f32[520,128]{1,0:T(8,128)S(1)} collective-permute-done((f32[520,128]{1,0:T(8,128)S(1)}, f32[520,128]{1,0:T(8,128)S(1)}, u32[]{:S(2)}, u32[]{:S(2)}) %collective-permute-start.10) | collective-permute-done | bytes 266272 | tf_op jit(solution)/shard_map/ppermute | solution.py:290
  13.4 2.1 %collective-permute-start.11 = (f32[264,128]{1,0:T(8,128)S(1)}, f32[264,128]{1,0:T(8,128)S(1)}, u32[]{:S(2)}, u32[]{:S(2)}) collective-permute-start(f32[264,128]{1,0:T(8,128)S(1)} %get-tuple-element.27), channel_id=1, source_target_pairs={{0,5},{1,2},{2,1},{3,6},{4,7},{5,0},{6,3},{7,4},{8,11},{9,12},{10,... | collective-permute-start | bytes 405512 | tf_op jit(solution)/shard_map/ppermute | solution.py:290
  15.5 0.7 %collective-permute-done.1.arrived = f32[520,128]{1,0:T(8,128)S(1)} collective-permute-done((f32[520,128]{1,0:T(8,128)S(1)}, f32[520,128]{1,0:T(8,128)S(1)}, u32[]{:S(2)}, u32[]{:S(2)}) %collective-permute-start.1) | collective-permute-done | bytes 266272 | tf_op jit(solution)/shard_map/ppermute | solution.py:290
  16.3 1.9 %collective-permute-start.2 = (f32[264,128]{1,0:T(8,128)S(1)}, f32[264,128]{1,0:T(8,128)S(1)}, u32[]{:S(2)}, u32[]{:S(2)}) collective-permute-start(f32[264,128]{1,0:T(8,128)S(1)} %get-tuple-element.21), channel_id=1, source_target_pairs={{0,5},{1,2},{2,1},{3,6},{4,7},{5,0},{6,3},{7,4},{8,11},{9,12},{10,... | collective-permute-start | bytes 405512 | tf_op jit(solution)/shard_map/ppermute | solution.py:290
  18.4 1.7 %collective-permute-start.12 = (f32[264,128]{1,0:T(8,128)S(1)}, f32[264,128]{1,0:T(8,128)S(1)}, u32[]{:S(2)}, u32[]{:S(2)}) collective-permute-start(f32[264,128]{1,0:T(8,128)S(1)} %add.18), channel_id=1, source_target_pairs={{0,9},{1,16},{2,19},{3,10},{4,21},{5,12},{6,15},{7,22},{8,25},{9,0... | collective-permute-start | bytes 405512 | tf_op jit(solution)/shard_map/ppermute | solution.py:290
  20.1 0.8 %collective-permute-done.2 = f32[264,128]{1,0:T(8,128)S(1)} collective-permute-done((f32[264,128]{1,0:T(8,128)S(1)}, f32[264,128]{1,0:T(8,128)S(1)}, u32[]{:S(2)}, u32[]{:S(2)}) %collective-permute-start.2) | collective-permute-done | bytes 135200 | tf_op jit(solution)/shard_map/ppermute | solution.py:290
  20.9 1.9 %collective-permute-start.3 = (f32[264,128]{1,0:T(8,128)S(1)}, f32[264,128]{1,0:T(8,128)S(1)}, u32[]{:S(2)}, u32[]{:S(2)}) collective-permute-start(f32[264,128]{1,0:T(8,128)S(1)} %add.16), channel_id=1, source_target_pairs={{0,9},{1,16},{2,19},{3,10},{4,21},{5,12},{6,15},{7,22},{8,25},{9,0... | collective-permute-start | bytes 405512 | tf_op jit(solution)/shard_map/ppermute | solution.py:290
  22.8 0.8 %collective-permute-done.12 = f32[264,128]{1,0:T(8,128)S(1)} collective-permute-done((f32[264,128]{1,0:T(8,128)S(1)}, f32[264,128]{1,0:T(8,128)S(1)}, u32[]{:S(2)}, u32[]{:S(2)}) %collective-permute-start.12) | collective-permute-done | bytes 135200 | tf_op jit(solution)/shard_map/ppermute | solution.py:290
  23.6 3.2 %collective-permute-start.13 = (f32[264,128]{1,0:T(8,128)S(1)}, f32[264,128]{1,0:T(8,128)S(1)}, u32[]{:S(2)}, u32[]{:S(2)}) collective-permute-start(f32[264,128]{1,0:T(8,128)S(1)} %add.19.kept), channel_id=1, source_target_pairs={{0,17},{1,8},{2,11},{3,18},{4,13},{5,20},{6,23},{7,14},{8,1},{9,24... | collective-permute-start | bytes 405512 | tf_op jit(solution)/shard_map/ppermute | solution.py:290
  26.9 2.8 %collective-permute-start.4 = (f32[264,128]{1,0:T(8,128)S(1)}, f32[264,128]{1,0:T(8,128)S(1)}, u32[]{:S(2)}, u32[]{:S(2)}) collective-permute-start(f32[264,128]{1,0:T(8,128)S(1)} %add.17.kept.rest_2_), channel_id=1, source_target_pairs={{0,17},{1,8},{2,11},{3,18},{4,13},{5,20},{6,23},{7,14},{8,1},{9,24... | collective-permute-start | bytes 405512 | tf_op jit(solution)/shard_map/ppermute | solution.py:290
  29.7 2.0 %collective-permute-done.13.arrived = f32[264,128]{1,0:T(8,128)S(1)} collective-permute-done((f32[264,128]{1,0:T(8,128)S(1)}, f32[264,128]{1,0:T(8,128)S(1)}, u32[]{:S(2)}, u32[]{:S(2)}) %collective-permute-start.13) | collective-permute-done | bytes 135200 | tf_op jit(solution)/shard_map/ppermute | solution.py:290
  32.3 2.6 %collective-permute-done.4.arrived.rest_3_ = f32[264,128]{1,0:T(8,128)S(1)} collective-permute-done((f32[264,128]{1,0:T(8,128)S(1)}, f32[264,128]{1,0:T(8,128)S(1)}, u32[]{:S(2)}, u32[]{:S(2)}) %collective-permute-start.4) | collective-permute-done | bytes 135200 | tf_op jit(solution)/shard_map/ppermute | solution.py:290
  35.1 1.3 %collective-permute-start.16 = (bf16[2,128,256]{2,1,0:T(8,128)(2,1)S(1)}, bf16[2,128,256]{2,1,0:T(8,128)(2,1)S(1)}, u32[]{:S(2)}, u32[]{:S(2)}) collective-permute-start(bf16[2,128,256]{2,1,0:T(8,128)(2,1)S(1)} %join.6.rest_1_), channel_id=1, source_target_pairs={{0,3},{1,4},{2,7},{3,0},{4,1},{5,6},{6,5},{7,2},{8,13},{9,10},{10,... | collective-permute-start | bytes 393224 | tf_op jit(solution)/shard_map/ppermute | solution.py:290
  36.4 1.2 %collective-permute-start.7 = (bf16[2,128,256]{2,1,0:T(8,128)(2,1)S(1)}, bf16[2,128,256]{2,1,0:T(8,128)(2,1)S(1)}, u32[]{:S(2)}, u32[]{:S(2)}) collective-permute-start(bf16[2,128,256]{2,1,0:T(8,128)(2,1)S(1)} %join.4.rest_0_), channel_id=1, source_target_pairs={{0,3},{1,4},{2,7},{3,0},{4,1},{5,6},{6,5},{7,2},{8,13},{9,10},{10,... | collective-permute-start | bytes 393224 | tf_op jit(solution)/shard_map/ppermute | solution.py:290
  37.6 1.6 %collective-permute-start.14 = (bf16[1,128,256]{2,1,0:T(8,128)(2,1)S(1)}, bf16[1,128,256]{2,1,0:T(8,128)(2,1)S(1)}, u32[]{:S(2)}, u32[]{:S(2)}) collective-permute-start(bf16[1,128,256]{2,1,0:T(8,128)(2,1)S(1)} %bitcast.11), channel_id=1, source_target_pairs={{0,6},{1,7},{2,4},{3,5},{4,2},{5,3},{6,0},{7,1},{8,14},{9,15},{10,... | collective-permute-start | bytes 196616 | tf_op jit(solution)/shard_map/ppermute | solution.py:290
  39.3 1.3 %collective-permute-start.5 = (bf16[1,128,256]{2,1,0:T(8,128)(2,1)S(1)}, bf16[1,128,256]{2,1,0:T(8,128)(2,1)S(1)}, u32[]{:S(2)}, u32[]{:S(2)}) collective-permute-start(bf16[1,128,256]{2,1,0:T(8,128)(2,1)S(1)} %bitcast.8), channel_id=1, source_target_pairs={{0,6},{1,7},{2,4},{3,5},{4,2},{5,3},{6,0},{7,1},{8,14},{9,15},{10,... | collective-permute-start | bytes 196616 | tf_op jit(solution)/shard_map/ppermute | solution.py:290
  40.6 3.8 %collective-permute-done.14.refs_0_ = bf16[1,128,256]{2,1,0:T(8,128)(2,1)S(1)} collective-permute-done((bf16[1,128,256]{2,1,0:T(8,128)(2,1)S(1)}, bf16[1,128,256]{2,1,0:T(8,128)(2,1)S(1)}, u32[]{:S(2)}, u32[]{:S(2)}) %collective-permute-start.14) | collective-permute-done | bytes 65568 | tf_op jit(solution)/shard_map/ppermute | solution.py:290
  44.4 0.6 %collective-permute-done.5.refs_0_ = bf16[1,128,256]{2,1,0:T(8,128)(2,1)S(1)} collective-permute-done((bf16[1,128,256]{2,1,0:T(8,128)(2,1)S(1)}, bf16[1,128,256]{2,1,0:T(8,128)(2,1)S(1)}, u32[]{:S(2)}, u32[]{:S(2)}) %collective-permute-start.5) | collective-permute-done | bytes 65568 | tf_op jit(solution)/shard_map/ppermute | solution.py:290
  45.2 1.9 %give_back.2 = (bf16[64,16,4096]{2,1,0:T(8,128)(2,1)}, s32[1,64]{1,0:T(1,128)}) custom-call(s32[1]{0:T(128)} %bitcast.where, s32[64]{0:T(128)S(1)} %bitcast.14, bf16[2,128,256]{2,1,0:T(8,128)(2,1)S(1)} %join.4.rest_0_, bf16[2,128,256]{2,1,0:T(8,128)(2,1)S(1)} %join.6.rest_1_, f32[264,128]{1,0:T(8,128)S(1)} %add.17.kept.rest_2_, ...), custom_call_target="tpu_custom_call" | custom-call | flops 67108864 | tf_op jit(solution)/shard_map/give_back/pallas_call | solution.py:268
  47.1 3.2 %give_back.3 = bf16[64,16,4096]{2,1,0:T(8,128)(2,1)} custom-call(s32[1]{0:T(128)} %bitcast.where, s32[64]{0:T(128)S(1)} %bitcast.16, bf16[3,128,256]{2,1,0:T(8,128)(2,1)S(1)} %join.5.rest_0_, bf16[3,128,256]{2,1,0:T(8,128)(2,1)S(1)} %collective-permute-done.8.rest_1_, bf16[3,128,256]{2,1,0:T(8,128)(2,1)S(1)} %join.7.rest_2_, ...), custom_call_target="tpu_custom_call", output_to_operand_aliasing={{}: (6, {})} | custom-call | flops 67108864 | tf_op jit(solution)/shard_map/give_back/pallas_call | solution.py:268
  (32 shorter events, 2.1 us)
Async XLA Ops:
  3.3 41.9 %copy-start = (s32[64,1]{0,1:T(1,128)S(1)}, s32[64,1]{0,1:T(1,128)}, u32[]{:S(2)}) copy-start(s32[64,1]{0,1:T(1,128)} %param.3) | copy-start | bytes 772
  3.3 3.3 %collective-permute-start.9 = (f32[1032,128]{1,0:T(8,128)S(1)}, f32[1032,128]{1,0:T(8,128)S(1)}, u32[]{:S(2)}, u32[]{:S(2)}) collective-permute-start(f32[1032,128]{1,0:T(8,128)S(1)} %get-tuple-element.23), channel_id=1, source_target_pairs={{0,1},{1,0},{2,3},{3,2},{4,5},{5,4},{6,7},{7,6},{8,9},{9,8},{10,11... | collective-permute-start | bytes 1585160 | tf_op jit(solution)/shard_map/ppermute | solution.py:290
  6.4 2.8 %collective-permute-start = (f32[1032,128]{1,0:T(8,128)S(1)}, f32[1032,128]{1,0:T(8,128)S(1)}, u32[]{:S(2)}, u32[]{:S(2)}) collective-permute-start(f32[1032,128]{1,0:T(8,128)S(1)} %get-tuple-element.17), channel_id=1, source_target_pairs={{0,1},{1,0},{2,3},{3,2},{4,5},{5,4},{6,7},{7,6},{8,9},{9,8},{10,11... | collective-permute-start | bytes 1585160 | tf_op jit(solution)/shard_map/ppermute | solution.py:290
  6.6 6.8 %collective-permute-start.10 = (f32[520,128]{1,0:T(8,128)S(1)}, f32[520,128]{1,0:T(8,128)S(1)}, u32[]{:S(2)}, u32[]{:S(2)}) collective-permute-start(f32[520,128]{1,0:T(8,128)S(1)} %get-tuple-element.25), channel_id=1, source_target_pairs={{0,3},{1,4},{2,7},{3,0},{4,1},{5,6},{6,5},{7,2},{8,13},{9,10},{10,... | collective-permute-start | bytes 798728 | tf_op jit(solution)/shard_map/ppermute | solution.py:290
  9.3 6.9 %collective-permute-start.1 = (f32[520,128]{1,0:T(8,128)S(1)}, f32[520,128]{1,0:T(8,128)S(1)}, u32[]{:S(2)}, u32[]{:S(2)}) collective-permute-start(f32[520,128]{1,0:T(8,128)S(1)} %get-tuple-element.19), channel_id=1, source_target_pairs={{0,3},{1,4},{2,7},{3,0},{4,1},{5,6},{6,5},{7,2},{8,13},{9,10},{10,... | collective-permute-start | bytes 798728 | tf_op jit(solution)/shard_map/ppermute | solution.py:290
  13.4 4.9 %collective-permute-start.11 = (f32[264,128]{1,0:T(8,128)S(1)}, f32[264,128]{1,0:T(8,128)S(1)}, u32[]{:S(2)}, u32[]{:S(2)}) collective-permute-start(f32[264,128]{1,0:T(8,128)S(1)} %get-tuple-element.27), channel_id=1, source_target_pairs={{0,5},{1,2},{2,1},{3,6},{4,7},{5,0},{6,3},{7,4},{8,11},{9,12},{10,... | collective-permute-start | bytes 405512 | tf_op jit(solution)/shard_map/ppermute | solution.py:290
  16.3 4.6 %collective-permute-start.2 = (f32[264,128]{1,0:T(8,128)S(1)}, f32[264,128]{1,0:T(8,128)S(1)}, u32[]{:S(2)}, u32[]{:S(2)}) collective-permute-start(f32[264,128]{1,0:T(8,128)S(1)} %get-tuple-element.21), channel_id=1, source_target_pairs={{0,5},{1,2},{2,1},{3,6},{4,7},{5,0},{6,3},{7,4},{8,11},{9,12},{10,... | collective-permute-start | bytes 405512 | tf_op jit(solution)/shard_map/ppermute | solution.py:290
  18.4 5.2 %collective-permute-start.12 = (f32[264,128]{1,0:T(8,128)S(1)}, f32[264,128]{1,0:T(8,128)S(1)}, u32[]{:S(2)}, u32[]{:S(2)}) collective-permute-start(f32[264,128]{1,0:T(8,128)S(1)} %add.18), channel_id=1, source_target_pairs={{0,9},{1,16},{2,19},{3,10},{4,21},{5,12},{6,15},{7,22},{8,25},{9,0... | collective-permute-start | bytes 405512 | tf_op jit(solution)/shard_map/ppermute | solution.py:290
  20.9 5.9 %collective-permute-start.3 = (f32[264,128]{1,0:T(8,128)S(1)}, f32[264,128]{1,0:T(8,128)S(1)}, u32[]{:S(2)}, u32[]{:S(2)}) collective-permute-start(f32[264,128]{1,0:T(8,128)S(1)} %add.16), channel_id=1, source_target_pairs={{0,9},{1,16},{2,19},{3,10},{4,21},{5,12},{6,15},{7,22},{8,25},{9,0... | collective-permute-start | bytes 405512 | tf_op jit(solution)/shard_map/ppermute | solution.py:290
  23.6 8.1 %collective-permute-start.13 = (f32[264,128]{1,0:T(8,128)S(1)}, f32[264,128]{1,0:T(8,128)S(1)}, u32[]{:S(2)}, u32[]{:S(2)}) collective-permute-start(f32[264,128]{1,0:T(8,128)S(1)} %add.19.kept), channel_id=1, source_target_pairs={{0,17},{1,8},{2,11},{3,18},{4,13},{5,20},{6,23},{7,14},{8,1},{9,24... | collective-permute-start | bytes 405512 | tf_op jit(solution)/shard_map/ppermute | solution.py:290
  26.9 8.1 %collective-permute-start.4 = (f32[264,128]{1,0:T(8,128)S(1)}, f32[264,128]{1,0:T(8,128)S(1)}, u32[]{:S(2)}, u32[]{:S(2)}) collective-permute-start(f32[264,128]{1,0:T(8,128)S(1)} %add.17.kept.rest_2_), channel_id=1, source_target_pairs={{0,17},{1,8},{2,11},{3,18},{4,13},{5,20},{6,23},{7,14},{8,1},{9,24... | collective-permute-start | bytes 405512 | tf_op jit(solution)/shard_map/ppermute | solution.py:290
  31.8 3.3 %collective-permute-start.15 = (bf16[1,128,256]{2,1,0:T(8,128)(2,1)S(1)}, bf16[1,128,256]{2,1,0:T(8,128)(2,1)S(1)}, u32[]{:S(2)}, u32[]{:S(2)}) collective-permute-start(bf16[1,128,256]{2,1,0:T(8,128)(2,1)S(1)} %bitcast.9), channel_id=1, source_target_pairs={{0,1},{1,0},{2,3},{3,2},{4,5},{5,4},{6,7},{7,6},{8,9},{9,8},{10,11... | collective-permute-start | bytes 196616 | tf_op jit(solution)/shard_map/ppermute | solution.py:290
  35.0 1.4 %collective-permute-start.6 = (bf16[1,128,256]{2,1,0:T(8,128)(2,1)S(1)}, bf16[1,128,256]{2,1,0:T(8,128)(2,1)S(1)}, u32[]{:S(2)}, u32[]{:S(2)}) collective-permute-start(bf16[1,128,256]{2,1,0:T(8,128)(2,1)S(1)} %bitcast.6), channel_id=1, source_target_pairs={{0,1},{1,0},{2,3},{3,2},{4,5},{5,4},{6,7},{7,6},{8,9},{9,8},{10,11... | collective-permute-start | bytes 196616 | tf_op jit(solution)/shard_map/ppermute | solution.py:290
  35.1 9.2 %collective-permute-start.16 = (bf16[2,128,256]{2,1,0:T(8,128)(2,1)S(1)}, bf16[2,128,256]{2,1,0:T(8,128)(2,1)S(1)}, u32[]{:S(2)}, u32[]{:S(2)}) collective-permute-start(bf16[2,128,256]{2,1,0:T(8,128)(2,1)S(1)} %join.6.rest_1_), channel_id=1, source_target_pairs={{0,3},{1,4},{2,7},{3,0},{4,1},{5,6},{6,5},{7,2},{8,13},{9,10},{10,... | collective-permute-start | bytes 393224 | tf_op jit(solution)/shard_map/ppermute | solution.py:290
  36.4 8.6 %collective-permute-start.7 = (bf16[2,128,256]{2,1,0:T(8,128)(2,1)S(1)}, bf16[2,128,256]{2,1,0:T(8,128)(2,1)S(1)}, u32[]{:S(2)}, u32[]{:S(2)}) collective-permute-start(bf16[2,128,256]{2,1,0:T(8,128)(2,1)S(1)} %join.4.rest_0_), channel_id=1, source_target_pairs={{0,3},{1,4},{2,7},{3,0},{4,1},{5,6},{6,5},{7,2},{8,13},{9,10},{10,... | collective-permute-start | bytes 393224 | tf_op jit(solution)/shard_map/ppermute | solution.py:290
  37.6 6.7 %collective-permute-start.14 = (bf16[1,128,256]{2,1,0:T(8,128)(2,1)S(1)}, bf16[1,128,256]{2,1,0:T(8,128)(2,1)S(1)}, u32[]{:S(2)}, u32[]{:S(2)}) collective-permute-start(bf16[1,128,256]{2,1,0:T(8,128)(2,1)S(1)} %bitcast.11), channel_id=1, source_target_pairs={{0,6},{1,7},{2,4},{3,5},{4,2},{5,3},{6,0},{7,1},{8,14},{9,15},{10,... | collective-permute-start | bytes 196616 | tf_op jit(solution)/shard_map/ppermute | solution.py:290
  39.3 5.8 %collective-permute-start.5 = (bf16[1,128,256]{2,1,0:T(8,128)(2,1)S(1)}, bf16[1,128,256]{2,1,0:T(8,128)(2,1)S(1)}, u32[]{:S(2)}, u32[]{:S(2)}) collective-permute-start(bf16[1,128,256]{2,1,0:T(8,128)(2,1)S(1)} %bitcast.8), channel_id=1, source_target_pairs={{0,6},{1,7},{2,4},{3,5},{4,2},{5,3},{6,0},{7,1},{8,14},{9,15},{10,... | collective-permute-start | bytes 196616 | tf_op jit(solution)/shard_map/ppermute | solution.py:290
  44.3 2.7 %collective-permute-start.17 = (bf16[3,128,256]{2,1,0:T(8,128)(2,1)S(1)}, bf16[3,128,256]{2,1,0:T(8,128)(2,1)S(1)}, u32[]{:S(2)}, u32[]{:S(2)}) collective-permute-start(bf16[3,128,256]{2,1,0:T(8,128)(2,1)S(1)} %join.7.rest_2_), channel_id=1, source_target_pairs={{0,1},{1,0},{2,3},{3,2},{4,5},{5,4},{6,7},{7,6},{8,9},{9,8},{10,11... | collective-permute-start | bytes 589832 | tf_op jit(solution)/shard_map/ppermute | solution.py:290
  45.1 2.0 %collective-permute-start.8 = (bf16[3,128,256]{2,1,0:T(8,128)(2,1)S(1)}, bf16[3,128,256]{2,1,0:T(8,128)(2,1)S(1)}, u32[]{:S(2)}, u32[]{:S(2)}) collective-permute-start(bf16[3,128,256]{2,1,0:T(8,128)(2,1)S(1)} %join.5.rest_0_), channel_id=1, source_target_pairs={{0,1},{1,0},{2,3},{3,2},{4,5},{5,4},{6,7},{7,6},{8,9},{9,8},{10,11... | collective-permute-start | bytes 589832 | tf_op jit(solution)/shard_map/ppermute | solution.py:290

commit v6 on v5

--- a/solution.py
+++ b/solution.py
@@ -203,21 +203,24 @@
     return jnp.sum(jnp.where(hits, before + local, 0.0), axis=0, keepdims=True).astype(jnp.int32)
 
 
-def own_places(me):
-    return [(quarter_of(me), [
-        (chain, other, chain, role_of(me) ^ other) for chain in range(CHAINS) for other in range(2)])]
-
-
-def rest_places(me):
+def early_places(me):
     role = role_of(me)
-    kinds = [
-        (me ^ 6, [(0, 0, role), (1, 0, 1 - role)]),
-        (me ^ (2 << role), [(0, 1, role), (0, 2, 1 - role)]),
-        (me ^ (4 >> role), [(1, 1, 1 - role), (1, 2, role)]),
+    return [
+        (quarter_of(me), [(chain, other, chain, role ^ other) for chain in range(CHAINS) for other in range(2)]),
+        (quarter_of(me ^ (2 << role)), [(CHAINS, 1, 0, role), (CHAINS, 2, 0, 1 - role)]),
+        (quarter_of(me ^ 6), [(CHAINS, 0, 0, role)]),
     ]
-    return [(quarter_of(chip), [
-        (2 * chain + array, slot, chain, half) for chain in range(CHAINS) for array, slot, half in pieces])
-        for chip, pieces in kinds]
+
+
+def late_places(me):
+    role = role_of(me)
+    return [
+        (quarter_of(me ^ (4 >> role)), [
+            (2 * chain, slot, chain, role ^ other) for chain in range(CHAINS) for slot, other in ((1, 1), (2, 0))]),
+        (quarter_of(me ^ (2 << role)), [(1, 1, 1, role), (1, 2, 1, 1 - role)]),
+        (quarter_of(me ^ 6), [(1, 0, 1, role), (2, 0, 1, 1 - role)]),
+        (quarter_of(me ^ 6), [(0, 0, 0, 1 - role)]),
+    ]
 
 
 def give_back_kernel(places, arrays, tail, where, labels, *rest):
@@ -232,13 +235,13 @@
     ends, offset = [], 0
     for at, (quarter, pieces) in enumerate(places(me)):
         size = len(pieces) * columns
-        first = pieces[0][2]
+        first = pieces[0][2] * 2 + (pieces[0][3] if len(pieces) == 1 else 0)
         for array, slot, chain, half in pieces:
-            to = offset + ((chain - first) * 2 + half) * columns
+            to = offset + (chain * 2 + half - first) * columns
             to = pl.ds(pl.multiple_of(to, LANES), columns)
             for cluster in range(CLUSTERS):
                 laid[cluster, :, to] = models[array][slot, cluster * blocks:(cluster + 1) * blocks, :]
-        across = pl.ds(pl.multiple_of((quarter * CHAINS + first) * 2 * columns, LANES), size)
+        across = pl.ds(pl.multiple_of((quarter * CHAINS * 2 + first) * columns, LANES), size)
         for client in range(clients):
             pltpu.make_async_copy(
                 laid.at[labels[client], :, offset:offset + size], returned.at[client, :, across], sem.at[at]).start()
@@ -256,7 +259,7 @@
 def give_back(places, where, labels, models, shape, returned=None, ranked=None):
     columns = models[0].shape[2]
     slots = sum(array.shape[0] for array in models)
-    scratch = [pltpu.VMEM((CLUSTERS, shape[1], slots * columns), jnp.bfloat16), pltpu.SemaphoreType.DMA((3,))]
+    scratch = [pltpu.VMEM((CLUSTERS, shape[1], slots * columns), jnp.bfloat16), pltpu.SemaphoreType.DMA((4,))]
     out = [jax.ShapeDtypeStruct(shape, jnp.bfloat16)]
     if ranked is None:
         tail, more, more_specs, aliases = 0, (returned,), [ANY], {2 + len(models): 0}
@@ -320,8 +323,8 @@
         rests.append([taken, send(taken, cores)])
 
     give = functools.partial(give_back, where=where, labels=labels_list, shape=deltas.shape)
-    returned, rank = give(own_places, models=pairs, ranked=(tail, *kept[0], labels_row))
-    returned, = give(rest_places, models=rests[0] + rests[1], returned=returned)
+    returned, rank = give(early_places, models=pairs + rests[0][:1], ranked=(tail, *kept[0], labels_row))
+    returned, = give(late_places, models=rests[0][1:] + rests[1], returned=returned)
     return returned, rank.reshape(clients)
 
 

time: 50.5 us -> 50.7 us (level)
  transfers between devices with their start and end apart: 18 -> 18, of which waited for: 9 -> 9; matrix products, arithmetic and copies ran while one was open for 0% -> 0% of each run, Pallas kernels for 10% -> 11%
where the time goes in v6:
time: 50.7 us; the launch traced here: 50.4 us
  starting transfers between devices  24.8 us (49%)
  waiting for transfers between devices  13.8 us (27%)
  Pallas kernels  10.9 us (21%)
  between operations  0.78 us (2%)
    ppermute x18, starting transfers between devices, send(): return lax.ppermute(value, AXES, [(i, i ^ flip(i)) for i in range(devices)])  24.8 us
    ppermute x18, waiting for transfers between devices, send(): return lax.ppermute(value, AXES, [(i, i ^ flip(i)) for i in range(devices)])  13.8 us
    pallas_call x2, Pallas kernels, give_back(): pl.pallas_call(functools.partial(give_back_kernel, places, len(models), t...  5.24 us
    pallas_call x2, Pallas kernels, local_sums(): pl.pallas_call(functools.partial(local_sums_kernel, devices, chain), out_...  5.23 us
  transfers between devices with their start and end apart: 18, of which 9 were waited for; matrix products, arithmetic and copies ran while one was open for 0% of the time, Pallas kernels for 11%

profile of v6, /device:TPU:0, one launch (start us, length us, event | category | flops | bytes accessed | tf_op | source)
XLA Modules:
  0.0 50.4 jit_solution(1919572710731486865)
XLA Ops:
  0.6 2.6 %local_sums.3 = (f32[1032,128]{1,0:T(8,128)S(1)}, f32[1032,128]{1,0:T(8,128)S(1)}) custom-call(s32[1]{0:T(128)} %bitcast.where, bf16[64,16,4096]{2,1,0:T(8,128)(2,1)} %deltas.3, s32[1,64]{1,0:T(1,128)} %bitcast.12), custom_call_target="tpu_custom_call" | custom-call | tf_op jit(solution)/shard_map/local_sums/pallas_call | solution.py:105
  3.8 2.6 %local_sums.2 = (f32[1032,128]{1,0:T(8,128)S(1)}, f32[1032,128]{1,0:T(8,128)S(1)}) custom-call(s32[1]{0:T(128)} %bitcast.where, bf16[64,16,4096]{2,1,0:T(8,128)(2,1)} %deltas.3, s32[1,64]{1,0:T(1,128)} %bitcast.13), custom_call_target="tpu_custom_call" | custom-call | tf_op jit(solution)/shard_map/local_sums/pallas_call | solution.py:105
  6.6 2.7 %collective-permute-start.10 = (f32[520,128]{1,0:T(8,128)S(1)}, f32[520,128]{1,0:T(8,128)S(1)}, u32[]{:S(2)}, u32[]{:S(2)}) collective-permute-start(f32[520,128]{1,0:T(8,128)S(1)} %get-tuple-element.25), channel_id=1, source_target_pairs={{0,3},{1,4},{2,7},{3,0},{4,1},{5,6},{6,5},{7,2},{8,13},{9,10},{10,... | collective-permute-start | bytes 798728 | tf_op jit(solution)/shard_map/ppermute | solution.py:293
  9.3 1.8 %collective-permute-start.1 = (f32[520,128]{1,0:T(8,128)S(1)}, f32[520,128]{1,0:T(8,128)S(1)}, u32[]{:S(2)}, u32[]{:S(2)}) collective-permute-start(f32[520,128]{1,0:T(8,128)S(1)} %get-tuple-element.19), channel_id=1, source_target_pairs={{0,3},{1,4},{2,7},{3,0},{4,1},{5,6},{6,5},{7,2},{8,13},{9,10},{10,... | collective-permute-start | bytes 798728 | tf_op jit(solution)/shard_map/ppermute | solution.py:293
  11.1 2.2 %collective-permute-done.10.arrived = f32[520,128]{1,0:T(8,128)S(1)} collective-permute-done((f32[520,128]{1,0:T(8,128)S(1)}, f32[520,128]{1,0:T(8,128)S(1)}, u32[]{:S(2)}, u32[]{:S(2)}) %collective-permute-start.10) | collective-permute-done | bytes 266272 | tf_op jit(solution)/shard_map/ppermute | solution.py:293
  13.4 2.1 %collective-permute-start.11 = (f32[264,128]{1,0:T(8,128)S(1)}, f32[264,128]{1,0:T(8,128)S(1)}, u32[]{:S(2)}, u32[]{:S(2)}) collective-permute-start(f32[264,128]{1,0:T(8,128)S(1)} %get-tuple-element.27), channel_id=1, source_target_pairs={{0,5},{1,2},{2,1},{3,6},{4,7},{5,0},{6,3},{7,4},{8,11},{9,12},{10,... | collective-permute-start | bytes 405512 | tf_op jit(solution)/shard_map/ppermute | solution.py:293
  15.5 0.7 %collective-permute-done.1.arrived = f32[520,128]{1,0:T(8,128)S(1)} collective-permute-done((f32[520,128]{1,0:T(8,128)S(1)}, f32[520,128]{1,0:T(8,128)S(1)}, u32[]{:S(2)}, u32[]{:S(2)}) %collective-permute-start.1) | collective-permute-done | bytes 266272 | tf_op jit(solution)/shard_map/ppermute | solution.py:293
  16.3 1.9 %collective-permute-start.2 = (f32[264,128]{1,0:T(8,128)S(1)}, f32[264,128]{1,0:T(8,128)S(1)}, u32[]{:S(2)}, u32[]{:S(2)}) collective-permute-start(f32[264,128]{1,0:T(8,128)S(1)} %get-tuple-element.21), channel_id=1, source_target_pairs={{0,5},{1,2},{2,1},{3,6},{4,7},{5,0},{6,3},{7,4},{8,11},{9,12},{10,... | collective-permute-start | bytes 405512 | tf_op jit(solution)/shard_map/ppermute | solution.py:293
  18.4 1.7 %collective-permute-start.12 = (f32[264,128]{1,0:T(8,128)S(1)}, f32[264,128]{1,0:T(8,128)S(1)}, u32[]{:S(2)}, u32[]{:S(2)}) collective-permute-start(f32[264,128]{1,0:T(8,128)S(1)} %add.18), channel_id=1, source_target_pairs={{0,9},{1,16},{2,19},{3,10},{4,21},{5,12},{6,15},{7,22},{8,25},{9,0... | collective-permute-start | bytes 405512 | tf_op jit(solution)/shard_map/ppermute | solution.py:293
  20.1 0.8 %collective-permute-done.2 = f32[264,128]{1,0:T(8,128)S(1)} collective-permute-done((f32[264,128]{1,0:T(8,128)S(1)}, f32[264,128]{1,0:T(8,128)S(1)}, u32[]{:S(2)}, u32[]{:S(2)}) %collective-permute-start.2) | collective-permute-done | bytes 135200 | tf_op jit(solution)/shard_map/ppermute | solution.py:293
  20.9 1.9 %collective-permute-start.3 = (f32[264,128]{1,0:T(8,128)S(1)}, f32[264,128]{1,0:T(8,128)S(1)}, u32[]{:S(2)}, u32[]{:S(2)}) collective-permute-start(f32[264,128]{1,0:T(8,128)S(1)} %add.16), channel_id=1, source_target_pairs={{0,9},{1,16},{2,19},{3,10},{4,21},{5,12},{6,15},{7,22},{8,25},{9,0... | collective-permute-start | bytes 405512 | tf_op jit(solution)/shard_map/ppermute | solution.py:293
  22.8 0.8 %collective-permute-done.12 = f32[264,128]{1,0:T(8,128)S(1)} collective-permute-done((f32[264,128]{1,0:T(8,128)S(1)}, f32[264,128]{1,0:T(8,128)S(1)}, u32[]{:S(2)}, u32[]{:S(2)}) %collective-permute-start.12) | collective-permute-done | bytes 135200 | tf_op jit(solution)/shard_map/ppermute | solution.py:293
  23.6 3.2 %collective-permute-start.13 = (f32[264,128]{1,0:T(8,128)S(1)}, f32[264,128]{1,0:T(8,128)S(1)}, u32[]{:S(2)}, u32[]{:S(2)}) collective-permute-start(f32[264,128]{1,0:T(8,128)S(1)} %add.19.kept), channel_id=1, source_target_pairs={{0,17},{1,8},{2,11},{3,18},{4,13},{5,20},{6,23},{7,14},{8,1},{9,24... | collective-permute-start | bytes 405512 | tf_op jit(solution)/shard_map/ppermute | solution.py:293
  26.9 2.8 %collective-permute-start.4 = (f32[264,128]{1,0:T(8,128)S(1)}, f32[264,128]{1,0:T(8,128)S(1)}, u32[]{:S(2)}, u32[]{:S(2)}) collective-permute-start(f32[264,128]{1,0:T(8,128)S(1)} %add.17.kept.rest_3_), channel_id=1, source_target_pairs={{0,17},{1,8},{2,11},{3,18},{4,13},{5,20},{6,23},{7,14},{8,1},{9,24... | collective-permute-start | bytes 405512 | tf_op jit(solution)/shard_map/ppermute | solution.py:293
  29.7 2.0 %collective-permute-done.13.arrived = f32[264,128]{1,0:T(8,128)S(1)} collective-permute-done((f32[264,128]{1,0:T(8,128)S(1)}, f32[264,128]{1,0:T(8,128)S(1)}, u32[]{:S(2)}, u32[]{:S(2)}) %collective-permute-start.13) | collective-permute-done | bytes 135200 | tf_op jit(solution)/shard_map/ppermute | solution.py:293
  32.3 2.6 %collective-permute-done.4.arrived.rest_4_ = f32[264,128]{1,0:T(8,128)S(1)} collective-permute-done((f32[264,128]{1,0:T(8,128)S(1)}, f32[264,128]{1,0:T(8,128)S(1)}, u32[]{:S(2)}, u32[]{:S(2)}) %collective-permute-start.4) | collective-permute-done | bytes 135200 | tf_op jit(solution)/shard_map/ppermute | solution.py:293
  35.1 1.3 %collective-permute-start.16 = (bf16[2,128,256]{2,1,0:T(8,128)(2,1)S(1)}, bf16[2,128,256]{2,1,0:T(8,128)(2,1)S(1)}, u32[]{:S(2)}, u32[]{:S(2)}) collective-permute-start(bf16[2,128,256]{2,1,0:T(8,128)(2,1)S(1)} %join.6.rest_1_), channel_id=1, source_target_pairs={{0,3},{1,4},{2,7},{3,0},{4,1},{5,6},{6,5},{7,2},{8,13},{9,10},{10,... | collective-permute-start | bytes 393224 | tf_op jit(solution)/shard_map/ppermute | solution.py:293
  36.4 1.2 %collective-permute-start.7 = (bf16[2,128,256]{2,1,0:T(8,128)(2,1)S(1)}, bf16[2,128,256]{2,1,0:T(8,128)(2,1)S(1)}, u32[]{:S(2)}, u32[]{:S(2)}) collective-permute-start(bf16[2,128,256]{2,1,0:T(8,128)(2,1)S(1)} %join.4.rest_0_), channel_id=1, source_target_pairs={{0,3},{1,4},{2,7},{3,0},{4,1},{5,6},{6,5},{7,2},{8,13},{9,10},{10,... | collective-permute-start | bytes 393224 | tf_op jit(solution)/shard_map/ppermute | solution.py:293
  37.6 1.6 %collective-permute-start.14 = (bf16[1,128,256]{2,1,0:T(8,128)(2,1)S(1)}, bf16[1,128,256]{2,1,0:T(8,128)(2,1)S(1)}, u32[]{:S(2)}, u32[]{:S(2)}) collective-permute-start(bf16[1,128,256]{2,1,0:T(8,128)(2,1)S(1)} %bitcast.11), channel_id=1, source_target_pairs={{0,6},{1,7},{2,4},{3,5},{4,2},{5,3},{6,0},{7,1},{8,14},{9,15},{10,... | collective-permute-start | bytes 196616 | tf_op jit(solution)/shard_map/ppermute | solution.py:293
  39.3 1.3 %collective-permute-start.5 = (bf16[1,128,256]{2,1,0:T(8,128)(2,1)S(1)}, bf16[1,128,256]{2,1,0:T(8,128)(2,1)S(1)}, u32[]{:S(2)}, u32[]{:S(2)}) collective-permute-start(bf16[1,128,256]{2,1,0:T(8,128)(2,1)S(1)} %bitcast.8), channel_id=1, source_target_pairs={{0,6},{1,7},{2,4},{3,5},{4,2},{5,3},{6,0},{7,1},{8,14},{9,15},{10,... | collective-permute-start | bytes 196616 | tf_op jit(solution)/shard_map/ppermute | solution.py:293
  40.6 3.8 %collective-permute-done.14.refs_0_ = bf16[1,128,256]{2,1,0:T(8,128)(2,1)S(1)} collective-permute-done((bf16[1,128,256]{2,1,0:T(8,128)(2,1)S(1)}, bf16[1,128,256]{2,1,0:T(8,128)(2,1)S(1)}, u32[]{:S(2)}, u32[]{:S(2)}) %collective-permute-start.14) | collective-permute-done | bytes 65568 | tf_op jit(solution)/shard_map/ppermute | solution.py:293
  44.4 0.6 %collective-permute-done.5.refs_0_ = bf16[1,128,256]{2,1,0:T(8,128)(2,1)S(1)} collective-permute-done((bf16[1,128,256]{2,1,0:T(8,128)(2,1)S(1)}, bf16[1,128,256]{2,1,0:T(8,128)(2,1)S(1)}, u32[]{:S(2)}, u32[]{:S(2)}) %collective-permute-start.5) | collective-permute-done | bytes 65568 | tf_op jit(solution)/shard_map/ppermute | solution.py:293
  45.2 2.5 %give_back.2 = (bf16[64,16,4096]{2,1,0:T(8,128)(2,1)}, s32[1,64]{1,0:T(1,128)}) custom-call(s32[1]{0:T(128)} %bitcast.where, s32[64]{0:T(128)S(1)} %bitcast.14, bf16[2,128,256]{2,1,0:T(8,128)(2,1)S(1)} %join.4.rest_0_, bf16[2,128,256]{2,1,0:T(8,128)(2,1)S(1)} %join.6.rest_1_, bf16[3,128,256]{2,1,0:T(8,128)(2,1)S(1)} %join.5.rest_2_, ...), custom_call_target="tpu_custom_call" | custom-call | flops 67108864 | tf_op jit(solution)/shard_map/give_back/pallas_call | solution.py:271
  47.6 2.8 %give_back.3 = bf16[64,16,4096]{2,1,0:T(8,128)(2,1)} custom-call(s32[1]{0:T(128)} %bitcast.where, s32[64]{0:T(128)S(1)} %bitcast.16, bf16[3,128,256]{2,1,0:T(8,128)(2,1)S(1)} %collective-permute-done.8.rest_0_, bf16[3,128,256]{2,1,0:T(8,128)(2,1)S(1)} %join.7.rest_1_, ...), custom_call_target="tpu_custom_call", output_to_operand_aliasing={{}: (5, {})} | custom-call | flops 67108864 | tf_op jit(solution)/shard_map/give_back/pallas_call | solution.py:271
  (32 shorter events, 2.1 us)
Async XLA Ops:
  3.3 41.9 %copy-start = (s32[64,1]{0,1:T(1,128)S(1)}, s32[64,1]{0,1:T(1,128)}, u32[]{:S(2)}) copy-start(s32[64,1]{0,1:T(1,128)} %param.3) | copy-start | bytes 772
  3.3 3.3 %collective-permute-start.9 = (f32[1032,128]{1,0:T(8,128)S(1)}, f32[1032,128]{1,0:T(8,128)S(1)}, u32[]{:S(2)}, u32[]{:S(2)}) collective-permute-start(f32[1032,128]{1,0:T(8,128)S(1)} %get-tuple-element.23), channel_id=1, source_target_pairs={{0,1},{1,0},{2,3},{3,2},{4,5},{5,4},{6,7},{7,6},{8,9},{9,8},{10,11... | collective-permute-start | bytes 1585160 | tf_op jit(solution)/shard_map/ppermute | solution.py:293
  6.4 2.8 %collective-permute-start = (f32[1032,128]{1,0:T(8,128)S(1)}, f32[1032,128]{1,0:T(8,128)S(1)}, u32[]{:S(2)}, u32[]{:S(2)}) collective-permute-start(f32[1032,128]{1,0:T(8,128)S(1)} %get-tuple-element.17), channel_id=1, source_target_pairs={{0,1},{1,0},{2,3},{3,2},{4,5},{5,4},{6,7},{7,6},{8,9},{9,8},{10,11... | collective-permute-start | bytes 1585160 | tf_op jit(solution)/shard_map/ppermute | solution.py:293
  6.6 6.8 %collective-permute-start.10 = (f32[520,128]{1,0:T(8,128)S(1)}, f32[520,128]{1,0:T(8,128)S(1)}, u32[]{:S(2)}, u32[]{:S(2)}) collective-permute-start(f32[520,128]{1,0:T(8,128)S(1)} %get-tuple-element.25), channel_id=1, source_target_pairs={{0,3},{1,4},{2,7},{3,0},{4,1},{5,6},{6,5},{7,2},{8,13},{9,10},{10,... | collective-permute-start | bytes 798728 | tf_op jit(solution)/shard_map/ppermute | solution.py:293
  9.3 6.9 %collective-permute-start.1 = (f32[520,128]{1,0:T(8,128)S(1)}, f32[520,128]{1,0:T(8,128)S(1)}, u32[]{:S(2)}, u32[]{:S(2)}) collective-permute-start(f32[520,128]{1,0:T(8,128)S(1)} %get-tuple-element.19), channel_id=1, source_target_pairs={{0,3},{1,4},{2,7},{3,0},{4,1},{5,6},{6,5},{7,2},{8,13},{9,10},{10,... | collective-permute-start | bytes 798728 | tf_op jit(solution)/shard_map/ppermute | solution.py:293
  13.4 4.9 %collective-permute-start.11 = (f32[264,128]{1,0:T(8,128)S(1)}, f32[264,128]{1,0:T(8,128)S(1)}, u32[]{:S(2)}, u32[]{:S(2)}) collective-permute-start(f32[264,128]{1,0:T(8,128)S(1)} %get-tuple-element.27), channel_id=1, source_target_pairs={{0,5},{1,2},{2,1},{3,6},{4,7},{5,0},{6,3},{7,4},{8,11},{9,12},{10,... | collective-permute-start | bytes 405512 | tf_op jit(solution)/shard_map/ppermute | solution.py:293
  16.3 4.6 %collective-permute-start.2 = (f32[264,128]{1,0:T(8,128)S(1)}, f32[264,128]{1,0:T(8,128)S(1)}, u32[]{:S(2)}, u32[]{:S(2)}) collective-permute-start(f32[264,128]{1,0:T(8,128)S(1)} %get-tuple-element.21), channel_id=1, source_target_pairs={{0,5},{1,2},{2,1},{3,6},{4,7},{5,0},{6,3},{7,4},{8,11},{9,12},{10,... | collective-permute-start | bytes 405512 | tf_op jit(solution)/shard_map/ppermute | solution.py:293
  18.4 5.2 %collective-permute-start.12 = (f32[264,128]{1,0:T(8,128)S(1)}, f32[264,128]{1,0:T(8,128)S(1)}, u32[]{:S(2)}, u32[]{:S(2)}) collective-permute-start(f32[264,128]{1,0:T(8,128)S(1)} %add.18), channel_id=1, source_target_pairs={{0,9},{1,16},{2,19},{3,10},{4,21},{5,12},{6,15},{7,22},{8,25},{9,0... | collective-permute-start | bytes 405512 | tf_op jit(solution)/shard_map/ppermute | solution.py:293
  20.9 5.9 %collective-permute-start.3 = (f32[264,128]{1,0:T(8,128)S(1)}, f32[264,128]{1,0:T(8,128)S(1)}, u32[]{:S(2)}, u32[]{:S(2)}) collective-permute-start(f32[264,128]{1,0:T(8,128)S(1)} %add.16), channel_id=1, source_target_pairs={{0,9},{1,16},{2,19},{3,10},{4,21},{5,12},{6,15},{7,22},{8,25},{9,0... | collective-permute-start | bytes 405512 | tf_op jit(solution)/shard_map/ppermute | solution.py:293
  23.6 8.1 %collective-permute-start.13 = (f32[264,128]{1,0:T(8,128)S(1)}, f32[264,128]{1,0:T(8,128)S(1)}, u32[]{:S(2)}, u32[]{:S(2)}) collective-permute-start(f32[264,128]{1,0:T(8,128)S(1)} %add.19.kept), channel_id=1, source_target_pairs={{0,17},{1,8},{2,11},{3,18},{4,13},{5,20},{6,23},{7,14},{8,1},{9,24... | collective-permute-start | bytes 405512 | tf_op jit(solution)/shard_map/ppermute | solution.py:293
  26.9 8.1 %collective-permute-start.4 = (f32[264,128]{1,0:T(8,128)S(1)}, f32[264,128]{1,0:T(8,128)S(1)}, u32[]{:S(2)}, u32[]{:S(2)}) collective-permute-start(f32[264,128]{1,0:T(8,128)S(1)} %add.17.kept.rest_3_), channel_id=1, source_target_pairs={{0,17},{1,8},{2,11},{3,18},{4,13},{5,20},{6,23},{7,14},{8,1},{9,24... | collective-permute-start | bytes 405512 | tf_op jit(solution)/shard_map/ppermute | solution.py:293
  31.8 3.3 %collective-permute-start.15 = (bf16[1,128,256]{2,1,0:T(8,128)(2,1)S(1)}, bf16[1,128,256]{2,1,0:T(8,128)(2,1)S(1)}, u32[]{:S(2)}, u32[]{:S(2)}) collective-permute-start(bf16[1,128,256]{2,1,0:T(8,128)(2,1)S(1)} %bitcast.9), channel_id=1, source_target_pairs={{0,1},{1,0},{2,3},{3,2},{4,5},{5,4},{6,7},{7,6},{8,9},{9,8},{10,11... | collective-permute-start | bytes 196616 | tf_op jit(solution)/shard_map/ppermute | solution.py:293
  35.0 1.4 %collective-permute-start.6 = (bf16[1,128,256]{2,1,0:T(8,128)(2,1)S(1)}, bf16[1,128,256]{2,1,0:T(8,128)(2,1)S(1)}, u32[]{:S(2)}, u32[]{:S(2)}) collective-permute-start(bf16[1,128,256]{2,1,0:T(8,128)(2,1)S(1)} %bitcast.6), channel_id=1, source_target_pairs={{0,1},{1,0},{2,3},{3,2},{4,5},{5,4},{6,7},{7,6},{8,9},{9,8},{10,11... | collective-permute-start | bytes 196616 | tf_op jit(solution)/shard_map/ppermute | solution.py:293
  35.1 9.2 %collective-permute-start.16 = (bf16[2,128,256]{2,1,0:T(8,128)(2,1)S(1)}, bf16[2,128,256]{2,1,0:T(8,128)(2,1)S(1)}, u32[]{:S(2)}, u32[]{:S(2)}) collective-permute-start(bf16[2,128,256]{2,1,0:T(8,128)(2,1)S(1)} %join.6.rest_1_), channel_id=1, source_target_pairs={{0,3},{1,4},{2,7},{3,0},{4,1},{5,6},{6,5},{7,2},{8,13},{9,10},{10,... | collective-permute-start | bytes 393224 | tf_op jit(solution)/shard_map/ppermute | solution.py:293
  36.4 8.6 %collective-permute-start.7 = (bf16[2,128,256]{2,1,0:T(8,128)(2,1)S(1)}, bf16[2,128,256]{2,1,0:T(8,128)(2,1)S(1)}, u32[]{:S(2)}, u32[]{:S(2)}) collective-permute-start(bf16[2,128,256]{2,1,0:T(8,128)(2,1)S(1)} %join.4.rest_0_), channel_id=1, source_target_pairs={{0,3},{1,4},{2,7},{3,0},{4,1},{5,6},{6,5},{7,2},{8,13},{9,10},{10,... | collective-permute-start | bytes 393224 | tf_op jit(solution)/shard_map/ppermute | solution.py:293
  37.6 6.7 %collective-permute-start.14 = (bf16[1,128,256]{2,1,0:T(8,128)(2,1)S(1)}, bf16[1,128,256]{2,1,0:T(8,128)(2,1)S(1)}, u32[]{:S(2)}, u32[]{:S(2)}) collective-permute-start(bf16[1,128,256]{2,1,0:T(8,128)(2,1)S(1)} %bitcast.11), channel_id=1, source_target_pairs={{0,6},{1,7},{2,4},{3,5},{4,2},{5,3},{6,0},{7,1},{8,14},{9,15},{10,... | collective-permute-start | bytes 196616 | tf_op jit(solution)/shard_map/ppermute | solution.py:293
  39.3 5.8 %collective-permute-start.5 = (bf16[1,128,256]{2,1,0:T(8,128)(2,1)S(1)}, bf16[1,128,256]{2,1,0:T(8,128)(2,1)S(1)}, u32[]{:S(2)}, u32[]{:S(2)}) collective-permute-start(bf16[1,128,256]{2,1,0:T(8,128)(2,1)S(1)} %bitcast.8), channel_id=1, source_target_pairs={{0,6},{1,7},{2,4},{3,5},{4,2},{5,3},{6,0},{7,1},{8,14},{9,15},{10,... | collective-permute-start | bytes 196616 | tf_op jit(solution)/shard_map/ppermute | solution.py:293
  44.3 3.3 %collective-permute-start.17 = (bf16[3,128,256]{2,1,0:T(8,128)(2,1)S(1)}, bf16[3,128,256]{2,1,0:T(8,128)(2,1)S(1)}, u32[]{:S(2)}, u32[]{:S(2)}) collective-permute-start(bf16[3,128,256]{2,1,0:T(8,128)(2,1)S(1)} %join.7.rest_1_), channel_id=1, source_target_pairs={{0,1},{1,0},{2,3},{3,2},{4,5},{5,4},{6,7},{7,6},{8,9},{9,8},{10,11... | collective-permute-start | bytes 589832 | tf_op jit(solution)/shard_map/ppermute | solution.py:293
  45.1 2.6 %collective-permute-start.8 = (bf16[3,128,256]{2,1,0:T(8,128)(2,1)S(1)}, bf16[3,128,256]{2,1,0:T(8,128)(2,1)S(1)}, u32[]{:S(2)}, u32[]{:S(2)}) collective-permute-start(bf16[3,128,256]{2,1,0:T(8,128)(2,1)S(1)} %join.5.rest_2_), channel_id=1, source_target_pairs={{0,1},{1,0},{2,3},{3,2},{4,5},{5,4},{6,7},{7,6},{8,9},{9,8},{10,11... | collective-permute-start | bytes 589832 | tf_op jit(solution)/shard_map/ppermute | solution.py:293

commit v7 on v6

--- a/solution.py
+++ b/solution.py
@@ -46,7 +46,7 @@
     return (index >> 1) & 3
 
 
-def local_sums_kernel(devices, chain, where, deltas, labels_row, other, mine, held, labels_here, sems):
+def local_sums_kernel(tail, chain, where, deltas, labels_row, other, mine, held, labels_here, sems):
     clients, blocks, _ = deltas.shape
     me = where[0]
     role = role_of(me)
@@ -80,7 +80,6 @@
     hits = (labels == lax.broadcasted_iota(jnp.int32, (CLUSTERS, clients), 0)).astype(jnp.float32)
     counts = jnp.sum(hits, axis=1, keepdims=True)
     lane = lax.broadcasted_iota(jnp.int32, (CLUSTERS, LANES), 1)
-    tail = count_rows(devices)
     for tile in range(tail // CLUSTERS):
         table = jnp.where(lane + tile * LANES == me, counts, 0.0)
         at = other.shape[0] - tail + tile * CLUSTERS
@@ -97,13 +96,13 @@
             target[to:to + rows, :] = sums[:, block * LANES:(block + 1) * LANES]
 
 
-def local_sums(devices, chain, where, deltas, labels_row):
+def local_sums(tail, chain, where, deltas, labels_row):
     clients, blocks, width = deltas.shape
     columns = width // (8 * CHAINS)
-    height = 4 * columns // LANES * CLUSTERS * blocks + count_rows(devices)
+    height = 4 * columns // LANES * CLUSTERS * blocks + tail
     out = pltpu.VMEM((height, LANES), jnp.float32)
     return pl.pallas_call(
-        functools.partial(local_sums_kernel, devices, chain),
+        functools.partial(local_sums_kernel, tail, chain),
         out_shape=(out, out),
         in_specs=[SMEM, HBM, HBM],
         out_specs=(VMEM, VMEM),
@@ -121,7 +120,8 @@
     for target, which in ((send, 1 - bit), (keep, bit)):
         rows = pl.ds(pl.multiple_of(which * half, CLUSTERS), half)
         target[0:half, :] = kept[rows, :] + arrived[rows, :]
-        target[half:half + tail, :] = kept[2 * half:2 * half + tail, :] + arrived[2 * half:2 * half + tail, :]
+        if tail:
+            target[half:half + tail, :] = kept[2 * half:2 * half + tail, :] + arrived[2 * half:2 * half + tail, :]
 
 
 def split(tail, step, where, kept, arrived):
@@ -142,11 +142,11 @@
     return [kept[at:at + CLUSTERS, :] + arrived[at:at + CLUSTERS, :] for at in ends]
 
 
-def finish_kernel(tail, blocks, kept, arrived, models):
+def finish_kernel(tail, own_tail, blocks, table, table_arrived, kept, arrived, models):
     rows = CLUSTERS * blocks
-    height = kept.shape[0] - tail
+    height = kept.shape[0] - own_tail
     totals = jnp.zeros((CLUSTERS, 1), jnp.float32)
-    for counts in table_of(tail, kept, arrived):
+    for counts in table_of(tail, table, table_arrived):
         totals = totals + jnp.sum(counts, axis=1, keepdims=True)
     for cluster in range(CLUSTERS):
         total = jnp.broadcast_to(totals[cluster:cluster + 1, :], (blocks, LANES))
@@ -157,17 +157,17 @@
                 sums / total).astype(jnp.bfloat16)
 
 
-def finish(tail, blocks, kept, arrived):
+def finish(tail, own_tail, blocks, table, kept, arrived):
     rows = CLUSTERS * blocks
-    columns = (kept.shape[0] - tail) // rows * LANES
-    return pl.pallas_call(
-        functools.partial(finish_kernel, tail, blocks),
+    columns = (kept.shape[0] - own_tail) // rows * LANES
+    return pl.pallas_call(
+        functools.partial(finish_kernel, tail, own_tail, blocks),
         out_shape=pltpu.VMEM((rows, columns), jnp.bfloat16),
-        in_specs=[VMEM, VMEM],
+        in_specs=[VMEM] * 4,
         out_specs=VMEM,
         compiler_params=pltpu.CompilerParams(vmem_limit_bytes=8 << 20),
         name="finish",
-    )(near(kept), near(arrived))
+    )(near(table[0]), near(table[1]), near(kept), near(arrived))
 
 
 def join_kernel(*refs):
@@ -287,6 +287,7 @@
     labels_row = labels.reshape(1, clients)
     labels_list = labels.reshape(clients)
     tail = count_rows(devices)
+    tails = [0 if chain else tail for chain in range(CHAINS)]
     bits = devices.bit_length() - 1
 
     def send(value, flip):
@@ -303,10 +304,10 @@
 
     kept = []
     for chain in range(CHAINS):
-        other, mine = local_sums(devices, chain, where, deltas, labels_row)
-        kept.append(split(tail, 0, where, mine, send(other, cores)))
+        other, mine = local_sums(tails[chain], chain, where, deltas, labels_row)
+        kept.append(split(tails[chain], 0, where, mine, send(other, cores)))
     for chain, (out, keep) in enumerate(kept):
-        kept[chain] = split(tail, 1, where, keep, send(out, crossed(1, 3, 0)))
+        kept[chain] = split(tails[chain], 1, where, keep, send(out, crossed(1, 3, 0)))
     for chain, (out, keep) in enumerate(kept):
         kept[chain] = (keep, send(out, crossed(1, 3, 1)))
     for step in range(bits - 3):
@@ -314,8 +315,8 @@
             total = keep + arrived
             kept[chain] = (total, send(total, crossed(3, bits, step)))
     pairs, rests = [], []
-    for pair in kept:
-        own = finish(tail, blocks, *pair)[None]
+    for chain, pair in enumerate(kept):
+        own = finish(tail, tails[chain], blocks, kept[0], *pair)[None]
         diagonal = send(own, lambda i: 6)
         pairs.append(join(own, send(own, cores)))
         beside = send(pairs[-1], lambda i: 2 << role_of(i) | 1)

time: 50.7 us -> 50.4 us (level)
    ppermute x18, waiting for transfers between devices: 13.8 us -> 13.3 us  [send(): return lax.ppermute(value, AXES, [(i, i ^ flip(i)) for i in range(devices)])]
where the time goes in v7:
time: 50.4 us; the launch traced here: 50.3 us
  starting transfers between devices  25.2 us (50%)
  waiting for transfers between devices  13.3 us (26%)
  Pallas kernels  10.9 us (22%)
  between operations  0.79 us (2%)
    ppermute x18, starting transfers between devices, send(): return lax.ppermute(value, AXES, [(i, i ^ flip(i)) for i in range(devices)])  25.2 us
    ppermute x18, waiting for transfers between devices, send(): return lax.ppermute(value, AXES, [(i, i ^ flip(i)) for i in range(devices)])  13.3 us
    pallas_call x2, Pallas kernels, give_back(): pl.pallas_call(functools.partial(give_back_kernel, places, len(models), t...  5.24 us
    pallas_call x2, Pallas kernels, local_sums(): pl.pallas_call(functools.partial(local_sums_kernel, tail, chain), out_sha...  5.23 us
  transfers between devices with their start and end apart: 18, of which 9 were waited for; matrix products, arithmetic and copies ran while one was open for 0% of the time, Pallas kernels for 11%

profile of v7, /device:TPU:0, one launch (start us, length us, event | category | flops | bytes accessed | tf_op | source)
XLA Modules:
  0.0 50.3 jit_solution(17468769969733446372)
XLA Ops:
  0.6 2.6 %local_sums.2 = (f32[1032,128]{1,0:T(8,128)S(1)}, f32[1032,128]{1,0:T(8,128)S(1)}) custom-call(s32[1]{0:T(128)} %bitcast.where, bf16[64,16,4096]{2,1,0:T(8,128)(2,1)} %deltas.3, s32[1,64]{1,0:T(1,128)} %bitcast.12), custom_call_target="tpu_custom_call" | custom-call | tf_op jit(solution)/shard_map/local_sums/pallas_call | solution.py:104
  3.8 2.6 %local_sums.3 = (f32[1024,128]{1,0:T(8,128)S(1)}, f32[1024,128]{1,0:T(8,128)S(1)}) custom-call(s32[1]{0:T(128)} %bitcast.where, bf16[64,16,4096]{2,1,0:T(8,128)(2,1)} %deltas.3, s32[1,64]{1,0:T(1,128)} %bitcast.13), custom_call_target="tpu_custom_call" | custom-call | tf_op jit(solution)/shard_map/local_sums/pallas_call | solution.py:104
  6.6 2.7 %collective-permute-start.1 = (f32[520,128]{1,0:T(8,128)S(1)}, f32[520,128]{1,0:T(8,128)S(1)}, u32[]{:S(2)}, u32[]{:S(2)}) collective-permute-start(f32[520,128]{1,0:T(8,128)S(1)} %get-tuple-element.19), channel_id=1, source_target_pairs={{0,3},{1,4},{2,7},{3,0},{4,1},{5,6},{6,5},{7,2},{8,13},{9,10},{10,... | collective-permute-start | bytes 798728 | tf_op jit(solution)/shard_map/ppermute | solution.py:294
  9.3 1.8 %collective-permute-start.10 = (f32[512,128]{1,0:T(8,128)S(1)}, f32[512,128]{1,0:T(8,128)S(1)}, u32[]{:S(2)}, u32[]{:S(2)}) collective-permute-start(f32[512,128]{1,0:T(8,128)S(1)} %get-tuple-element.25), channel_id=1, source_target_pairs={{0,3},{1,4},{2,7},{3,0},{4,1},{5,6},{6,5},{7,2},{8,13},{9,10},{10,... | collective-permute-start | bytes 786440 | tf_op jit(solution)/shard_map/ppermute | solution.py:294
  11.1 2.2 %collective-permute-done.1.arrived = f32[520,128]{1,0:T(8,128)S(1)} collective-permute-done((f32[520,128]{1,0:T(8,128)S(1)}, f32[520,128]{1,0:T(8,128)S(1)}, u32[]{:S(2)}, u32[]{:S(2)}) %collective-permute-start.1) | collective-permute-done | bytes 266272 | tf_op jit(solution)/shard_map/ppermute | solution.py:294
  13.4 2.1 %collective-permute-start.2 = (f32[264,128]{1,0:T(8,128)S(1)}, f32[264,128]{1,0:T(8,128)S(1)}, u32[]{:S(2)}, u32[]{:S(2)}) collective-permute-start(f32[264,128]{1,0:T(8,128)S(1)} %get-tuple-element.21), channel_id=1, source_target_pairs={{0,5},{1,2},{2,1},{3,6},{4,7},{5,0},{6,3},{7,4},{8,11},{9,12},{10,... | collective-permute-start | bytes 405512 | tf_op jit(solution)/shard_map/ppermute | solution.py:294
  16.2 1.9 %collective-permute-start.11 = (f32[256,128]{1,0:T(8,128)S(1)}, f32[256,128]{1,0:T(8,128)S(1)}, u32[]{:S(2)}, u32[]{:S(2)}) collective-permute-start(f32[256,128]{1,0:T(8,128)S(1)} %get-tuple-element.27), channel_id=1, source_target_pairs={{0,5},{1,2},{2,1},{3,6},{4,7},{5,0},{6,3},{7,4},{8,11},{9,12},{10,... | collective-permute-start | bytes 393224 | tf_op jit(solution)/shard_map/ppermute | solution.py:294
  18.3 1.8 %collective-permute-start.3 = (f32[264,128]{1,0:T(8,128)S(1)}, f32[264,128]{1,0:T(8,128)S(1)}, u32[]{:S(2)}, u32[]{:S(2)}) collective-permute-start(f32[264,128]{1,0:T(8,128)S(1)} %add.16), channel_id=1, source_target_pairs={{0,9},{1,16},{2,19},{3,10},{4,21},{5,12},{6,15},{7,22},{8,25},{9,0... | collective-permute-start | bytes 405512 | tf_op jit(solution)/shard_map/ppermute | solution.py:294
  20.1 0.7 %collective-permute-done.11 = f32[256,128]{1,0:T(8,128)S(1)} collective-permute-done((f32[256,128]{1,0:T(8,128)S(1)}, f32[256,128]{1,0:T(8,128)S(1)}, u32[]{:S(2)}, u32[]{:S(2)}) %collective-permute-start.11) | collective-permute-done | bytes 131104 | tf_op jit(solution)/shard_map/ppermute | solution.py:294
  20.8 1.9 %collective-permute-start.12 = (f32[256,128]{1,0:T(8,128)S(1)}, f32[256,128]{1,0:T(8,128)S(1)}, u32[]{:S(2)}, u32[]{:S(2)}) collective-permute-start(f32[256,128]{1,0:T(8,128)S(1)} %add.18), channel_id=1, source_target_pairs={{0,9},{1,16},{2,19},{3,10},{4,21},{5,12},{6,15},{7,22},{8,25},{9,0... | collective-permute-start | bytes 393224 | tf_op jit(solution)/shard_map/ppermute | solution.py:294
  22.7 0.9 %collective-permute-done.3 = f32[264,128]{1,0:T(8,128)S(1)} collective-permute-done((f32[264,128]{1,0:T(8,128)S(1)}, f32[264,128]{1,0:T(8,128)S(1)}, u32[]{:S(2)}, u32[]{:S(2)}) %collective-permute-start.3) | collective-permute-done | bytes 135200 | tf_op jit(solution)/shard_map/ppermute | solution.py:294
  23.6 3.3 %collective-permute-start.4 = (f32[264,128]{1,0:T(8,128)S(1)}, f32[264,128]{1,0:T(8,128)S(1)}, u32[]{:S(2)}, u32[]{:S(2)}) collective-permute-start(f32[264,128]{1,0:T(8,128)S(1)} %add.17.table.kept.rest_3_), channel_id=1, source_target_pairs={{0,17},{1,8},{2,11},{3,18},{4,13},{5,20},{6,23},{7,14},{8,1},{9,24... | collective-permute-start | bytes 405512 | tf_op jit(solution)/shard_map/ppermute | solution.py:294
  26.9 2.6 %collective-permute-start.13 = (f32[256,128]{1,0:T(8,128)S(1)}, f32[256,128]{1,0:T(8,128)S(1)}, u32[]{:S(2)}, u32[]{:S(2)}) collective-permute-start(f32[256,128]{1,0:T(8,128)S(1)} %add.19.kept), channel_id=1, source_target_pairs={{0,17},{1,8},{2,11},{3,18},{4,13},{5,20},{6,23},{7,14},{8,1},{9,24... | collective-permute-start | bytes 393224 | tf_op jit(solution)/shard_map/ppermute | solution.py:294
  29.6 1.8 %collective-permute-done.4.table_arrived.arrived.rest_4_ = f32[264,128]{1,0:T(8,128)S(1)} collective-permute-done((f32[264,128]{1,0:T(8,128)S(1)}, f32[264,128]{1,0:T(8,128)S(1)}, u32[]{:S(2)}, u32[]{:S(2)}) %collective-permute-start.4) | collective-permute-done | bytes 135200 | tf_op jit(solution)/shard_map/ppermute | solution.py:294
  31.5 0.7 %collective-permute-start.6 = (bf16[1,128,256]{2,1,0:T(8,128)(2,1)S(1)}, bf16[1,128,256]{2,1,0:T(8,128)(2,1)S(1)}, u32[]{:S(2)}, u32[]{:S(2)}) collective-permute-start(bf16[1,128,256]{2,1,0:T(8,128)(2,1)S(1)} %bitcast.9), channel_id=1, source_target_pairs={{0,1},{1,0},{2,3},{3,2},{4,5},{5,4},{6,7},{7,6},{8,9},{9,8},{10,11... | collective-permute-start | bytes 196616 | tf_op jit(solution)/shard_map/ppermute | solution.py:294
  32.2 2.3 %collective-permute-done.13.arrived = f32[256,128]{1,0:T(8,128)S(1)} collective-permute-done((f32[256,128]{1,0:T(8,128)S(1)}, f32[256,128]{1,0:T(8,128)S(1)}, u32[]{:S(2)}, u32[]{:S(2)}) %collective-permute-start.13) | collective-permute-done | bytes 131104 | tf_op jit(solution)/shard_map/ppermute | solution.py:294
  34.7 1.4 %collective-permute-start.7 = (bf16[2,128,256]{2,1,0:T(8,128)(2,1)S(1)}, bf16[2,128,256]{2,1,0:T(8,128)(2,1)S(1)}, u32[]{:S(2)}, u32[]{:S(2)}) collective-permute-start(bf16[2,128,256]{2,1,0:T(8,128)(2,1)S(1)} %join.4.rest_0_), channel_id=1, source_target_pairs={{0,3},{1,4},{2,7},{3,0},{4,1},{5,6},{6,5},{7,2},{8,13},{9,10},{10,... | collective-permute-start | bytes 393224 | tf_op jit(solution)/shard_map/ppermute | solution.py:294
  36.1 1.2 %collective-permute-start.16 = (bf16[2,128,256]{2,1,0:T(8,128)(2,1)S(1)}, bf16[2,128,256]{2,1,0:T(8,128)(2,1)S(1)}, u32[]{:S(2)}, u32[]{:S(2)}) collective-permute-start(bf16[2,128,256]{2,1,0:T(8,128)(2,1)S(1)} %join.6.rest_1_), channel_id=1, source_target_pairs={{0,3},{1,4},{2,7},{3,0},{4,1},{5,6},{6,5},{7,2},{8,13},{9,10},{10,... | collective-permute-start | bytes 393224 | tf_op jit(solution)/shard_map/ppermute | solution.py:294
  37.4 1.8 %collective-permute-start.5 = (bf16[1,128,256]{2,1,0:T(8,128)(2,1)S(1)}, bf16[1,128,256]{2,1,0:T(8,128)(2,1)S(1)}, u32[]{:S(2)}, u32[]{:S(2)}) collective-permute-start(bf16[1,128,256]{2,1,0:T(8,128)(2,1)S(1)} %bitcast.11), channel_id=1, source_target_pairs={{0,6},{1,7},{2,4},{3,5},{4,2},{5,3},{6,0},{7,1},{8,14},{9,15},{10,... | collective-permute-start | bytes 196616 | tf_op jit(solution)/shard_map/ppermute | solution.py:294
  39.1 1.1 %collective-permute-start.14 = (bf16[1,128,256]{2,1,0:T(8,128)(2,1)S(1)}, bf16[1,128,256]{2,1,0:T(8,128)(2,1)S(1)}, u32[]{:S(2)}, u32[]{:S(2)}) collective-permute-start(bf16[1,128,256]{2,1,0:T(8,128)(2,1)S(1)} %bitcast.8), channel_id=1, source_target_pairs={{0,6},{1,7},{2,4},{3,5},{4,2},{5,3},{6,0},{7,1},{8,14},{9,15},{10,... | collective-permute-start | bytes 196616 | tf_op jit(solution)/shard_map/ppermute | solution.py:294
  40.3 3.9 %collective-permute-done.5.refs_0_ = bf16[1,128,256]{2,1,0:T(8,128)(2,1)S(1)} collective-permute-done((bf16[1,128,256]{2,1,0:T(8,128)(2,1)S(1)}, bf16[1,128,256]{2,1,0:T(8,128)(2,1)S(1)}, u32[]{:S(2)}, u32[]{:S(2)}) %collective-permute-start.5) | collective-permute-done | bytes 65568 | tf_op jit(solution)/shard_map/ppermute | solution.py:294
  44.2 0.7 %collective-permute-done.14.refs_0_ = bf16[1,128,256]{2,1,0:T(8,128)(2,1)S(1)} collective-permute-done((bf16[1,128,256]{2,1,0:T(8,128)(2,1)S(1)}, bf16[1,128,256]{2,1,0:T(8,128)(2,1)S(1)}, u32[]{:S(2)}, u32[]{:S(2)}) %collective-permute-start.14) | collective-permute-done | bytes 65568 | tf_op jit(solution)/shard_map/ppermute | solution.py:294
  45.0 2.5 %give_back.2 = (bf16[64,16,4096]{2,1,0:T(8,128)(2,1)}, s32[1,64]{1,0:T(1,128)}) custom-call(s32[1]{0:T(128)} %bitcast.where, s32[64]{0:T(128)S(1)} %bitcast.14, bf16[2,128,256]{2,1,0:T(8,128)(2,1)S(1)} %join.4.rest_0_, bf16[2,128,256]{2,1,0:T(8,128)(2,1)S(1)} %join.6.rest_1_, bf16[3,128,256]{2,1,0:T(8,128)(2,1)S(1)} %join.5.rest_2_, ...), custom_call_target="tpu_custom_call" | custom-call | flops 67108864 | tf_op jit(solution)/shard_map/give_back/pallas_call | solution.py:271
  47.5 2.8 %give_back.3 = bf16[64,16,4096]{2,1,0:T(8,128)(2,1)} custom-call(s32[1]{0:T(128)} %bitcast.where, s32[64]{0:T(128)S(1)} %bitcast.16, bf16[3,128,256]{2,1,0:T(8,128)(2,1)S(1)} %collective-permute-done.8.rest_0_, bf16[3,128,256]{2,1,0:T(8,128)(2,1)S(1)} %join.7.rest_1_, ...), custom_call_target="tpu_custom_call", output_to_operand_aliasing={{}: (5, {})} | custom-call | flops 67108864 | tf_op jit(solution)/shard_map/give_back/pallas_call | solution.py:271
  (32 shorter events, 2.2 us)
Async XLA Ops:
  3.3 41.7 %copy-start = (s32[64,1]{0,1:T(1,128)S(1)}, s32[64,1]{0,1:T(1,128)}, u32[]{:S(2)}) copy-start(s32[64,1]{0,1:T(1,128)} %param.3) | copy-start | bytes 772
  3.3 3.3 %collective-permute-start = (f32[1032,128]{1,0:T(8,128)S(1)}, f32[1032,128]{1,0:T(8,128)S(1)}, u32[]{:S(2)}, u32[]{:S(2)}) collective-permute-start(f32[1032,128]{1,0:T(8,128)S(1)} %get-tuple-element.17), channel_id=1, source_target_pairs={{0,1},{1,0},{2,3},{3,2},{4,5},{5,4},{6,7},{7,6},{8,9},{9,8},{10,11... | collective-permute-start | bytes 1585160 | tf_op jit(solution)/shard_map/ppermute | solution.py:294
  6.4 2.8 %collective-permute-start.9 = (f32[1024,128]{1,0:T(8,128)S(1)}, f32[1024,128]{1,0:T(8,128)S(1)}, u32[]{:S(2)}, u32[]{:S(2)}) collective-permute-start(f32[1024,128]{1,0:T(8,128)S(1)} %get-tuple-element.23), channel_id=1, source_target_pairs={{0,1},{1,0},{2,3},{3,2},{4,5},{5,4},{6,7},{7,6},{8,9},{9,8},{10,11... | collective-permute-start | bytes 1572872 | tf_op jit(solution)/shard_map/ppermute | solution.py:294
  6.6 6.8 %collective-permute-start.1 = (f32[520,128]{1,0:T(8,128)S(1)}, f32[520,128]{1,0:T(8,128)S(1)}, u32[]{:S(2)}, u32[]{:S(2)}) collective-permute-start(f32[520,128]{1,0:T(8,128)S(1)} %get-tuple-element.19), channel_id=1, source_target_pairs={{0,3},{1,4},{2,7},{3,0},{4,1},{5,6},{6,5},{7,2},{8,13},{9,10},{10,... | collective-permute-start | bytes 798728 | tf_op jit(solution)/shard_map/ppermute | solution.py:294
  9.3 6.8 %collective-permute-start.10 = (f32[512,128]{1,0:T(8,128)S(1)}, f32[512,128]{1,0:T(8,128)S(1)}, u32[]{:S(2)}, u32[]{:S(2)}) collective-permute-start(f32[512,128]{1,0:T(8,128)S(1)} %get-tuple-element.25), channel_id=1, source_target_pairs={{0,3},{1,4},{2,7},{3,0},{4,1},{5,6},{6,5},{7,2},{8,13},{9,10},{10,... | collective-permute-start | bytes 786440 | tf_op jit(solution)/shard_map/ppermute | solution.py:294
  13.4 4.9 %collective-permute-start.2 = (f32[264,128]{1,0:T(8,128)S(1)}, f32[264,128]{1,0:T(8,128)S(1)}, u32[]{:S(2)}, u32[]{:S(2)}) collective-permute-start(f32[264,128]{1,0:T(8,128)S(1)} %get-tuple-element.21), channel_id=1, source_target_pairs={{0,5},{1,2},{2,1},{3,6},{4,7},{5,0},{6,3},{7,4},{8,11},{9,12},{10,... | collective-permute-start | bytes 405512 | tf_op jit(solution)/shard_map/ppermute | solution.py:294
  16.2 4.6 %collective-permute-start.11 = (f32[256,128]{1,0:T(8,128)S(1)}, f32[256,128]{1,0:T(8,128)S(1)}, u32[]{:S(2)}, u32[]{:S(2)}) collective-permute-start(f32[256,128]{1,0:T(8,128)S(1)} %get-tuple-element.27), channel_id=1, source_target_pairs={{0,5},{1,2},{2,1},{3,6},{4,7},{5,0},{6,3},{7,4},{8,11},{9,12},{10,... | collective-permute-start | bytes 393224 | tf_op jit(solution)/shard_map/ppermute | solution.py:294
  18.3 5.3 %collective-permute-start.3 = (f32[264,128]{1,0:T(8,128)S(1)}, f32[264,128]{1,0:T(8,128)S(1)}, u32[]{:S(2)}, u32[]{:S(2)}) collective-permute-start(f32[264,128]{1,0:T(8,128)S(1)} %add.16), channel_id=1, source_target_pairs={{0,9},{1,16},{2,19},{3,10},{4,21},{5,12},{6,15},{7,22},{8,25},{9,0... | collective-permute-start | bytes 405512 | tf_op jit(solution)/shard_map/ppermute | solution.py:294
  20.8 6.1 %collective-permute-start.12 = (f32[256,128]{1,0:T(8,128)S(1)}, f32[256,128]{1,0:T(8,128)S(1)}, u32[]{:S(2)}, u32[]{:S(2)}) collective-permute-start(f32[256,128]{1,0:T(8,128)S(1)} %add.18), channel_id=1, source_target_pairs={{0,9},{1,16},{2,19},{3,10},{4,21},{5,12},{6,15},{7,22},{8,25},{9,0... | collective-permute-start | bytes 393224 | tf_op jit(solution)/shard_map/ppermute | solution.py:294
  23.6 7.7 %collective-permute-start.4 = (f32[264,128]{1,0:T(8,128)S(1)}, f32[264,128]{1,0:T(8,128)S(1)}, u32[]{:S(2)}, u32[]{:S(2)}) collective-permute-start(f32[264,128]{1,0:T(8,128)S(1)} %add.17.table.kept.rest_3_), channel_id=1, source_target_pairs={{0,17},{1,8},{2,11},{3,18},{4,13},{5,20},{6,23},{7,14},{8,1},{9,24... | collective-permute-start | bytes 405512 | tf_op jit(solution)/shard_map/ppermute | solution.py:294
  26.9 7.6 %collective-permute-start.13 = (f32[256,128]{1,0:T(8,128)S(1)}, f32[256,128]{1,0:T(8,128)S(1)}, u32[]{:S(2)}, u32[]{:S(2)}) collective-permute-start(f32[256,128]{1,0:T(8,128)S(1)} %add.19.kept), channel_id=1, source_target_pairs={{0,17},{1,8},{2,11},{3,18},{4,13},{5,20},{6,23},{7,14},{8,1},{9,24... | collective-permute-start | bytes 393224 | tf_op jit(solution)/shard_map/ppermute | solution.py:294
  31.5 3.2 %collective-permute-start.6 = (bf16[1,128,256]{2,1,0:T(8,128)(2,1)S(1)}, bf16[1,128,256]{2,1,0:T(8,128)(2,1)S(1)}, u32[]{:S(2)}, u32[]{:S(2)}) collective-permute-start(bf16[1,128,256]{2,1,0:T(8,128)(2,1)S(1)} %bitcast.9), channel_id=1, source_target_pairs={{0,1},{1,0},{2,3},{3,2},{4,5},{5,4},{6,7},{7,6},{8,9},{9,8},{10,11... | collective-permute-start | bytes 196616 | tf_op jit(solution)/shard_map/ppermute | solution.py:294
  34.6 1.5 %collective-permute-start.15 = (bf16[1,128,256]{2,1,0:T(8,128)(2,1)S(1)}, bf16[1,128,256]{2,1,0:T(8,128)(2,1)S(1)}, u32[]{:S(2)}, u32[]{:S(2)}) collective-permute-start(bf16[1,128,256]{2,1,0:T(8,128)(2,1)S(1)} %bitcast.6), channel_id=1, source_target_pairs={{0,1},{1,0},{2,3},{3,2},{4,5},{5,4},{6,7},{7,6},{8,9},{9,8},{10,11... | collective-permute-start | bytes 196616 | tf_op jit(solution)/shard_map/ppermute | solution.py:294
  34.7 9.4 %collective-permute-start.7 = (bf16[2,128,256]{2,1,0:T(8,128)(2,1)S(1)}, bf16[2,128,256]{2,1,0:T(8,128)(2,1)S(1)}, u32[]{:S(2)}, u32[]{:S(2)}) collective-permute-start(bf16[2,128,256]{2,1,0:T(8,128)(2,1)S(1)} %join.4.rest_0_), channel_id=1, source_target_pairs={{0,3},{1,4},{2,7},{3,0},{4,1},{5,6},{6,5},{7,2},{8,13},{9,10},{10,... | collective-permute-start | bytes 393224 | tf_op jit(solution)/shard_map/ppermute | solution.py:294
  36.1 8.7 %collective-permute-start.16 = (bf16[2,128,256]{2,1,0:T(8,128)(2,1)S(1)}, bf16[2,128,256]{2,1,0:T(8,128)(2,1)S(1)}, u32[]{:S(2)}, u32[]{:S(2)}) collective-permute-start(bf16[2,128,256]{2,1,0:T(8,128)(2,1)S(1)} %join.6.rest_1_), channel_id=1, source_target_pairs={{0,3},{1,4},{2,7},{3,0},{4,1},{5,6},{6,5},{7,2},{8,13},{9,10},{10,... | collective-permute-start | bytes 393224 | tf_op jit(solution)/shard_map/ppermute | solution.py:294
  37.4 6.8 %collective-permute-start.5 = (bf16[1,128,256]{2,1,0:T(8,128)(2,1)S(1)}, bf16[1,128,256]{2,1,0:T(8,128)(2,1)S(1)}, u32[]{:S(2)}, u32[]{:S(2)}) collective-permute-start(bf16[1,128,256]{2,1,0:T(8,128)(2,1)S(1)} %bitcast.11), channel_id=1, source_target_pairs={{0,6},{1,7},{2,4},{3,5},{4,2},{5,3},{6,0},{7,1},{8,14},{9,15},{10,... | collective-permute-start | bytes 196616 | tf_op jit(solution)/shard_map/ppermute | solution.py:294
  39.1 5.8 %collective-permute-start.14 = (bf16[1,128,256]{2,1,0:T(8,128)(2,1)S(1)}, bf16[1,128,256]{2,1,0:T(8,128)(2,1)S(1)}, u32[]{:S(2)}, u32[]{:S(2)}) collective-permute-start(bf16[1,128,256]{2,1,0:T(8,128)(2,1)S(1)} %bitcast.8), channel_id=1, source_target_pairs={{0,6},{1,7},{2,4},{3,5},{4,2},{5,3},{6,0},{7,1},{8,14},{9,15},{10,... | collective-permute-start | bytes 196616 | tf_op jit(solution)/shard_map/ppermute | solution.py:294
  44.2 3.3 %collective-permute-start.8 = (bf16[3,128,256]{2,1,0:T(8,128)(2,1)S(1)}, bf16[3,128,256]{2,1,0:T(8,128)(2,1)S(1)}, u32[]{:S(2)}, u32[]{:S(2)}) collective-permute-start(bf16[3,128,256]{2,1,0:T(8,128)(2,1)S(1)} %join.5.rest_2_), channel_id=1, source_target_pairs={{0,1},{1,0},{2,3},{3,2},{4,5},{5,4},{6,7},{7,6},{8,9},{9,8},{10,11... | collective-permute-start | bytes 589832 | tf_op jit(solution)/shard_map/ppermute | solution.py:294
  44.9 2.6 %collective-permute-start.17 = (bf16[3,128,256]{2,1,0:T(8,128)(2,1)S(1)}, bf16[3,128,256]{2,1,0:T(8,128)(2,1)S(1)}, u32[]{:S(2)}, u32[]{:S(2)}) collective-permute-start(bf16[3,128,256]{2,1,0:T(8,128)(2,1)S(1)} %join.7.rest_1_), channel_id=1, source_target_pairs={{0,1},{1,0},{2,3},{3,2},{4,5},{5,4},{6,7},{7,6},{8,9},{9,8},{10,11... | collective-permute-start | bytes 589832 | tf_op jit(solution)/shard_map/ppermute | solution.py:294
